TPU v7x, 32 devices: a whole 2x2x4 slice. The times are simulated.
32 devices in a mesh: dp: 4 (over x, core), fsdp: 8 (over z, y).
Axes of the slice: x: 2, y: 2, z: 4, core: 2. Of those that a mesh axis runs over, the one named last changes fastest.
Arguments:
- pixels: bfloat16 [50176, 768], P(('dp', 'fsdp')), may hold values from -6 to 6
- resolution: int32 [256], P(('dp', 'fsdp')), may hold values from 0 to 2, as said below
- kept: int32 [12544], P(('dp', 'fsdp')), may hold values from 0 to 1567, as said below
- step_count: int32 [1], replicated, may hold values from 2 to 20
- encoder_in: float32 [768, 7424], P(('dp', 'fsdp')), may hold values from -0.21875 to 0.21875
- encoder_out: float32 [3072, 768], P(('dp', 'fsdp')), may hold values from -0.109375 to 0.109375
- decoder_in: float32 [512, 4864], P(('dp', 'fsdp')), may hold values from -0.25 to 0.25
- decoder_out: float32 [2048, 512], P(('dp', 'fsdp')), may hold values from -0.125 to 0.125
- norm_gains: float32 [3840], P(('dp', 'fsdp')), may hold values from 0.5 to 1.5
- all_biases: float32 [16640], P(('dp', 'fsdp')), may hold values from -2.4 to 2.4
- moment_encoder_in: float32 [768, 7424], P(('dp', 'fsdp')), may hold values from -4.172325e-07 to 4.172325e-07
- moment_encoder_out: float32 [3072, 768], P(('dp', 'fsdp')), may hold values from -4.172325e-07 to 4.172325e-07
- moment_decoder_in: float32 [512, 4864], P(('dp', 'fsdp')), may hold values from -4.172325e-07 to 4.172325e-07
- moment_decoder_out: float32 [2048, 512], P(('dp', 'fsdp')), may hold values from -4.172325e-07 to 4.172325e-07
- moment_gains: float32 [3840], P(('dp', 'fsdp')), may hold values from -1.66893e-06 to 1.66893e-06
- moment_biases: float32 [16640], P(('dp', 'fsdp')), may hold values from -1.66893e-06 to 1.66893e-06
- square_encoder_in: float32 [768, 7424], P(('dp', 'fsdp')), may hold values from 1.1319536e-14 to 1.8008353e-13
- square_encoder_out: float32 [3072, 768], P(('dp', 'fsdp')), may hold values from 1.1319536e-14 to 1.8008353e-13
- square_decoder_in: float32 [512, 4864], P(('dp', 'fsdp')), may hold values from 1.1319536e-14 to 1.8008353e-13
- square_decoder_out: float32 [2048, 512], P(('dp', 'fsdp')), may hold values from 1.1319536e-14 to 1.8008353e-13
- square_gains: float32 [3840], P(('dp', 'fsdp')), may hold values from 1.8008353e-13 to 2.8813364e-12
- square_biases: float32 [16640], P(('dp', 'fsdp')), may hold values from 1.8008353e-13 to 2.8813364e-12
Outputs:
- loss: float32 [], replicated
- grad_norm: float32 [], replicated
- updated_encoder_in: float32 [768, 7424], P(('dp', 'fsdp'))
- updated_encoder_out: float32 [3072, 768], P(('dp', 'fsdp'))
- updated_decoder_in: float32 [512, 4864], P(('dp', 'fsdp'))
- updated_decoder_out: float32 [2048, 512], P(('dp', 'fsdp'))
- updated_gains: float32 [3840], P(('dp', 'fsdp'))
- updated_biases: float32 [16640], P(('dp', 'fsdp'))
- updated_moment_encoder_in: float32 [768, 7424], P(('dp', 'fsdp'))
- updated_moment_encoder_out: float32 [3072, 768], P(('dp', 'fsdp'))
- updated_moment_decoder_in: float32 [512, 4864], P(('dp', 'fsdp'))
- updated_moment_decoder_out: float32 [2048, 512], P(('dp', 'fsdp'))
- updated_moment_gains: float32 [3840], P(('dp', 'fsdp'))
- updated_moment_biases: float32 [16640], P(('dp', 'fsdp'))
- updated_square_encoder_in: float32 [768, 7424], P(('dp', 'fsdp'))
- updated_square_encoder_out: float32 [3072, 768], P(('dp', 'fsdp'))
- updated_square_decoder_in: float32 [512, 4864], P(('dp', 'fsdp'))
- updated_square_decoder_out: float32 [2048, 512], P(('dp', 'fsdp'))
- updated_square_gains: float32 [3840], P(('dp', 'fsdp'))
- updated_square_biases: float32 [16640], P(('dp', 'fsdp'))
Inputs may be any that keep to these rules, and one draw needn't show every extreme that they name: `resolution`: each device's 8 entries, in a random order, are k of class 1, 4 * (2 - k) of class 0 and 3 * k of class 2, for some k from 0 to 2, so that its images fill its 1568 patches exactly. One device has k = 2 and another k = 0. `kept`: each device's 392 entries are distinct indices of its own patches in rising order, exactly a quarter of the patches of every one of its images.
All inputs are finite; a program needn't handle non-finite values.
Results may differ from a plain program's by a relative error of at most 0.0003.
The roundings to bfloat16 on the way count: a program that leaves them out, or rounds other values in their place, can miss the bound.
Values may be sent and summed in bfloat16 or wider, within the bound.
A program may use at most 256 MiB of HBM per device.

v0:
```python
import math

import jax
import jax.numpy as jnp
from jax import lax
from jax.sharding import PartitionSpec as P

D = 768
HEADS = 12
FF = 3072
DD = 512
DHEADS = 16
DFF = 2048
PIX = 768
SIDE_BIG = 28
SIDE_SMALL = 14


BETA_ONE = 0.9
BETA_TWO = 0.95
EPSILON = 1e-08
RATE = 0.05
DECAY = 0.05


def round_plain(value):
    return lax.optimization_barrier(value.astype(jnp.bfloat16)).astype(jnp.float32)


def value_fwd(value):
    return (round_plain(value), None)


def value_bwd(unused, grad):
    return (grad,)


def identity_plain(value):
    return value


def grad_fwd(value):
    return (value, None)


def grad_bwd(unused, grad):
    return (round_plain(grad),)


def make_rounders():
    value_rule = jax.custom_vjp(round_plain)
    value_rule.defvjp(value_fwd, value_bwd)
    grad_rule = jax.custom_vjp(identity_plain)
    grad_rule.defvjp(grad_fwd, grad_bwd)
    return (value_rule, grad_rule)


def value_round(value):
    return make_rounders()[0](value)


def grad_round(value):
    return make_rounders()[1](value)


def matmul(left, right):
    return jnp.dot(left, right, preferred_element_type=jnp.float32)


def both(value):
    return value_round(grad_round(value))


def pieces(vector, widths):
    result = []
    start = 0
    for width in widths:
        result.append(vector[..., start : start + width])
        start += width
    return result


def layout(resolution, count):
    slot_ids = jnp.arange(resolution.shape[0], dtype=jnp.int32)
    lengths = jnp.where(
        resolution == 1, SIDE_BIG * SIDE_BIG, jnp.where(resolution == 0, SIDE_SMALL * SIDE_SMALL, 0)
    ).astype(jnp.int32)
    sides = jnp.where(resolution == 1, SIDE_BIG, SIDE_SMALL).astype(jnp.int32)
    starts = jnp.cumsum(lengths) - lengths
    position = jnp.arange(count, dtype=jnp.int32)[:, None]
    inside = (position >= starts[None, :]) & (position < (starts + lengths)[None, :])
    image = jnp.sum(jnp.where(inside, slot_ids[None, :], 0), axis=1)
    place = jnp.sum(jnp.where(inside, position - starts[None, :], 0), axis=1)
    side = jnp.sum(jnp.where(inside, sides[None, :], 0), axis=1)
    return (image, place // side, place % side)


def sine_table(row_pos, col_pos, width):
    quarter = width // 4
    omega = 1.0 / 10000.0 ** (jnp.arange(quarter, dtype=jnp.float32) / quarter)
    across = row_pos.astype(jnp.float32)[:, None] * omega[None, :]
    downward = col_pos.astype(jnp.float32)[:, None] * omega[None, :]
    return jnp.concatenate(
        [jnp.sin(across), jnp.cos(across), jnp.sin(downward), jnp.cos(downward)], axis=1
    )


def layer_norm(stream, gain, shift):
    centered = stream - jnp.mean(stream, axis=1, keepdims=True)
    spread = jnp.mean(centered * centered, axis=1, keepdims=True)
    return centered * lax.rsqrt(spread + 1e-06) * gain + shift


def attend(queries, key_rows, values, image, heads):
    count, width = queries.shape
    size = width // heads
    scale = 1.0 / math.sqrt(size)
    same = image[:, None] == image[None, :]

    def split_heads(tensor):
        return tensor.reshape(count, heads, size).transpose(1, 0, 2)

    def one_head(trio):
        query_head, key_head, value_head = trio
        scores = grad_round(matmul(query_head, key_head.T) * scale)
        scores = jnp.where(same, scores, -1e30)
        shifted = jnp.exp(scores - jnp.max(scores, axis=1, keepdims=True))
        weights = value_round(shifted / jnp.sum(shifted, axis=1, keepdims=True))
        return matmul(weights, value_head)

    mixed = lax.map(
        jax.checkpoint(one_head), (split_heads(queries), split_heads(key_rows), split_heads(values))
    )
    return mixed.transpose(1, 0, 2).reshape(count, width)


def block(stream, image, params, heads):
    (
        gain_one,
        shift_one,
        w_qkv,
        bias_query,
        bias_value,
        w_out,
        bias_out,
        gain_two,
        shift_two,
        w_up,
        bias_up,
        w_down,
        bias_down,
    ) = params
    width = stream.shape[1]
    normed = value_round(layer_norm(stream, gain_one, shift_one))
    joined = matmul(normed, w_qkv)
    queries = both(joined[:, :width] + bias_query)
    key_rows = both(joined[:, width : 2 * width])
    values = both(joined[:, 2 * width :] + bias_value)
    mixed = both(attend(queries, key_rows, values, image, heads))
    stream = stream + grad_round(matmul(mixed, w_out) + bias_out)
    normed = value_round(layer_norm(stream, gain_two, shift_two))
    hidden = grad_round(matmul(normed, w_up) + bias_up)
    return stream + grad_round(
        matmul(value_round(jax.nn.gelu(hidden, approximate=False)), w_down) + bias_down
    )


def section_a(mats, gain_vec, bias_vec, pixel_rows, kept, resolution):
    w_patch, w_qkv, w_out, w_up, w_lift = pieces(mats[0], (D, 3 * D, D, FF, DD))
    gain_one, gain_two, gain_final = pieces(gain_vec, (D, D, D))
    (
        bias_patch,
        shift_one,
        bias_query,
        bias_value,
        bias_out,
        shift_two,
        bias_up,
        bias_down,
        shift_final,
        bias_lift,
        mask_token,
    ) = pieces(bias_vec, (D, D, D, D, D, D, FF, D, D, DD, DD))
    count = pixel_rows.shape[0]
    image, rows, cols = layout(resolution, count)
    stream = grad_round(matmul(pixel_rows[kept], w_patch) + bias_patch) + sine_table(
        rows[kept], cols[kept], D
    )
    stream = block(
        stream,
        image[kept],
        (
            gain_one,
            shift_one,
            w_qkv,
            bias_query,
            bias_value,
            w_out,
            bias_out,
            gain_two,
            shift_two,
            w_up,
            bias_up,
            mats[1],
            bias_down,
        ),
        HEADS,
    )
    lifted = grad_round(
        matmul(value_round(layer_norm(stream, gain_final, shift_final)), w_lift) + bias_lift
    )
    full = jnp.broadcast_to(mask_token[None, :], (count, DD)).at[kept].set(lifted)
    return full + sine_table(rows, cols, DD)


def section_b(mats, gain_vec, bias_vec, stream, pixel_rows, kept, resolution, denom):
    w_qkv, w_out, w_up, w_head = pieces(mats[0], (3 * DD, DD, DFF, PIX))
    gain_one, gain_two, gain_final = pieces(gain_vec[3 * D :], (DD, DD, DD))
    (
        shift_one,
        bias_query,
        bias_value,
        bias_out,
        shift_two,
        bias_up,
        bias_down,
        shift_final,
        bias_head,
    ) = pieces(bias_vec[8 * D + FF + 2 * DD :], (DD, DD, DD, DD, DD, DFF, DD, DD, PIX))
    count = pixel_rows.shape[0]
    image, rows, cols = layout(resolution, count)
    stream = block(
        stream,
        image,
        (
            gain_one,
            shift_one,
            w_qkv,
            bias_query,
            bias_value,
            w_out,
            bias_out,
            gain_two,
            shift_two,
            w_up,
            bias_up,
            mats[1],
            bias_down,
        ),
        DHEADS,
    )
    predicted = grad_round(
        matmul(value_round(layer_norm(stream, gain_final, shift_final)), w_head) + bias_head
    )
    centered = pixel_rows - jnp.mean(pixel_rows, axis=1, keepdims=True)
    target = centered * lax.rsqrt(jnp.mean(centered * centered, axis=1, keepdims=True) + 1e-06)
    error = jnp.mean((predicted - target) ** 2, axis=1)
    weight = jnp.ones((count,), jnp.float32).at[kept].set(0.1)
    return jnp.sum(error * weight) / denom


def adamw(weight, grad, first, second, decay, times):
    first_new = BETA_ONE * first + (1.0 - BETA_ONE) * grad
    second_new = BETA_TWO * second + (1.0 - BETA_TWO) * grad * grad
    first_hat = first_new / (1.0 - BETA_ONE**times)
    second_hat = second_new / (1.0 - BETA_TWO**times)
    weight_new = weight - RATE * (first_hat / (jnp.sqrt(second_hat) + EPSILON) + decay * weight)
    return (weight_new, first_new, second_new)


def widen(arrays):
    return tuple((array.astype(jnp.float32) for array in arrays))


def per_device(
    pixels,
    resolution,
    kept,
    step_count,
    encoder_in,
    encoder_out,
    decoder_in,
    decoder_out,
    norm_gains,
    all_biases,
    moment_encoder_in,
    moment_encoder_out,
    moment_decoder_in,
    moment_decoder_out,
    moment_gains,
    moment_biases,
    square_encoder_in,
    square_encoder_out,
    square_decoder_in,
    square_decoder_out,
    square_gains,
    square_biases,
):
    devices = lax.axis_size("dp") * lax.axis_size("fsdp")
    patches_all = pixels.shape[0] * devices
    denom = (0.75 + 0.1 * 0.25) * patches_all
    pixel_rows = pixels.astype(jnp.float32)
    cotangent = jnp.ones((), jnp.float32)

    def forward_a(mats, gain_vec, bias_vec):
        return section_a(mats, gain_vec, bias_vec, pixel_rows, kept, resolution)

    def forward_b(mats, gain_vec, bias_vec, stream):
        return section_b(mats, gain_vec, bias_vec, stream, pixel_rows, kept, resolution, denom)

    encoder_whole = widen(
        (
            lax.all_gather(encoder_in.astype(jnp.bfloat16), ("dp", "fsdp"), axis=0, tiled=True),
            lax.all_gather(encoder_out.astype(jnp.bfloat16), ("dp", "fsdp"), axis=0, tiled=True),
            lax.all_gather(norm_gains.astype(jnp.bfloat16), ("dp", "fsdp"), axis=0, tiled=True),
            lax.all_gather(all_biases.astype(jnp.bfloat16), ("dp", "fsdp"), axis=0, tiled=True),
        )
    )
    encoder_mats = encoder_whole[:2]
    gains_full, biases_full = (encoder_whole[2], encoder_whole[3])
    lifted = forward_a(encoder_mats, gains_full, biases_full)
    loss_local = forward_b(
        widen(
            (
                lax.all_gather(decoder_in.astype(jnp.bfloat16), ("dp", "fsdp"), axis=0, tiled=True),
                lax.all_gather(
                    decoder_out.astype(jnp.bfloat16), ("dp", "fsdp"), axis=0, tiled=True
                ),
            )
        ),
        gains_full,
        biases_full,
        lifted,
    )
    loss_total = lax.psum(loss_local, ("dp", "fsdp"))
    decoder_again = widen(
        (
            lax.all_gather(decoder_in.astype(jnp.bfloat16), ("dp", "fsdp"), axis=0, tiled=True),
            lax.all_gather(decoder_out.astype(jnp.bfloat16), ("dp", "fsdp"), axis=0, tiled=True),
        )
    )
    unused, pull_decoder = jax.vjp(forward_b, decoder_again, gains_full, biases_full, lifted)
    decoder_terms, gain_back, bias_back, stream_back = pull_decoder(cotangent)
    decoder_grads = (
        lax.psum_scatter(decoder_terms[0], ("dp", "fsdp"), scatter_dimension=0, tiled=True),
        lax.psum_scatter(decoder_terms[1], ("dp", "fsdp"), scatter_dimension=0, tiled=True),
    )
    encoder_again = widen(
        (
            lax.all_gather(encoder_in.astype(jnp.bfloat16), ("dp", "fsdp"), axis=0, tiled=True),
            lax.all_gather(encoder_out.astype(jnp.bfloat16), ("dp", "fsdp"), axis=0, tiled=True),
        )
    )
    unused, pull_encoder = jax.vjp(forward_a, encoder_again, gains_full, biases_full)
    encoder_terms, gain_front, bias_front = pull_encoder(stream_back)
    encoder_grads = (
        lax.psum_scatter(encoder_terms[0], ("dp", "fsdp"), scatter_dimension=0, tiled=True),
        lax.psum_scatter(encoder_terms[1], ("dp", "fsdp"), scatter_dimension=0, tiled=True),
        lax.psum_scatter(gain_front + gain_back, ("dp", "fsdp"), scatter_dimension=0, tiled=True),
        lax.psum_scatter(bias_front + bias_back, ("dp", "fsdp"), scatter_dimension=0, tiled=True),
    )
    grads = (
        encoder_grads[0],
        encoder_grads[1],
        decoder_grads[0],
        decoder_grads[1],
        encoder_grads[2],
        encoder_grads[3],
    )
    squares = sum((jnp.sum(grad * grad) for grad in grads))
    total_squares = lax.psum(squares, ("dp", "fsdp"))
    grad_norm = jnp.sqrt(total_squares)
    factor = jnp.minimum(1.0, 0.5 / math.sqrt(patches_all) / (grad_norm + 1e-06))
    times = step_count[0].astype(jnp.float32)
    masters = (encoder_in, encoder_out, decoder_in, decoder_out, norm_gains, all_biases)
    firsts = (
        moment_encoder_in,
        moment_encoder_out,
        moment_decoder_in,
        moment_decoder_out,
        moment_gains,
        moment_biases,
    )
    seconds = (
        square_encoder_in,
        square_encoder_out,
        square_decoder_in,
        square_decoder_out,
        square_gains,
        square_biases,
    )
    results = [
        adamw(
            masters[index],
            grads[index] * factor,
            firsts[index],
            seconds[index],
            DECAY if index < 4 else 0.0,
            times,
        )
        for index in range(6)
    ]
    return (
        loss_total,
        grad_norm,
        results[0][0],
        results[1][0],
        results[2][0],
        results[3][0],
        results[4][0],
        results[5][0],
        results[0][1],
        results[1][1],
        results[2][1],
        results[3][1],
        results[4][1],
        results[5][1],
        results[0][2],
        results[1][2],
        results[2][2],
        results[3][2],
        results[4][2],
        results[5][2],
    )


def solution(mesh):
    in_specs = (
        P(("dp", "fsdp"), None),
        P(("dp", "fsdp")),
        P(("dp", "fsdp")),
        P(),
        P(("dp", "fsdp"), None),
        P(("dp", "fsdp"), None),
        P(("dp", "fsdp"), None),
        P(("dp", "fsdp"), None),
        P(("dp", "fsdp")),
        P(("dp", "fsdp")),
        P(("dp", "fsdp"), None),
        P(("dp", "fsdp"), None),
        P(("dp", "fsdp"), None),
        P(("dp", "fsdp"), None),
        P(("dp", "fsdp")),
        P(("dp", "fsdp")),
        P(("dp", "fsdp"), None),
        P(("dp", "fsdp"), None),
        P(("dp", "fsdp"), None),
        P(("dp", "fsdp"), None),
        P(("dp", "fsdp")),
        P(("dp", "fsdp")),
    )
    out_specs = (
        P(),
        P(),
        P(("dp", "fsdp"), None),
        P(("dp", "fsdp"), None),
        P(("dp", "fsdp"), None),
        P(("dp", "fsdp"), None),
        P(("dp", "fsdp")),
        P(("dp", "fsdp")),
        P(("dp", "fsdp"), None),
        P(("dp", "fsdp"), None),
        P(("dp", "fsdp"), None),
        P(("dp", "fsdp"), None),
        P(("dp", "fsdp")),
        P(("dp", "fsdp")),
        P(("dp", "fsdp"), None),
        P(("dp", "fsdp"), None),
        P(("dp", "fsdp"), None),
        P(("dp", "fsdp"), None),
        P(("dp", "fsdp")),
        P(("dp", "fsdp")),
    )
    return jax.shard_map(
        per_device, mesh=mesh, in_specs=in_specs, out_specs=out_specs, check_vma=False
    )
```

profile of v0, /device:TPU:0, one launch (start us, length us, event | category | flops | bytes accessed | tf_op | source)
XLA Modules:
  0.0 2080.4 jit_solution(10178314379982214943)
XLA Ops:
  18.1 43.7 %all-reduce.48 = (bf16[16640]{0:T(1024)(128)(2,1)S(1)}, bf16[3840]{0:T(1024)(128)(2,1)S(1)}) all-reduce(bf16[16640]{0:T(1024)(128)(2,1)S(1)} %dynamic-update-slice, bf16[3840]{0:T(1024)(128)(2,1)S(1)} %dynamic-update-slice.1), channel_id=1, replica_groups=mesh['dp'=4,'fsdp'=8] {'dp','fsdp'}, use_global_device_ids=true, to_apply=%add.43 | all-reduce | flops 20480 | bytes 81920
  89.0 7.2 multiply_sine_fusion.1
  96.2 8.4 all-gather.5.cloned.1.call-done
  121.5 21.8 %while.80 = (s32[]{:T(128)}, bf16[12,392,64]{1,2,0:T(8,128)(2,1)S(1)}, bf16[12,392,64]{2,1,0:T(8,128)(2,1)}, bf16[12,392,64]{2,1,0:T(8,128)(2,1)}, bf16[12,392,6...) while((s32[]{:T(128)}, bf16[12,392,64]{1,2,0:T(8,128)(2,1)S(1)}, ...), condition=%wide.region_9.10_spmd.clone, body=%wide.region_6.9_spmd.clone.sunk | while | flops 40720176 | bytes 2933365 | solution.py:131
  147.0 16.0 multiply_convert_fusion.2
  163.1 7.1 all-gather.7.cloned.1.call-done
  193.7 42.9 %all-gather.9.cloned.1.call-done = bf16[512,4864]{1,0:T(8,128)(2,1)} async-done(((bf16[16,4864]{1,0:T(8,128)(2,1)}), bf16[512,4864]{1,0:T(8,128)(2,1)}) %all-gather.9.cloned.1.call-update) | async-done | bytes 4980752 | tf_op jit(solution)/shard_map/all_gather | solution.py:325
  256.0 6.2 copy.105
  262.2 6.1 copy.103
  268.4 6.2 copy.104
  275.9 210.5 %while.81 = (s32[]{:T(128)}, bf16[16,1568,32]{1,2,0:T(8,128)(2,1)}, bf16[16,1568,32]{2,1,0:T(8,128)(2,1)}, bf16[16,1568,32]{2,1,0:T(8,128)(2,1)}, bf16[16,1568,3...) while((s32[]{:T(128)}, bf16[16,1568,32]{1,2,0:T(8,128)(2,1)}, ...), condition=%wide.region_20.21_spmd.clone, body=%wide.region_17.20_spmd.clone.sunk | while | flops 336828352 | bytes 40999636 | solution.py:131
  491.4 32.9 %multiply_convert_fusion = (bf16[1568,2048]{1,0:T(8,128)(2,1)}, f32[1568,2048]{1,0:T(8,128)}, f32[1568,2048]{1,0:T(8,128)}) fusion(f32[2048]{0:T(1024)S(1)} %copy-done.134, bf16[1568,512]{1,0:T(8,128)(2,1)S(1)} %add_convert_fusion.3, bf16[512,4864]{1,0:T(8,128)(2,1)} %all-gather.9.cloned.1.call-done), kind=kOutput, calls=%fused_computation.106 | convolution fusion | flops 3500277760 | bytes 35823616 | tf_op jit(solution)/shard_map/dot_general | solution.py:67
  524.3 8.2 fusion.168
  547.2 13.0 add_convert_fusion
  564.5 7.0 multiply_reduce_fusion.4
  584.4 438.5 %while.82 = (s32[]{:T(128)}, bf16[16,1568,32]{1,2,0:T(8,128)(2,1)}, bf16[16,1568,32]{1,2,0:T(8,128)(2,1)}, bf16[16,1568,32]{1,2,0:T(8,128)(2,1)}, bf16[16,1568,3...) while((s32[]{:T(128)}, bf16[16,1568,32]{1,2,0:T(8,128)(2,1)}, ...), condition=%wide.region_58.59_spmd.clone, body=%wide.region_52.58_spmd.clone.sunk | while | flops 865435648 | bytes 117725184 | solution.py:131
  600.0 5.8 divide_convert_fusion.10
  627.4 5.8 divide_convert_fusion.10
  654.8 5.8 divide_convert_fusion.10
  682.2 5.8 divide_convert_fusion.10
  709.6 5.8 divide_convert_fusion.10
  1048.9 6.6 add_convert_fusion.1
  1064.3 81.1 %while.83 = (s32[]{:T(128)}, bf16[12,392,64]{1,2,0:T(8,128)(2,1)}, bf16[12,392,64]{1,2,0:T(8,128)(2,1)}, bf16[12,392,64]{1,2,0:T(8,128)(2,1)S(1)}, bf16[12,392,6...) while((s32[]{:T(128)}, bf16[12,392,64]{1,2,0:T(8,128)(2,1)}, ...), condition=%wide.region_71.72_spmd.clone, body=%wide.region_65.71_spmd.clone.sunk | while | flops 103262208 | bytes 8452273 | solution.py:131
  1155.0 9.4 fusion.177
  1200.5 7.9 pad_add_fusion
  1210.7 39.3 %all-reduce.45 = f32[3840]{0:T(1024)S(1)} all-reduce(f32[3840]{0:T(1024)S(1)} %pad_add_fusion.10), channel_id=6, replica_groups=mesh['dp'=4,'fsdp'=8] {'dp','fsdp'}, use_global_device_ids=true, to_apply=%region_88.89.clone | all-reduce | flops 3840 | bytes 30720
  1250.7 22.4 %all-reduce.51.cloned.1.call-done = f32[16640]{0:T(1024)} async-done(((f32[16640]{0:T(1024)}), f32[16640]{0:T(1024)}) %all-reduce.51.cloned.1.call-update) | async-done | bytes 66576
  1274.4 148.9 %reduce-scatter.11.cloned.1.call-done = f32[64,512]{1,0:T(8,128)} async-done(((f32[2048,512]{1,0:T(8,128)}), f32[64,512]{1,0:T(8,128)}) %reduce-scatter.11.cloned.1.call-update) | async-done | bytes 131088 | tf_op jit(solution)/shard_map/reduce_scatter | solution.py:346
  1424.9 138.3 %reduce-scatter.7.cloned.1.call-done = f32[96,768]{1,0:T(8,128)} async-done(((f32[3072,768]{1,0:T(8,128)}), f32[96,768]{1,0:T(8,128)}) %reduce-scatter.7.cloned.1.call-update) | async-done | bytes 294928 | tf_op jit(solution)/shard_map/reduce_scatter | solution.py:358
  1564.8 216.7 %reduce-scatter.9.cloned.1.call-done = f32[16,4864]{1,0:T(8,128)} async-done(((f32[512,4864]{1,0:T(8,128)}), f32[16,4864]{1,0:T(8,128)}) %reduce-scatter.9.cloned.1.call-update) | async-done | bytes 311312 | tf_op jit(solution)/shard_map/reduce_scatter | solution.py:345
  1783.2 233.6 %reduce-scatter.5.cloned.1.call-done = f32[24,7424]{1,0:T(8,128)} async-done(((f32[768,7424]{1,0:T(8,128)}), f32[24,7424]{1,0:T(8,128)}) %reduce-scatter.5.cloned.1.call-update) | async-done | bytes 712720 | tf_op jit(solution)/shard_map/reduce_scatter | solution.py:357
  2022.7 40.2 %all-reduce.47 = (f32[]{:T(128)}, f32[]{:T(128)}) all-reduce(f32[]{:T(128)S(6)} %div.428, f32[]{:T(128)S(6)} %add.750), channel_id=1, replica_groups=mesh['dp'=4,'fsdp'=8] {'dp','fsdp'}, use_global_device_ids=true, to_apply=%region_30.31 | all-reduce | flops 2 | bytes 16 | tf_op jit(solution)/shard_map/psum | solution.py:335
  (1071 shorter events, 957.7 us)
Async XLA Ops:
  7.2 57.1 %copy-start.146 = (s32[8]{0:T(128)S(1)}, s32[8]{0:T(128)}, u32[]{:S(2)}) copy-start(s32[8]{0:T(128)} %param.35) | copy-start | bytes 100
  7.2 57.3 %copy-start.10 = (bf16[1568,768]{1,0:T(8,128)(2,1)S(1)}, bf16[1568,768]{1,0:T(8,128)(2,1)}, u32[]{:S(2)}) copy-start(bf16[1568,768]{1,0:T(8,128)(2,1)} %param.34) | copy-start | bytes 7225348
  7.2 97.3 %all-gather.5.cloned.1.call-start = ((), (), s32[]{:S(2)}) async-start(), calls=%async_computation.4 | async-start | bytes 11759616 | tf_op jit(solution)/shard_map/all_gather | solution.py:313
  9.3 160.9 %all-gather.7.cloned.1.call-start = ((), (), s32[]{:S(2)}) async-start(), calls=%async_computation.5 | async-start | bytes 4866048 | tf_op jit(solution)/shard_map/all_gather | solution.py:314
  11.0 225.6 %all-gather.9.cloned.1.call-start = ((), (), s32[]{:S(2)}) async-start(), calls=%async_computation.6 | async-start | bytes 5136384 | tf_op jit(solution)/shard_map/all_gather | solution.py:325
  12.8 511.6 %all-gather.11.cloned.1.call-start = ((), (), s32[]{:S(2)}) async-start(), calls=%async_computation.7 | async-start | bytes 2162688 | tf_op jit(solution)/shard_map/all_gather | solution.py:326
  14.4 1258.7 %all-reduce.51.cloned.1.call-start = ((), (), s32[]{:S(2)}) async-start(), calls=%async_computation.12 | async-start | bytes 139264
  16.3 61.0 %copy-start.108 = (u32[392]{0:T(512)}, u32[392]{0:T(512)S(1)}, u32[]{:S(2)}) copy-start(u32[392]{0:T(512)S(1)} %iota_add_fusion) | copy-start | bytes 4708
  62.4 129.0 %copy-start.120 = (f32[512]{0:T(512)}, f32[512]{0:T(512)S(1)}, u32[]{:S(2)}) copy-start(f32[512]{0:T(512)S(1)} %get-tuple-element.931) | copy-start | bytes 6148
  62.4 84.3 %copy-start.93 = (f32[768]{0:T(1024)}, f32[768]{0:T(1024)S(1)}, u32[]{:S(2)}) copy-start(f32[768]{0:T(1024)S(1)} %get-tuple-element.933) | copy-start | bytes 9220
  62.4 113.5 %copy-start.95 = (f32[768]{0:T(1024)}, f32[768]{0:T(1024)S(1)}, u32[]{:S(2)}) copy-start(f32[768]{0:T(1024)S(1)} %get-tuple-element.932) | copy-start | bytes 9220
  63.1 83.9 %copy-start.127 = (f32[3072]{0:T(1024)}, f32[3072]{0:T(1024)S(1)}, u32[]{:S(2)}) copy-start(f32[3072]{0:T(1024)S(1)} %slice.249) | copy-start | bytes 36868
  189.8 296.6 %copy-start.2 = (f32[1568,512]{1,0:T(8,128)}, f32[1568,512]{1,0:T(8,128)S(1)}, u32[]{:S(2)}) copy-start(f32[1568,512]{1,0:T(8,128)S(1)} %get-tuple-element.870) | copy-start | bytes 9633796
  275.9 210.5 %copy-start.124 = (f32[512]{0:T(512)S(1)}, f32[512]{0:T(512)}, u32[]{:S(2)}) copy-start(f32[512]{0:T(512)} %get-tuple-element.917) | copy-start | bytes 6148
  1154.8 268.5 %reduce-scatter.11.cloned.1.call-start = ((), (), s32[]{:S(2)}) async-start(), calls=%async_computation.11 | async-start | bytes 4325376 | tf_op jit(solution)/shard_map/reduce_scatter | solution.py:346
  1164.4 398.8 %reduce-scatter.7.cloned.1.call-start = ((), (), s32[]{:S(2)}) async-start(), calls=%async_computation.9 | async-start | bytes 9732096 | tf_op jit(solution)/shard_map/reduce_scatter | solution.py:358
  1171.4 610.1 %reduce-scatter.9.cloned.1.call-start = ((), (), s32[]{:S(2)}) async-start(), calls=%async_computation.10 | async-start | bytes 10272768 | tf_op jit(solution)/shard_map/reduce_scatter | solution.py:345
  1191.0 825.9 %reduce-scatter.5.cloned.1.call-start = ((), (), s32[]{:S(2)}) async-start(), calls=%async_computation.8 | async-start | bytes 23519232 | tf_op jit(solution)/shard_map/reduce_scatter | solution.py:357
  1208.4 855.2 %copy-start.147 = (f32[120]{0:T(128)S(1)}, f32[120]{0:T(128)}, u32[]{:S(2)}) copy-start(f32[120]{0:T(128)} %param.42) | copy-start | bytes 1444
  1208.4 855.2 %copy-start.148 = (f32[120]{0:T(128)S(1)}, f32[120]{0:T(128)}, u32[]{:S(2)}) copy-start(f32[120]{0:T(128)} %param.54) | copy-start | bytes 1444
  1208.4 855.2 %copy-start.149 = (f32[120]{0:T(128)S(1)}, f32[120]{0:T(128)}, u32[]{:S(2)}) copy-start(f32[120]{0:T(128)} %param.48) | copy-start | bytes 1444
  1208.4 855.9 %copy-start.126 = (f32[520]{0:T(1024)S(1)}, f32[520]{0:T(1024)}, u32[]{:S(2)}) copy-start(f32[520]{0:T(1024)} %param.43) | copy-start | bytes 6244
  1208.4 855.8 %copy-start.137 = (f32[520]{0:T(1024)S(1)}, f32[520]{0:T(1024)}, u32[]{:S(2)}) copy-start(f32[520]{0:T(1024)} %param.55) | copy-start | bytes 6244
  1208.4 855.8 %copy-start.138 = (f32[520]{0:T(1024)S(1)}, f32[520]{0:T(1024)}, u32[]{:S(2)}) copy-start(f32[520]{0:T(1024)} %param.49) | copy-start | bytes 6244
  1208.4 857.2 %copy-start.70 = (f32[64,512]{1,0:T(8,128)S(1)}, f32[64,512]{1,0:T(8,128)}, u32[]{:S(2)}) copy-start(f32[64,512]{1,0:T(8,128)} %param.41) | copy-start | bytes 393220
  1208.4 859.0 %copy-start.61 = (f32[96,768]{1,0:T(8,128)S(1)}, f32[96,768]{1,0:T(8,128)}, u32[]{:S(2)}) copy-start(f32[96,768]{1,0:T(8,128)} %param.39) | copy-start | bytes 884740
  1208.5 861.2 %copy-start.59 = (f32[16,4864]{1,0:T(8,128)S(1)}, f32[16,4864]{1,0:T(8,128)}, u32[]{:S(2)}) copy-start(f32[16,4864]{1,0:T(8,128)} %param.40) | copy-start | bytes 933892
  1208.5 861.2 %copy-start.71 = (f32[16,4864]{1,0:T(8,128)S(1)}, f32[16,4864]{1,0:T(8,128)}, u32[]{:S(2)}) copy-start(f32[16,4864]{1,0:T(8,128)} %param.52) | copy-start | bytes 933892
  1424.9 645.8 %copy-start.43 = (f32[24,7424]{1,0:T(8,128)S(1)}, f32[24,7424]{1,0:T(8,128)}, u32[]{:S(2)}) copy-start(f32[24,7424]{1,0:T(8,128)} %param.38) | copy-start | bytes 2138116
  1424.9 645.8 %copy-start.64 = (f32[24,7424]{1,0:T(8,128)S(1)}, f32[24,7424]{1,0:T(8,128)}, u32[]{:S(2)}) copy-start(f32[24,7424]{1,0:T(8,128)} %param.50) | copy-start | bytes 2138116
  1781.5 288.2 %copy-start.60 = (f32[16,4864]{1,0:T(8,128)S(1)}, f32[16,4864]{1,0:T(8,128)}, u32[]{:S(2)}) copy-start(f32[16,4864]{1,0:T(8,128)} %reduce-scatter.9.cloned.1.call-done) | copy-start | bytes 933892
  2016.8 53.9 %copy-start.44 = (f32[24,7424]{1,0:T(8,128)S(1)}, f32[24,7424]{1,0:T(8,128)}, u32[]{:S(2)}) copy-start(f32[24,7424]{1,0:T(8,128)} %reduce-scatter.5.cloned.1.call-done) | copy-start | bytes 2138116
  (135 other events, 779.6 us)
Sparse Core Ops, SparseCore 0:
  11.5 92.9 all-gather.4
  108.0 62.1 all-gather.6
  173.7 62.9 all-gather.8
  240.1 54.6 all-gather.10
  1154.9 118.0 all-reduce.50
  1275.2 148.1 reduce-scatter.10
  1429.3 133.8 reduce-scatter.6
  1565.5 215.9 reduce-scatter.8
  1787.9 228.8 reduce-scatter.4
where the time goes:
time: 2090 us; the launch traced here: 2080 us
  waiting for transfers between devices  818 us (39%)
  matrix products  509 us (24%)
  other arithmetic  408 us (20%)
  local copies, waits for them, and re-layouts  196 us (9%)
  blocking collectives  123 us (6%)
  between operations  23.6 us (1%)
    dot_general x228, matrix products, matmul(): return jnp.dot(left, right, preferred_element_type=jnp.float32)  509 us
    reduce_scatter x1, waiting for transfers between devices, per_device(): lax.psum_scatter(encoder_terms[0], ('dp', 'fsdp'), scatter_dimension=0, t...  234 us
    reduce_scatter x1, waiting for transfers between devices, per_device(): lax.psum_scatter(decoder_terms[0], ('dp', 'fsdp'), scatter_dimension=0, t...  217 us
    reduce_scatter x1, waiting for transfers between devices, per_device(): lax.psum_scatter(decoder_terms[1], ('dp', 'fsdp'), scatter_dimension=0, t...  149 us
    reduce_scatter x1, waiting for transfers between devices, per_device(): lax.psum_scatter(encoder_terms[1], ('dp', 'fsdp'), scatter_dimension=0, t...  138 us
    convert_element_type x28, other arithmetic, value_round(): return make_rounders()[0](value)  97.8 us
    unnamed x2, blocking collectives  83 us
    reduce_sum x28, other arithmetic, one_head(): shifted = jnp.exp(scores - jnp.max(scores, axis=1, keepdims=True))  78.8 us
  transfers between devices with their start and end apart: 9, of which 8 were waited for; matrix products, arithmetic and copies ran while one was open for 22% of the time, Pallas kernels for 0%

commit v1 on v0

--- a/solution.py
+++ b/solution.py
@@ -1,8 +1,11 @@
+import functools
 import math
 
 import jax
 import jax.numpy as jnp
 from jax import lax
+from jax.experimental import pallas as pl
+from jax.experimental.pallas import tpu as pltpu
 from jax.sharding import PartitionSpec as P
 
 D = 768
@@ -80,19 +83,39 @@
     return result
 
 
-def layout(resolution, count):
-    slot_ids = jnp.arange(resolution.shape[0], dtype=jnp.int32)
-    lengths = jnp.where(
-        resolution == 1, SIDE_BIG * SIDE_BIG, jnp.where(resolution == 0, SIDE_SMALL * SIDE_SMALL, 0)
-    ).astype(jnp.int32)
-    sides = jnp.where(resolution == 1, SIDE_BIG, SIDE_SMALL).astype(jnp.int32)
-    starts = jnp.cumsum(lengths) - lengths
-    position = jnp.arange(count, dtype=jnp.int32)[:, None]
-    inside = (position >= starts[None, :]) & (position < (starts + lengths)[None, :])
-    image = jnp.sum(jnp.where(inside, slot_ids[None, :], 0), axis=1)
-    place = jnp.sum(jnp.where(inside, position - starts[None, :], 0), axis=1)
-    side = jnp.sum(jnp.where(inside, sides[None, :], 0), axis=1)
-    return (image, place // side, place % side)
+def layout(resolution, kept, count):
+    big, small = SIDE_BIG * SIDE_BIG, SIDE_SMALL * SIDE_SMALL
+    ratio = big // small
+    units = count // small
+    is_big = (resolution == 1).astype(jnp.int32)
+    is_small = (resolution == 0).astype(jnp.int32)
+    bigs = jnp.sum(is_big)
+    lengths = ratio * is_big + is_small
+    slots = jnp.arange(resolution.shape[0], dtype=jnp.int32)
+    before = slots[:, None] > slots[None, :]
+
+    def earlier(values):
+        return jnp.sum(jnp.where(before, values[None, :], 0), axis=1)
+
+    old_start = earlier(lengths)
+    new_start = jnp.where(resolution == 1, ratio * earlier(is_big), ratio * bigs + earlier(is_small))
+    unit = jnp.arange(units, dtype=jnp.int32)[:, None]
+    inside = (unit >= old_start[None, :]) & (unit < (old_start + lengths)[None, :])
+    new_of_old = jnp.sum(jnp.where(inside, unit + (new_start - old_start)[None, :], 0), axis=1)
+    old_of_new = jnp.sum(jnp.where(unit == new_of_old[None, :], jnp.arange(units, dtype=jnp.int32)[None, :], 0), axis=1)
+    kept_unit = kept // small
+    matches = kept_unit[:, None] == jnp.arange(units, dtype=jnp.int32)[None, :]
+    kept_new = jnp.sum(jnp.where(matches, new_of_old[None, :], 0), axis=1) * small + kept % small
+
+    def places(position):
+        whole = position < bigs * big
+        place = jnp.where(whole, position % big, position % small)
+        side = jnp.where(whole, SIDE_BIG, SIDE_SMALL)
+        row = place // side
+        part = (position % big) // small
+        return (row, place - row * side, jnp.where(whole, 0, part), position // big)
+
+    return places, old_of_new, kept_new
 
 
 def sine_table(row_pos, col_pos, width):
@@ -111,30 +134,150 @@
     return centered * lax.rsqrt(spread + 1e-06) * gain + shift
 
 
-def attend(queries, key_rows, values, image, heads):
-    count, width = queries.shape
+LOG2E = 1.4426950408889634
+SEGMENTS = 16
+FAR = -1e30
+CONTRACT_ROWS = (((0,), (0,)), ((), ()))
+CONTRACT_PLAIN = (((1,), (0,)), ((), ()))
+CONTRACT_LANES = (((1,), (1,)), ((), ()))
+
+
+def tile_dot(left, right, dims):
+    return lax.dot_general(left, right, dims, preferred_element_type=jnp.float32)
+
+
+def attend_fwd_kernel(heads, size, q_ref, k_ref, v_ref, away_ref, own_ref, o_ref, lse_ref):
+    factor = LOG2E / math.sqrt(size)
+    away, own = away_ref[0], own_ref[0]
+
+    def one_head(head, carry):
+        rows = pl.ds(pl.multiple_of(head * size, size), size)
+        queries = jnp.concatenate([q_ref[0, rows, :], away], axis=0)
+        keys = jnp.concatenate([k_ref[0, rows, :], own], axis=0)
+        scores = tile_dot(keys, queries, CONTRACT_ROWS)
+        top = jnp.max(scores, axis=0, keepdims=True)
+        shifted = jnp.exp2((scores - top) * factor)
+        total = jnp.sum(shifted, axis=0, keepdims=True)
+        weights = (shifted * (1.0 / total)).astype(jnp.bfloat16)
+        o_ref[0, rows, :] = tile_dot(v_ref[0, rows, :], weights, CONTRACT_PLAIN).astype(o_ref.dtype)
+        lse_ref[0, pl.ds(head, 1), :] = top * factor + jnp.log2(total)
+        return carry
+
+    lax.fori_loop(0, heads, one_head, 0)
+
+
+def attend_bwd_kernel(
+    heads, size, q_ref, k_ref, v_ref, do_ref, lse_ref, away_ref, own_ref, dq_ref, dk_ref, dv_ref
+):
+    scale = 1.0 / math.sqrt(size)
+    factor = LOG2E * scale
+    away, own = away_ref[0], own_ref[0]
+
+    def one_head(head, carry):
+        rows = pl.ds(pl.multiple_of(head * size, size), size)
+        q_rows, k_rows, do_rows = q_ref[0, rows, :], k_ref[0, rows, :], do_ref[0, rows, :]
+        queries = jnp.concatenate([q_rows, away], axis=0)
+        keys = jnp.concatenate([k_rows, own], axis=0)
+        scores = tile_dot(keys, queries, CONTRACT_ROWS)
+        weights = jnp.exp2(scores * factor - lse_ref[0, pl.ds(head, 1), :])
+        spread = tile_dot(v_ref[0, rows, :], do_rows, CONTRACT_ROWS)
+        product = weights * spread
+        inner = jnp.sum(product, axis=0, keepdims=True)
+        dscores = (product - weights * inner).astype(jnp.bfloat16)
+        rounded = weights.astype(jnp.bfloat16)
+        dv_ref[0, rows, :] = tile_dot(do_rows, rounded, CONTRACT_LANES).astype(dv_ref.dtype)
+        dk_ref[0, rows, :] = (tile_dot(q_rows, dscores, CONTRACT_LANES) * scale).astype(dk_ref.dtype)
+        dq_ref[0, rows, :] = (tile_dot(k_rows, dscores, CONTRACT_PLAIN) * scale).astype(dq_ref.dtype)
+        return carry
+
+    lax.fori_loop(0, heads, one_head, 0)
+
+
+def attend_specs(groups, width, count, heads):
     size = width // heads
-    scale = 1.0 / math.sqrt(size)
-    same = image[:, None] == image[None, :]
-
-    def split_heads(tensor):
-        return tensor.reshape(count, heads, size).transpose(1, 0, 2)
-
-    def one_head(trio):
-        query_head, key_head, value_head = trio
-        scores = grad_round(matmul(query_head, key_head.T) * scale)
-        scores = jnp.where(same, scores, -1e30)
-        shifted = jnp.exp(scores - jnp.max(scores, axis=1, keepdims=True))
-        weights = value_round(shifted / jnp.sum(shifted, axis=1, keepdims=True))
-        return matmul(weights, value_head)
-
-    mixed = lax.map(
-        jax.checkpoint(one_head), (split_heads(queries), split_heads(key_rows), split_heads(values))
-    )
-    return mixed.transpose(1, 0, 2).reshape(count, width)
-
-
-def block(stream, image, params, heads):
+    step = 8 if heads % 8 == 0 else heads
+    wide = pl.BlockSpec((1, step * size, count), lambda g, i: (g, i, 0))
+    stats = pl.BlockSpec((1, step, count), lambda g, i: (g, i, 0))
+    marks = pl.BlockSpec((1, SEGMENTS, count), lambda g, i: (g, 0, 0))
+    return size, step, (groups, heads // step), wide, stats, marks
+
+
+def attend_forward(queries, keys, values, away, own, heads):
+    groups, width, count = queries.shape
+    size, step, grid, wide, stats, marks = attend_specs(groups, width, count, heads)
+    return pl.pallas_call(
+        functools.partial(attend_fwd_kernel, step, size),
+        grid=grid,
+        in_specs=[wide, wide, wide, marks, marks],
+        out_specs=[wide, stats],
+        out_shape=[
+            jax.ShapeDtypeStruct((groups, width, count), jnp.bfloat16),
+            jax.ShapeDtypeStruct((groups, heads, count), jnp.float32),
+        ],
+        compiler_params=pltpu.CompilerParams(vmem_limit_bytes=60 << 20),
+        cost_estimate=pl.CostEstimate(
+            flops=4 * groups * width * count * count,
+            bytes_accessed=8 * groups * width * count,
+            transcendentals=groups * heads * count * count,
+        ),
+        name="attend_forward",
+    )(queries, keys, values, away, own)
+
+
+def attend_backward(queries, keys, values, grads, lse, away, own, heads):
+    groups, width, count = queries.shape
+    size, step, grid, wide, stats, marks = attend_specs(groups, width, count, heads)
+    shape = jax.ShapeDtypeStruct((groups, width, count), jnp.bfloat16)
+    return pl.pallas_call(
+        functools.partial(attend_bwd_kernel, step, size),
+        grid=grid,
+        in_specs=[wide, wide, wide, wide, stats, marks, marks],
+        out_specs=[wide, wide, wide],
+        out_shape=[shape, shape, shape],
+        compiler_params=pltpu.CompilerParams(vmem_limit_bytes=60 << 20),
+        cost_estimate=pl.CostEstimate(
+            flops=10 * groups * width * count * count,
+            bytes_accessed=14 * groups * width * count,
+            transcendentals=groups * heads * count * count,
+        ),
+        name="attend_backward",
+    )(queries, keys, values, grads, lse, away, own)
+
+
+def attend_plain(heads, queries, keys, values, away, own):
+    return attend_keep(heads, queries, keys, values, away, own)[0]
+
+
+def attend_keep(heads, queries, keys, values, away, own):
+    queries, keys, values = (t.astype(jnp.bfloat16) for t in (queries, keys, values))
+    mixed, lse = attend_forward(queries, keys, values, away, own, heads)
+    return mixed.astype(jnp.float32), (queries, keys, values, lse, away, own)
+
+
+def attend_pull(heads, saved, grad):
+    queries, keys, values, lse, away, own = saved
+    dq, dk, dv = attend_backward(queries, keys, values, grad.astype(jnp.bfloat16), lse, away, own, heads)
+    none = jnp.zeros_like(away)
+    return tuple(t.astype(jnp.float32) for t in (dq, dk, dv)) + (none, none)
+
+
+def attend(queries, keys, values, marks, heads):
+    rule = jax.custom_vjp(attend_plain, nondiff_argnums=(0,))
+    rule.defvjp(attend_keep, attend_pull)
+    return rule(heads, queries, keys, values, marks[0], marks[1])
+
+
+def gelu(value):
+    return 0.5 * value * (1.0 + lax.erf(value * math.sqrt(0.5)))
+
+
+def segment_marks(segment, groups):
+    segment = segment.reshape(groups, 1, -1)
+    hot = segment == jnp.arange(SEGMENTS, dtype=jnp.int32)[None, :, None]
+    return (jnp.where(hot, 0.0, 1.0).astype(jnp.bfloat16), jnp.where(hot, FAR, 0.0).astype(jnp.bfloat16))
+
+
+def block(stream, marks, params, heads):
     (
         gain_one,
         shift_one,
@@ -151,21 +294,23 @@
         bias_down,
     ) = params
     width = stream.shape[1]
-    normed = value_round(layer_norm(stream, gain_one, shift_one))
-    joined = matmul(normed, w_qkv)
-    queries = both(joined[:, :width] + bias_query)
+    groups = marks[0].shape[0]
+    normed = value_round(layer_norm(stream, gain_one, shift_one)).reshape(groups, -1, width)
+    joined = jnp.einsum("gtd,df->gft", normed, w_qkv, preferred_element_type=jnp.float32)
+    queries = both(joined[:, :width] + bias_query[None, :, None])
     key_rows = both(joined[:, width : 2 * width])
-    values = both(joined[:, 2 * width :] + bias_value)
-    mixed = both(attend(queries, key_rows, values, image, heads))
-    stream = stream + grad_round(matmul(mixed, w_out) + bias_out)
+    values = both(joined[:, 2 * width :] + bias_value[None, :, None])
+    mixed = both(attend(queries, key_rows, values, marks, heads))
+    projected = jnp.einsum("gft,fd->gtd", mixed, w_out, preferred_element_type=jnp.float32).reshape(-1, width)
+    stream = stream + grad_round(projected + bias_out)
     normed = value_round(layer_norm(stream, gain_two, shift_two))
     hidden = grad_round(matmul(normed, w_up) + bias_up)
     return stream + grad_round(
-        matmul(value_round(jax.nn.gelu(hidden, approximate=False)), w_down) + bias_down
-    )
-
-
-def section_a(mats, gain_vec, bias_vec, pixel_rows, kept, resolution):
+        matmul(value_round(gelu(hidden)), w_down) + bias_down
+    )
+
+
+def section_a(mats, gain_vec, bias_vec, pixel_rows, kept, order):
     w_patch, w_qkv, w_out, w_up, w_lift = pieces(mats[0], (D, 3 * D, D, FF, DD))
     gain_one, gain_two, gain_final = pieces(gain_vec, (D, D, D))
     (
@@ -182,13 +327,13 @@
         mask_token,
     ) = pieces(bias_vec, (D, D, D, D, D, D, FF, D, D, DD, DD))
     count = pixel_rows.shape[0]
-    image, rows, cols = layout(resolution, count)
-    stream = grad_round(matmul(pixel_rows[kept], w_patch) + bias_patch) + sine_table(
-        rows[kept], cols[kept], D
-    )
+    places, unused, kept_new = order
+    rows, cols, part, run = places(kept_new)
+    stream = grad_round(matmul(pixel_rows[kept], w_patch) + bias_patch) + sine_table(rows, cols, D)
+    runs = count // (SIDE_BIG * SIDE_BIG)
     stream = block(
         stream,
-        image[kept],
+        segment_marks(part * runs + run, 1),
         (
             gain_one,
             shift_one,
@@ -209,11 +354,12 @@
     lifted = grad_round(
         matmul(value_round(layer_norm(stream, gain_final, shift_final)), w_lift) + bias_lift
     )
-    full = jnp.broadcast_to(mask_token[None, :], (count, DD)).at[kept].set(lifted)
+    full = jnp.broadcast_to(mask_token[None, :], (count, DD)).at[kept_new].set(lifted)
+    rows, cols, part, run = places(jnp.arange(count, dtype=jnp.int32))
     return full + sine_table(rows, cols, DD)
 
 
-def section_b(mats, gain_vec, bias_vec, stream, pixel_rows, kept, resolution, denom):
+def section_b(mats, gain_vec, bias_vec, stream, pixel_rows, order, denom):
     w_qkv, w_out, w_up, w_head = pieces(mats[0], (3 * DD, DD, DFF, PIX))
     gain_one, gain_two, gain_final = pieces(gain_vec[3 * D :], (DD, DD, DD))
     (
@@ -228,10 +374,11 @@
         bias_head,
     ) = pieces(bias_vec[8 * D + FF + 2 * DD :], (DD, DD, DD, DD, DD, DFF, DD, DD, PIX))
     count = pixel_rows.shape[0]
-    image, rows, cols = layout(resolution, count)
+    places, old_of_new, kept_new = order
+    rows, cols, part, run = places(jnp.arange(count, dtype=jnp.int32))
     stream = block(
         stream,
-        image,
+        segment_marks(part, count // (SIDE_BIG * SIDE_BIG)),
         (
             gain_one,
             shift_one,
@@ -252,10 +399,13 @@
     predicted = grad_round(
         matmul(value_round(layer_norm(stream, gain_final, shift_final)), w_head) + bias_head
     )
+    units = pixel_rows.reshape(-1, SIDE_SMALL * SIDE_SMALL, PIX)
+    pixel_rows = units[old_of_new].reshape(count, PIX).astype(jnp.float32)
     centered = pixel_rows - jnp.mean(pixel_rows, axis=1, keepdims=True)
     target = centered * lax.rsqrt(jnp.mean(centered * centered, axis=1, keepdims=True) + 1e-06)
     error = jnp.mean((predicted - target) ** 2, axis=1)
-    weight = jnp.ones((count,), jnp.float32).at[kept].set(0.1)
+    chosen = jnp.any(jnp.arange(count, dtype=jnp.int32)[:, None] == kept_new[None, :], axis=1)
+    weight = jnp.where(chosen, 0.1, 1.0)
     return jnp.sum(error * weight) / denom
 
 
@@ -299,14 +449,14 @@
     devices = lax.axis_size("dp") * lax.axis_size("fsdp")
     patches_all = pixels.shape[0] * devices
     denom = (0.75 + 0.1 * 0.25) * patches_all
-    pixel_rows = pixels.astype(jnp.float32)
+    order = layout(resolution, kept, pixels.shape[0])
     cotangent = jnp.ones((), jnp.float32)
 
     def forward_a(mats, gain_vec, bias_vec):
-        return section_a(mats, gain_vec, bias_vec, pixel_rows, kept, resolution)
+        return section_a(mats, gain_vec, bias_vec, pixels, kept, order)
 
     def forward_b(mats, gain_vec, bias_vec, stream):
-        return section_b(mats, gain_vec, bias_vec, stream, pixel_rows, kept, resolution, denom)
+        return section_b(mats, gain_vec, bias_vec, stream, pixels, order, denom)
 
     encoder_whole = widen(
         (

time: 2090 us -> 1420 us (0.68)
  matrix products: 509 us -> 135 us
  other arithmetic: 408 us -> 91.2 us
  local copies, waits for them, and re-layouts: 196 us -> 52.6 us
  Pallas kernels: 0 us -> 134 us
  waiting for transfers between devices: 818 us -> 852 us
    dot_general x228 -> x20, matrix products: 509 us -> 96.5 us  [matmul(): return jnp.dot(left, right, preferred_element_type=jnp.float32)]
    pallas_call x0 -> x4, Pallas kernels: none -> 134 us  [the longest x2 80.6 us: attend(): return rule(heads, queries, keys, values, marks[0], marks[1])]
    reduce_sum x94 -> x16, other arithmetic: 136 us -> 7.7 us  [the longest x2 2.22 us: block(): queries = both(joined[:, :width] + bias_query[None, :, None])]
    convert_element_type x28 -> x3, other arithmetic: 97.8 us -> 1.94 us  [the longest x2 1.28 us: segment_marks(): jnp.where(hot, FAR, 0.0).astype(jnp.bfloat16)]
    convert_element_type x36 -> x8, other arithmetic: 72.2 us -> 7.46 us  [round_plain(): value.astype(jnp.bfloat16)]
    squeeze x56 -> x0, local copies, waits for them, and re-layouts: 57.9 us -> none  [attend(): lax.map(jax.checkpoint(one_head), (split_heads(queries), split_heads(key_...]
    dot_general x0 -> x12, matrix products: none -> 38.7 us  [the longest x6 25.9 us: block(): jnp.einsum('gtd,df->gft', normed, w_qkv, preferred_element_type=jnp.float32)]
    dynamic_slice x56 -> x0, local copies, waits for them, and re-layouts: 30.4 us -> none  [attend(): lax.map(jax.checkpoint(one_head), (split_heads(queries), split_heads(key_...]
  transfers between devices with their start and end apart: 9 -> 9, of which waited for: 8 -> 8; matrix products, arithmetic and copies ran while one was open for 22% -> 11% of each run, Pallas kernels for 0% -> 4%
where the time goes in v1:
time: 1420 us; the launch traced here: 1410 us
  waiting for transfers between devices  852 us (60%)
  matrix products  135 us (10%)
  Pallas kernels  134 us (9%)
  blocking collectives  123 us (9%)
  other arithmetic  91.2 us (6%)
  local copies, waits for them, and re-layouts  52.6 us (4%)
  between operations  24.7 us (2%)
    reduce_scatter x1, waiting for transfers between devices, per_device(): lax.psum_scatter(encoder_terms[0], ('dp', 'fsdp'), scatter_dimension=0, t...  234 us
    reduce_scatter x1, waiting for transfers between devices, per_device(): lax.psum_scatter(decoder_terms[0], ('dp', 'fsdp'), scatter_dimension=0, t...  217 us
    reduce_scatter x1, waiting for transfers between devices, per_device(): lax.psum_scatter(decoder_terms[1], ('dp', 'fsdp'), scatter_dimension=0, t...  149 us
    reduce_scatter x1, waiting for transfers between devices, per_device(): lax.psum_scatter(encoder_terms[1], ('dp', 'fsdp'), scatter_dimension=0, t...  138 us
    dot_general x20, matrix products, matmul(): return jnp.dot(left, right, preferred_element_type=jnp.float32)  96.5 us
    unnamed x2, blocking collectives  82.9 us
    pallas_call x2, Pallas kernels, attend(): return rule(heads, queries, keys, values, marks[0], marks[1])  80.6 us
    pallas_call x2, Pallas kernels, attend_forward(): pl.pallas_call(functools.partial(attend_fwd_kernel, step, size), grid=gri...  53.2 us
  transfers between devices with their start and end apart: 9, of which 8 were waited for; matrix products, arithmetic and copies ran while one was open for 11% of the time, Pallas kernels for 4%

profile of v1, /device:TPU:0, one launch (start us, length us, event | category | flops | bytes accessed | tf_op | source)
XLA Modules:
  0.0 1413.1 jit_solution(3381133450292847030)
XLA Ops:
  18.2 43.7 %all-reduce.48 = (bf16[16640]{0:T(1024)(128)(2,1)S(1)}, bf16[3840]{0:T(1024)(128)(2,1)S(1)}) all-reduce(bf16[16640]{0:T(1024)(128)(2,1)S(1)} %dynamic-update-slice, bf16[3840]{0:T(1024)(128)(2,1)S(1)} %dynamic-update-slice.1), channel_id=1, replica_groups=mesh['dp'=4,'fsdp'=8] {'dp','fsdp'}, use_global_device_ids=true, to_apply=%add.43 | all-reduce | flops 20480 | bytes 81920
  74.5 5.0 gather_fusion
  89.1 7.2 multiply_sine_fusion.1
  96.3 8.3 all-gather.5.cloned.1.call-done
  114.1 10.3 attend_forward.2
  127.3 6.6 multiply_convert_fusion.2
  133.9 36.4 %all-gather.7.cloned.1.call-done = bf16[3072,768]{1,0:T(8,128)(2,1)} async-done(((bf16[96,768]{1,0:T(8,128)(2,1)}), bf16[3072,768]{1,0:T(8,128)(2,1)}) %all-gather.7.cloned.1.call-update) | async-done | bytes 4718608 | tf_op jit(solution)/shard_map/all_gather | solution.py:464
  170.4 5.2 fusion.126
  190.4 46.4 %all-gather.9.cloned.1.call-done = bf16[512,4864]{1,0:T(8,128)(2,1)} async-done(((bf16[16,4864]{1,0:T(8,128)(2,1)}), bf16[512,4864]{1,0:T(8,128)(2,1)}) %all-gather.9.cloned.1.call-update) | async-done | bytes 4980752 | tf_op jit(solution)/shard_map/all_gather | solution.py:475
  236.8 5.2 convolution_bitcast_fusion
  245.8 42.9 %attend_forward.3 = (bf16[2,512,784]{2,1,0:T(8,128)(2,1)}, f32[2,16,784]{2,1,0:T(8,128)}) custom-call(bf16[2,512,784]{2,1,0:T(8,128)(2,1)} %get-tuple-element.102.q_ref, bf16[2,512,784]{2,1,0:T(8,128)(2,1)} %slice.316.k_ref, bf16[2,512,784]{2,1,0:T(8,128)(2,1)} %get-tuple-element.101.v_ref, bf16[2,16,784]{2,1,0:T(8,128)(2,1)} %get-tuple-element.136.away_ref, ...), custom_call_target="tpu_custom_call" | custom-call | flops 2517630976 | bytes 6422528 | tf_op jit(solution)/shard_map/attend_forward/pallas_call | solution.py:208
  294.4 10.1 multiply_convert_fusion
  304.5 8.2 fusion.127
  313.9 6.6 multiply_convert_fusion.1
  328.0 11.3 add_convert_fusion
  339.3 4.6 multiply_reduce_fusion.2
  353.8 67.8 %transpose_jvp_attend_backward__.2 = (bf16[2,512,784]{2,1,0:T(8,128)(2,1)}, bf16[2,512,784]{2,1,0:T(8,128)(2,1)}, bf16[2,512,784]{2,1,0:T(8,128)(2,1)}) custom-call(bf16[2,512,784]{2,1,0:T(8,128)(2,1)} %get-tuple-element.102.q_ref, bf16[2,512,784]{2,1,0:T(8,128)(2,1)} %slice.316.k_ref, bf16[2,512,784]{2,1,0:T(8,128)(2,1)} %get-tuple-element.101.v_ref, ...), custom_call_target="tpu_custom_call" | custom-call | flops 6294077440 | bytes 11239424 | tf_op jit(solution)/shard_map/transpose(jvp(attend_backward))/pallas_call | solution.py:267
  432.3 4.6 fusion.128
  450.2 6.8 add_convert_fusion.1
  462.1 12.8 transpose_jvp_attend_backward__.3
  480.5 4.4 multiply_reduce_fusion.10
  487.5 8.7 fusion.135
  498.1 5.1 fusion.132
  508.6 5.3 fusion.16
  532.2 7.9 pad_add_fusion
  542.4 39.2 %all-reduce.45 = f32[3840]{0:T(1024)S(1)} all-reduce(f32[3840]{0:T(1024)S(1)} %pad_add_fusion.10), channel_id=6, replica_groups=mesh['dp'=4,'fsdp'=8] {'dp','fsdp'}, use_global_device_ids=true, to_apply=%region_53.54.clone | all-reduce | flops 3840 | bytes 30720
  582.3 23.3 %all-reduce.51.cloned.1.call-done = f32[16640]{0:T(1024)} async-done(((f32[16640]{0:T(1024)}), f32[16640]{0:T(1024)}) %all-reduce.51.cloned.1.call-update) | async-done | bytes 66576
  607.0 148.9 %reduce-scatter.11.cloned.1.call-done = f32[64,512]{1,0:T(8,128)} async-done(((f32[2048,512]{1,0:T(8,128)}), f32[64,512]{1,0:T(8,128)}) %reduce-scatter.11.cloned.1.call-update) | async-done | bytes 131088 | tf_op jit(solution)/shard_map/reduce_scatter | solution.py:496
  757.5 138.3 %reduce-scatter.7.cloned.1.call-done = f32[96,768]{1,0:T(8,128)} async-done(((f32[3072,768]{1,0:T(8,128)}), f32[96,768]{1,0:T(8,128)}) %reduce-scatter.7.cloned.1.call-update) | async-done | bytes 294928 | tf_op jit(solution)/shard_map/reduce_scatter | solution.py:508
  897.4 216.6 %reduce-scatter.9.cloned.1.call-done = f32[16,4864]{1,0:T(8,128)} async-done(((f32[512,4864]{1,0:T(8,128)}), f32[16,4864]{1,0:T(8,128)}) %reduce-scatter.9.cloned.1.call-update) | async-done | bytes 311312 | tf_op jit(solution)/shard_map/reduce_scatter | solution.py:495
  1115.7 233.7 %reduce-scatter.5.cloned.1.call-done = f32[24,7424]{1,0:T(8,128)} async-done(((f32[768,7424]{1,0:T(8,128)}), f32[24,7424]{1,0:T(8,128)}) %reduce-scatter.5.cloned.1.call-update) | async-done | bytes 712720 | tf_op jit(solution)/shard_map/reduce_scatter | solution.py:507
  1355.2 40.1 %all-reduce.47 = (f32[]{:T(128)}, f32[]{:T(128)}) all-reduce(f32[]{:T(128)S(6)} %div.307, f32[]{:T(128)S(6)} %add.767), channel_id=1, replica_groups=mesh['dp'=4,'fsdp'=8] {'dp','fsdp'}, use_global_device_ids=true, to_apply=%region_25.26 | all-reduce | flops 2 | bytes 16 | tf_op jit(solution)/shard_map/psum | solution.py:485
  (434 shorter events, 166.8 us)
Async XLA Ops:
  7.2 56.6 %copy-start.101 = (s32[8]{0:T(128)S(1)}, s32[8]{0:T(128)}, u32[]{:S(2)}) copy-start(s32[8]{0:T(128)} %param.23) | copy-start | bytes 100
  7.2 56.4 %copy-start.93 = (s32[392]{0:T(512)S(1)}, s32[392]{0:T(512)}, u32[]{:S(2)}) copy-start(s32[392]{0:T(512)} %param.24) | copy-start | bytes 4708
  7.2 58.0 %copy-start.9 = (bf16[1568,768]{1,0:T(8,128)(2,1)S(1)}, bf16[1568,768]{1,0:T(8,128)(2,1)}, u32[]{:S(2)}) copy-start(bf16[1568,768]{1,0:T(8,128)(2,1)} %param.22) | copy-start | bytes 7225348
  7.2 97.4 %all-gather.5.cloned.1.call-start = ((), (), s32[]{:S(2)}) async-start(), calls=%async_computation.4 | async-start | bytes 11759616 | tf_op jit(solution)/shard_map/all_gather | solution.py:463
  9.3 161.0 %all-gather.7.cloned.1.call-start = ((), (), s32[]{:S(2)}) async-start(), calls=%async_computation.5 | async-start | bytes 4866048 | tf_op jit(solution)/shard_map/all_gather | solution.py:464
  11.0 225.8 %all-gather.9.cloned.1.call-start = ((), (), s32[]{:S(2)}) async-start(), calls=%async_computation.6 | async-start | bytes 5136384 | tf_op jit(solution)/shard_map/all_gather | solution.py:475
  12.8 291.7 %all-gather.11.cloned.1.call-start = ((), (), s32[]{:S(2)}) async-start(), calls=%async_computation.7 | async-start | bytes 2162688 | tf_op jit(solution)/shard_map/all_gather | solution.py:476
  14.4 591.2 %all-reduce.51.cloned.1.call-start = ((), (), s32[]{:S(2)}) async-start(), calls=%async_computation.12 | async-start | bytes 139264
  61.9 65.4 %copy-start.91 = (f32[3072]{0:T(1024)}, f32[3072]{0:T(1024)S(1)}, u32[]{:S(2)}) copy-start(f32[3072]{0:T(1024)S(1)} %slice.245) | copy-start | bytes 36868
  61.9 45.1 %copy-start.70 = (f32[768]{0:T(1024)}, f32[768]{0:T(1024)S(1)}, u32[]{:S(2)}) copy-start(f32[768]{0:T(1024)S(1)} %get-tuple-element.134) | copy-start | bytes 9220
  61.9 65.1 %copy-start.72 = (f32[768]{0:T(1024)}, f32[768]{0:T(1024)S(1)}, u32[]{:S(2)}) copy-start(f32[768]{0:T(1024)S(1)} %get-tuple-element.133) | copy-start | bytes 9220
  126.7 43.7 %copy-start.12 = (f32[392,768]{1,0:T(8,128)}, f32[392,768]{1,0:T(8,128)S(1)}, u32[]{:S(2)}) copy-start(f32[392,768]{1,0:T(8,128)S(1)} %get-tuple-element.161) | copy-start | bytes 3612676
  447.3 32.2 %copy-start.37 = (bf16[392,512]{1,0:T(8,128)(2,1)}, bf16[392,512]{1,0:T(8,128)(2,1)S(1)}, u32[]{:S(2)}) copy-start(bf16[392,512]{1,0:T(8,128)(2,1)S(1)} %select_convert_fusion) | copy-start | bytes 1204228
  450.1 29.3 %copy-start.49 = (bf16[392,768]{1,0:T(8,128)(2,1)}, bf16[392,768]{1,0:T(8,128)(2,1)S(1)}, u32[]{:S(2)}) copy-start(bf16[392,768]{1,0:T(8,128)(2,1)S(1)} %add_convert_fusion.10) | copy-start | bytes 1806340
  487.4 268.5 %reduce-scatter.11.cloned.1.call-start = ((), (), s32[]{:S(2)}) async-start(), calls=%async_computation.11 | async-start | bytes 4325376 | tf_op jit(solution)/shard_map/reduce_scatter | solution.py:496
  496.2 399.5 %reduce-scatter.7.cloned.1.call-start = ((), (), s32[]{:S(2)}) async-start(), calls=%async_computation.9 | async-start | bytes 9732096 | tf_op jit(solution)/shard_map/reduce_scatter | solution.py:508
  503.2 610.8 %reduce-scatter.9.cloned.1.call-start = ((), (), s32[]{:S(2)}) async-start(), calls=%async_computation.10 | async-start | bytes 10272768 | tf_op jit(solution)/shard_map/reduce_scatter | solution.py:495
  522.7 826.7 %reduce-scatter.5.cloned.1.call-start = ((), (), s32[]{:S(2)}) async-start(), calls=%async_computation.8 | async-start | bytes 23519232 | tf_op jit(solution)/shard_map/reduce_scatter | solution.py:507
  540.1 856.1 %copy-start.102 = (f32[120]{0:T(128)S(1)}, f32[120]{0:T(128)}, u32[]{:S(2)}) copy-start(f32[120]{0:T(128)} %param.30) | copy-start | bytes 1444
  540.1 856.1 %copy-start.103 = (f32[120]{0:T(128)S(1)}, f32[120]{0:T(128)}, u32[]{:S(2)}) copy-start(f32[120]{0:T(128)} %param.42) | copy-start | bytes 1444
  540.1 856.1 %copy-start.104 = (f32[120]{0:T(128)S(1)}, f32[120]{0:T(128)}, u32[]{:S(2)}) copy-start(f32[120]{0:T(128)} %param.36) | copy-start | bytes 1444
  540.1 856.7 %copy-start.88 = (f32[520]{0:T(1024)S(1)}, f32[520]{0:T(1024)}, u32[]{:S(2)}) copy-start(f32[520]{0:T(1024)} %param.31) | copy-start | bytes 6244
  540.1 856.7 %copy-start.97 = (f32[520]{0:T(1024)S(1)}, f32[520]{0:T(1024)}, u32[]{:S(2)}) copy-start(f32[520]{0:T(1024)} %param.43) | copy-start | bytes 6244
  540.1 856.7 %copy-start.98 = (f32[520]{0:T(1024)S(1)}, f32[520]{0:T(1024)}, u32[]{:S(2)}) copy-start(f32[520]{0:T(1024)} %param.37) | copy-start | bytes 6244
  540.1 858.1 %copy-start.66 = (f32[64,512]{1,0:T(8,128)S(1)}, f32[64,512]{1,0:T(8,128)}, u32[]{:S(2)}) copy-start(f32[64,512]{1,0:T(8,128)} %param.29) | copy-start | bytes 393220
  540.1 859.9 %copy-start.57 = (f32[16,4864]{1,0:T(8,128)S(1)}, f32[16,4864]{1,0:T(8,128)}, u32[]{:S(2)}) copy-start(f32[16,4864]{1,0:T(8,128)} %param.28) | copy-start | bytes 933892
  540.2 859.9 %copy-start.67 = (f32[16,4864]{1,0:T(8,128)S(1)}, f32[16,4864]{1,0:T(8,128)}, u32[]{:S(2)}) copy-start(f32[16,4864]{1,0:T(8,128)} %param.40) | copy-start | bytes 933892
  540.2 862.0 %copy-start.58 = (f32[96,768]{1,0:T(8,128)S(1)}, f32[96,768]{1,0:T(8,128)}, u32[]{:S(2)}) copy-start(f32[96,768]{1,0:T(8,128)} %param.27) | copy-start | bytes 884740
  757.4 645.8 %copy-start.41 = (f32[24,7424]{1,0:T(8,128)S(1)}, f32[24,7424]{1,0:T(8,128)}, u32[]{:S(2)}) copy-start(f32[24,7424]{1,0:T(8,128)} %param.26) | copy-start | bytes 2138116
  757.4 645.8 %copy-start.60 = (f32[24,7424]{1,0:T(8,128)S(1)}, f32[24,7424]{1,0:T(8,128)}, u32[]{:S(2)}) copy-start(f32[24,7424]{1,0:T(8,128)} %param.38) | copy-start | bytes 2138116
  895.7 506.4 %copy-start.59 = (f32[96,768]{1,0:T(8,128)S(1)}, f32[96,768]{1,0:T(8,128)}, u32[]{:S(2)}) copy-start(f32[96,768]{1,0:T(8,128)} %reduce-scatter.7.cloned.1.call-done) | copy-start | bytes 884740
  1349.4 53.9 %copy-start.42 = (f32[24,7424]{1,0:T(8,128)S(1)}, f32[24,7424]{1,0:T(8,128)}, u32[]{:S(2)}) copy-start(f32[24,7424]{1,0:T(8,128)} %reduce-scatter.5.cloned.1.call-done) | copy-start | bytes 2138116
  (98 other events, 475.5 us)
Sparse Core Ops, SparseCore 0:
  11.5 93.0 all-gather.4
  108.1 62.2 all-gather.6
  173.9 62.9 all-gather.8
  240.2 54.8 all-gather.10
  487.6 117.9 all-reduce.50
  607.7 148.1 reduce-scatter.10
  761.8 133.8 reduce-scatter.6
  898.0 215.9 reduce-scatter.8
  1120.5 228.8 reduce-scatter.4

commit v2 on v1

--- a/solution.py
+++ b/solution.py
@@ -418,8 +418,358 @@
     return (weight_new, first_new, second_new)
 
 
+LANES = 128
+AXES = ("dp", "fsdp")
+GRID_DIMS = (2, 2, 4, 2)
+MESH_IDS = pl.DeviceIdType.MESH
+
+
+def place_of():
+    dp, fsdp = lax.axis_index("dp"), lax.axis_index("fsdp")
+    x, core = dp // 2, dp % 2
+    z, y = fsdp // 2, fsdp % 2
+    flip_x = ((1 - x) * 2 + core, fsdp)
+    flip_y = (dp, z * 2 + 1 - y)
+
+    def choose(zero, one):
+        return tuple(a * (1 - core) + b * core for a, b in zip(zero, one))
+
+    partners = [(x * 2 + 1 - core, fsdp), choose(flip_x, flip_y), choose(flip_y, flip_x)]
+    partners += [(dp, lax.rem(z + step, 4) * 2 + y) for step in (1, 2, 3)]
+    return x, core, z, y, partners
+
+
+def greet(partners):
+    barrier = pltpu.get_barrier_semaphore()
+    for partner in partners:
+        pl.semaphore_signal(barrier, inc=1, device_id=partner, device_id_type=MESH_IDS)
+    pl.semaphore_wait(barrier, len(partners))
+
+
+def column_cuts(columns, parts):
+    tiles = columns // LANES
+    cuts = [LANES * (tiles * part // parts) for part in range(parts + 1)]
+    return [(low, high - low) for low, high in zip(cuts[:-1], cuts[1:])]
+
+
+def xy_of(core, first, second):
+    return first * (1 - core) + second * core, second * (1 - core) + first * core
+
+
+def scatter_kernel(chunks, slots, arrays, *refs):
+    sources, loss_ref = refs[:arrays], refs[arrays]
+    outs, total_ref = refs[arrays + 1 : 2 * arrays + 1], refs[2 * arrays + 1]
+    scratch = refs[2 * arrays + 2 :]
+    count = len(chunks)
+    arrive = [scratch[4 * j : 4 * j + 4] for j in range(count)]
+    kept = scratch[4 * count : -7]
+    own = [kept[slot].at[:, :, pl.ds(0, width)] for slot, width in slots]
+    pair, quad, send_sem, recv_sem, own_sem, last_send, last_recv = scratch[-7:]
+    x, core, z, y, partners = place_of()
+    first, second = xy_of(core, x, y)
+
+    def remote(source, target, j, phase, partner):
+        return pltpu.make_async_remote_copy(
+            source, target, send_sem.at[j, phase], recv_sem.at[j, phase], device_id=partner, device_id_type=MESH_IDS
+        )
+
+    def view(j, side, b1, b2):
+        array, low, width = chunks[j]
+        at_x, at_y = xy_of(side, b1, b2)
+        return sources[array].at[at_x, side, :, at_y, :, pl.ds(low, width)]
+
+    def start_swap(j):
+        for b1 in range(2):
+            for b2 in range(2):
+                place = pl.ds((b1 * 2 + b2) * 4, 4)
+                remote(view(j, 1 - core, b1, b2), arrive[j][0].at[place], j, 0, partners[0]).start()
+
+    def start_own(j):
+        for b1 in range(2):
+            for b2 in range(2):
+                place = pl.ds((b1 * 2 + b2) * 4, 4)
+                pltpu.make_async_copy(view(j, core, b1, b2), own[j].at[place], own_sem.at[j]).start()
+
+    def whole(j, phase):
+        buffer = arrive[j][phase]
+        return pltpu.make_async_copy(buffer, buffer, recv_sem.at[j, phase])
+
+    def add_into(target, other, offset, blocks):
+        def step(n, carry):
+            target[n] = target[n] + other[offset + n]
+            return carry
+
+        lax.fori_loop(0, blocks, step, 0)
+
+    sends = []
+
+    def stage_one(j):
+        pltpu.make_async_copy(own[j], own[j], own_sem.at[j]).wait()
+        whole(j, 0).wait()
+        add_into(arrive[j][0], own[j], 0, 16)
+        remote(arrive[j][0].at[pl.ds((1 - first) * 8, 8)], arrive[j][1], j, 1, partners[1]).start()
+
+    def stage_two(j):
+        whole(j, 1).wait()
+        add_into(arrive[j][1], arrive[j][0], first * 8, 8)
+        remote(arrive[j][1].at[pl.ds((1 - second) * 4, 4)], arrive[j][2], j, 2, partners[2]).start()
+
+    def stage_three(j):
+        whole(j, 2).wait()
+        add_into(arrive[j][2], arrive[j][1], second * 4, 4)
+        for step in range(3):
+            there = lax.rem(z + step + 1, 4)
+            remote(arrive[j][2].at[there], arrive[j][3].at[step], j, 3 + step, partners[3 + step]).start()
+
+    def stage_four(j):
+        array, low, width = chunks[j]
+        for step in range(3):
+            slot = arrive[j][3].at[step]
+            pltpu.make_async_copy(slot, slot, recv_sem.at[j, 3 + step]).wait()
+        result = (arrive[j][2][z] + arrive[j][3][0]) + (arrive[j][3][1] + arrive[j][3][2])
+        outs[array][:, low : low + width] = result
+        square = result * result
+        rows = square.shape[0]
+        tile = functools.reduce(
+            jnp.add,
+            [square[r : r + 8, c : c + LANES] for r in range(0, rows, 8) for c in range(0, width, LANES)],
+        )
+        pair[0, 0] = pair[0, 0] + tile
+
+    greet(partners)
+    pair[0, 0] = jnp.zeros((8, LANES), jnp.float32)
+    pair[0, 1] = loss_ref[...]
+    ahead = 2
+    for j in range(min(ahead, count)):
+        start_swap(j)
+        start_own(j)
+    for t in range(count + 3):
+        if t < count:
+            if t + ahead < count:
+                start_swap(t + ahead)
+            stage_one(t)
+            if t + ahead < count:
+                start_own(t + ahead)
+        if 0 <= t - 1 < count:
+            stage_two(t - 1)
+        if 0 <= t - 2 < count:
+            stage_three(t - 2)
+        if 0 <= t - 3 < count:
+            stage_four(t - 3)
+
+    def share(source, target, n, partner):
+        return pltpu.make_async_remote_copy(
+            source, target, last_send.at[n], last_recv.at[n], device_id=partner, device_id_type=MESH_IDS
+        )
+
+    tail = []
+    for n in range(3):
+        copy = share(pair.at[n], pair.at[4 + n], n, partners[n])
+        copy.start()
+        copy.wait_recv()
+        tail.append(copy)
+        target = pair.at[n + 1] if n < 2 else quad.at[z]
+        target[...] = pair[n] + pair[4 + n]
+    for step in range(3):
+        copy = share(quad.at[z], quad.at[z], 3 + step, partners[3 + step])
+        copy.start()
+        tail.append(copy)
+    for copy in tail[3:]:
+        copy.wait_recv()
+    total_ref[...] = (quad[0] + quad[1]) + (quad[2] + quad[3])
+    for copy in tail:
+        copy.wait_send()
+    for j in range(count):
+        pltpu.make_async_copy(arrive[j][0], arrive[j][0], send_sem.at[j, 0]).wait()
+        pltpu.make_async_copy(arrive[j][1], arrive[j][1], send_sem.at[j, 1]).wait()
+        pltpu.make_async_copy(arrive[j][2], arrive[j][2], send_sem.at[j, 2]).wait()
+        for step in range(3):
+            slot = arrive[j][3].at[step]
+            pltpu.make_async_copy(slot, slot, send_sem.at[j, 3 + step]).wait()
+
+
+def scatter_sums(arrays, parts, loss, collective_id):
+    sources, chunks, slots, scratch_a, scratch_b = [], [], [], [], []
+    for index, (array, cuts) in enumerate(zip(arrays, parts)):
+        devices, rows, columns = array.shape
+        sources.append(array.reshape(GRID_DIMS + (rows, columns)))
+        cut = column_cuts(columns, cuts)
+        widest = max(width for low, width in cut)
+        base = len(scratch_b)
+        scratch_b += [pltpu.VMEM((16, rows, widest), jnp.float32)] * min(2, cuts)
+        for number, (low, width) in enumerate(cut):
+            chunks.append((index, low, width))
+            slots.append((base + number % 2, width))
+            scratch_a += [pltpu.VMEM((n, rows, width), jnp.float32) for n in (16, 8, 4, 3)]
+    count = len(chunks)
+    sent = sum(array.size for array in arrays) * 4
+    vmem = pl.BlockSpec(memory_space=pltpu.VMEM)
+    return pl.pallas_call(
+        functools.partial(scatter_kernel, tuple(chunks), tuple(slots), len(arrays)),
+        in_specs=[pl.BlockSpec(memory_space=pl.ANY)] * len(arrays) + [vmem],
+        out_specs=[vmem] * (len(arrays) + 1),
+        out_shape=[jax.ShapeDtypeStruct(a.shape[1:], jnp.float32) for a in arrays]
+        + [jax.ShapeDtypeStruct((2, 8, LANES), jnp.float32)],
+        scratch_shapes=scratch_a + scratch_b
+        + [
+            pltpu.VMEM((7, 2, 8, LANES), jnp.float32),
+            pltpu.VMEM((4, 2, 8, LANES), jnp.float32),
+            pltpu.SemaphoreType.DMA((count, 6)),
+            pltpu.SemaphoreType.DMA((count, 6)),
+            pltpu.SemaphoreType.DMA((count,)),
+            pltpu.SemaphoreType.DMA((6,)),
+            pltpu.SemaphoreType.DMA((6,)),
+        ],
+        compiler_params=pltpu.CompilerParams(
+            collective_id=collective_id, has_side_effects=True, vmem_limit_bytes=63 << 20
+        ),
+        cost_estimate=pl.CostEstimate(flops=sent // 2, bytes_accessed=3 * sent, transcendentals=0),
+        name="scatter_sums",
+    )(*sources, loss)
+
+
+def gather_kernel(chunks, arrays, *refs):
+    shards, wholes = refs[:arrays], refs[arrays : 2 * arrays]
+    send_sem, recv_sem, own_sem = refs[2 * arrays :]
+    x, core, z, y, partners = place_of()
+    first, second = xy_of(core, x, y)
+
+    def remote(source, target, j, phase, partner):
+        return pltpu.make_async_remote_copy(
+            source, target, send_sem.at[j, phase], recv_sem.at[j, phase], device_id=partner, device_id_type=MESH_IDS
+        )
+
+    def line(j, b1, b2):
+        array, low, width = chunks[j]
+        at_x, at_y = xy_of(core, b1, b2)
+        return wholes[array].at[at_x, core, :, at_y, :, pl.ds(low, width)]
+
+    def mine(j):
+        array, low, width = chunks[j]
+        return shards[array].at[:, pl.ds(low, width)], wholes[array].at[x, core, z, y, :, pl.ds(low, width)]
+
+    def along_z(j):
+        source, target = mine(j)
+        copies = [remote(source, target, j, step, partners[3 + step]) for step in range(3)]
+        return copies
+
+    def along_second(j):
+        return [remote(line(j, first, second), line(j, first, second), j, 3, partners[2])]
+
+    def along_first(j):
+        return [remote(line(j, first, b2), line(j, first, b2), j, 4 + b2, partners[1]) for b2 in range(2)]
+
+    def across(j):
+        return [
+            remote(line(j, b1, b2), line(j, b1, b2), j, 6 + b1 * 2 + b2, partners[0])
+            for b1 in range(2)
+            for b2 in range(2)
+        ]
+
+    greet(partners)
+    count = len(chunks)
+    stages = (along_z, along_second, along_first, across)
+    flights = [[None] * count for stage in stages]
+    for j in range(count):
+        source, target = mine(j)
+        pltpu.make_async_copy(source, target, own_sem.at[j]).start()
+    for t in range(count + len(stages) - 1):
+        for s, stage in enumerate(stages):
+            j = t - s
+            if 0 <= j < count:
+                if s == 1:
+                    source, target = mine(j)
+                    pltpu.make_async_copy(source, target, own_sem.at[j]).wait()
+                if s > 0:
+                    for copy in flights[s - 1][j]:
+                        copy.wait_recv()
+                flights[s][j] = stage(j)
+                for copy in flights[s][j]:
+                    copy.start()
+    for j in range(count):
+        for copy in flights[-1][j]:
+            copy.wait_recv()
+    for j in range(count):
+        for flight in flights:
+            for copy in flight[j]:
+                copy.wait_send()
+
+
+def gather_whole(shards, parts, collective_id):
+    chunks = []
+    for index, (shard, cuts) in enumerate(zip(shards, parts)):
+        chunks += [(index, low, width) for low, width in column_cuts(shard.shape[1], cuts)]
+    count = len(chunks)
+    wholes = pl.pallas_call(
+        functools.partial(gather_kernel, tuple(chunks), len(shards)),
+        in_specs=[pl.BlockSpec(memory_space=pltpu.VMEM)] * len(shards),
+        out_specs=[pl.BlockSpec(memory_space=pl.ANY)] * len(shards),
+        out_shape=[jax.ShapeDtypeStruct(GRID_DIMS + s.shape, s.dtype) for s in shards],
+        scratch_shapes=[
+            pltpu.SemaphoreType.DMA((count, 10)),
+            pltpu.SemaphoreType.DMA((count, 10)),
+            pltpu.SemaphoreType.DMA((count,)),
+        ],
+        compiler_params=pltpu.CompilerParams(
+            collective_id=collective_id, has_side_effects=True, vmem_limit_bytes=16 << 20
+        ),
+        name="gather_whole",
+    )(*shards)
+    return [w.reshape((math.prod(GRID_DIMS),) + s.shape) for w, s in zip(wholes, shards)]
+
+
 def widen(arrays):
     return tuple((array.astype(jnp.float32) for array in arrays))
+
+
+def vector_tile(vectors):
+    joined = jnp.concatenate(vectors, axis=-1)
+    lead, length = joined.shape[:-1], joined.shape[-1]
+    columns = LANES * (-(-length // (8 * LANES)))
+    joined = jnp.pad(joined, [(0, 0)] * len(lead) + [(0, 8 * columns - length)])
+    return joined.reshape(lead + (8, columns))
+
+
+def cut_tile(tile, lengths):
+    lead = tile.shape[:-2]
+    flat = tile.reshape(lead + (-1,))
+    return pieces(flat, lengths)
+
+
+def kernels_fit():
+    return (lax.axis_size("dp"), lax.axis_size("fsdp")) == (4, 8)
+
+
+def gather_weights(matrices, vectors):
+    matrices = [m.astype(jnp.bfloat16) for m in matrices]
+    vectors = [v.astype(jnp.bfloat16) for v in vectors]
+    if not kernels_fit():
+        whole = [lax.all_gather(a, AXES, axis=0, tiled=True) for a in matrices + vectors]
+        return whole[: len(matrices)], whole[len(matrices) :]
+    tile = vector_tile(vectors)
+    whole = gather_whole([tile] + matrices, (1,) + GATHER_CUTS, 1)
+    cut = cut_tile(whole[0], [v.shape[0] for v in vectors])
+    full = [w.reshape((-1, w.shape[-1])) for w in whole[1:]]
+    return full, [c.reshape(-1) for c in cut]
+
+
+def scatter_grads(matrices, vectors, loss):
+    if not kernels_fit():
+        sums = [lax.psum_scatter(g, AXES, scatter_dimension=0, tiled=True) for g in matrices + vectors]
+        squares = sum(jnp.sum(g * g) for g in sums)
+        return sums, lax.psum(squares, AXES), lax.psum(loss, AXES)
+    devices = math.prod(GRID_DIMS)
+    blocks = [m.reshape((devices, -1, m.shape[-1])) for m in matrices]
+    tile = vector_tile([v.reshape(devices, -1) for v in vectors])
+    corner = lax.broadcasted_iota(jnp.int32, (8, LANES), 0) + lax.broadcasted_iota(jnp.int32, (8, LANES), 1) == 0
+    outs = scatter_sums(blocks + [tile], SCATTER_CUTS + (1,), jnp.where(corner, loss, 0.0), 2)
+    cut = cut_tile(outs[len(matrices)], [v.shape[0] // devices for v in vectors])
+    totals = outs[-1]
+    return list(outs[: len(matrices)]) + list(cut), jnp.sum(totals[0]), jnp.sum(totals[1])
+
+
+GATHER_CUTS = (4, 2, 2, 1)
+SCATTER_CUTS = (8, 3, 4, 2)
 
 
 def per_device(
@@ -427,30 +777,13 @@
     resolution,
     kept,
     step_count,
-    encoder_in,
-    encoder_out,
-    decoder_in,
-    decoder_out,
-    norm_gains,
-    all_biases,
-    moment_encoder_in,
-    moment_encoder_out,
-    moment_decoder_in,
-    moment_decoder_out,
-    moment_gains,
-    moment_biases,
-    square_encoder_in,
-    square_encoder_out,
-    square_decoder_in,
-    square_decoder_out,
-    square_gains,
-    square_biases,
+    *state,
 ):
+    masters, firsts, seconds = state[:6], state[6:12], state[12:]
     devices = lax.axis_size("dp") * lax.axis_size("fsdp")
     patches_all = pixels.shape[0] * devices
     denom = (0.75 + 0.1 * 0.25) * patches_all
     order = layout(resolution, kept, pixels.shape[0])
-    cotangent = jnp.ones((), jnp.float32)
 
     def forward_a(mats, gain_vec, bias_vec):
         return section_a(mats, gain_vec, bias_vec, pixels, kept, order)
@@ -458,87 +791,18 @@
     def forward_b(mats, gain_vec, bias_vec, stream):
         return section_b(mats, gain_vec, bias_vec, stream, pixels, order, denom)
 
-    encoder_whole = widen(
-        (
-            lax.all_gather(encoder_in.astype(jnp.bfloat16), ("dp", "fsdp"), axis=0, tiled=True),
-            lax.all_gather(encoder_out.astype(jnp.bfloat16), ("dp", "fsdp"), axis=0, tiled=True),
-            lax.all_gather(norm_gains.astype(jnp.bfloat16), ("dp", "fsdp"), axis=0, tiled=True),
-            lax.all_gather(all_biases.astype(jnp.bfloat16), ("dp", "fsdp"), axis=0, tiled=True),
-        )
-    )
-    encoder_mats = encoder_whole[:2]
-    gains_full, biases_full = (encoder_whole[2], encoder_whole[3])
-    lifted = forward_a(encoder_mats, gains_full, biases_full)
-    loss_local = forward_b(
-        widen(
-            (
-                lax.all_gather(decoder_in.astype(jnp.bfloat16), ("dp", "fsdp"), axis=0, tiled=True),
-                lax.all_gather(
-                    decoder_out.astype(jnp.bfloat16), ("dp", "fsdp"), axis=0, tiled=True
-                ),
-            )
-        ),
-        gains_full,
-        biases_full,
-        lifted,
-    )
-    loss_total = lax.psum(loss_local, ("dp", "fsdp"))
-    decoder_again = widen(
-        (
-            lax.all_gather(decoder_in.astype(jnp.bfloat16), ("dp", "fsdp"), axis=0, tiled=True),
-            lax.all_gather(decoder_out.astype(jnp.bfloat16), ("dp", "fsdp"), axis=0, tiled=True),
-        )
-    )
-    unused, pull_decoder = jax.vjp(forward_b, decoder_again, gains_full, biases_full, lifted)
-    decoder_terms, gain_back, bias_back, stream_back = pull_decoder(cotangent)
-    decoder_grads = (
-        lax.psum_scatter(decoder_terms[0], ("dp", "fsdp"), scatter_dimension=0, tiled=True),
-        lax.psum_scatter(decoder_terms[1], ("dp", "fsdp"), scatter_dimension=0, tiled=True),
-    )
-    encoder_again = widen(
-        (
-            lax.all_gather(encoder_in.astype(jnp.bfloat16), ("dp", "fsdp"), axis=0, tiled=True),
-            lax.all_gather(encoder_out.astype(jnp.bfloat16), ("dp", "fsdp"), axis=0, tiled=True),
-        )
-    )
-    unused, pull_encoder = jax.vjp(forward_a, encoder_again, gains_full, biases_full)
+    matrices, vectors = gather_weights(masters[:4], masters[4:])
+    matrices, vectors = widen(matrices), widen(vectors)
+    lifted, pull_encoder = jax.vjp(forward_a, matrices[:2], *vectors)
+    loss_local, pull_decoder = jax.vjp(forward_b, matrices[2:], *vectors, lifted)
+    decoder_terms, gain_back, bias_back, stream_back = pull_decoder(jnp.ones((), jnp.float32))
     encoder_terms, gain_front, bias_front = pull_encoder(stream_back)
-    encoder_grads = (
-        lax.psum_scatter(encoder_terms[0], ("dp", "fsdp"), scatter_dimension=0, tiled=True),
-        lax.psum_scatter(encoder_terms[1], ("dp", "fsdp"), scatter_dimension=0, tiled=True),
-        lax.psum_scatter(gain_front + gain_back, ("dp", "fsdp"), scatter_dimension=0, tiled=True),
-        lax.psum_scatter(bias_front + bias_back, ("dp", "fsdp"), scatter_dimension=0, tiled=True),
-    )
-    grads = (
-        encoder_grads[0],
-        encoder_grads[1],
-        decoder_grads[0],
-        decoder_grads[1],
-        encoder_grads[2],
-        encoder_grads[3],
-    )
-    squares = sum((jnp.sum(grad * grad) for grad in grads))
-    total_squares = lax.psum(squares, ("dp", "fsdp"))
+    grads, total_squares, loss_total = scatter_grads(
+        list(encoder_terms) + list(decoder_terms), [gain_front + gain_back, bias_front + bias_back], loss_local
+    )
     grad_norm = jnp.sqrt(total_squares)
     factor = jnp.minimum(1.0, 0.5 / math.sqrt(patches_all) / (grad_norm + 1e-06))
     times = step_count[0].astype(jnp.float32)
-    masters = (encoder_in, encoder_out, decoder_in, decoder_out, norm_gains, all_biases)
-    firsts = (
-        moment_encoder_in,
-        moment_encoder_out,
-        moment_decoder_in,
-        moment_decoder_out,
-        moment_gains,
-        moment_biases,
-    )
-    seconds = (
-        square_encoder_in,
-        square_encoder_out,
-        square_decoder_in,
-        square_decoder_out,
-        square_gains,
-        square_biases,
-    )
     results = [
         adamw(
             masters[index],
@@ -550,28 +814,7 @@
         )
         for index in range(6)
     ]
-    return (
-        loss_total,
-        grad_norm,
-        results[0][0],
-        results[1][0],
-        results[2][0],
-        results[3][0],
-        results[4][0],
-        results[5][0],
-        results[0][1],
-        results[1][1],
-        results[2][1],
-        results[3][1],
-        results[4][1],
-        results[5][1],
-        results[0][2],
-        results[1][2],
-        results[2][2],
-        results[3][2],
-        results[4][2],
-        results[5][2],
-    )
+    return (loss_total, grad_norm) + tuple(result[part] for part in range(3) for result in results)
 
 
 def solution(mesh):

time: 1420 us -> 774 us (0.55)
  waiting for transfers between devices: 852 us -> 0 us
  Pallas kernels: 134 us -> 476 us
  blocking collectives: 123 us -> 0 us
  between operations: 24.7 us -> 7.95 us
    reduce_scatter x4 -> x0, waiting for transfers between devices: 737 us -> none  [the longest x1 234 us: per_device(): lax.psum_scatter(encoder_terms[0], ('dp', 'fsdp'), scatter_dimension=0, t...]
    pallas_call x0 -> x2, Pallas kernels: none -> 343 us  [the longest x1 225 us: scatter_sums(): pl.pallas_call(functools.partial(scatter_kernel, tuple(chunks), tuple(slo...]
    all_gather x4 -> x0, waiting for transfers between devices: 91.2 us -> none  [the longest x1 46.4 us: per_device(): lax.all_gather(decoder_in.astype(jnp.bfloat16), ('dp', 'fsdp'), axis=0, t...]
    unnamed x2 -> x0, blocking collectives: 82.9 us -> none
    psum x1 -> x0, blocking collectives: 40.1 us -> none  [per_device(): loss_total = lax.psum(loss_local, ('dp', 'fsdp'))]
    unnamed x10 -> x0, waiting for transfers between devices: 23.5 us -> none
  transfers between devices with their start and end apart: 9 -> 0, of which waited for: 8 -> 0; matrix products, arithmetic and copies ran while one was open for 11% -> 0% of each run, Pallas kernels for 4% -> 0%
where the time goes in v2:
time: 774 us; the launch traced here: 767 us
  Pallas kernels  476 us (61%)
  matrix products  127 us (16%)
  other arithmetic  105 us (14%)
  local copies, waits for them, and re-layouts  52.2 us (7%)
  between operations  7.95 us (1%)
    pallas_call x1, Pallas kernels, scatter_sums(): pl.pallas_call(functools.partial(scatter_kernel, tuple(chunks), tuple(slo...  225 us
    pallas_call x1, Pallas kernels, gather_whole(): pl.pallas_call(functools.partial(gather_kernel, tuple(chunks), len(shards...  117 us
    dot_general x20, matrix products, matmul(): return jnp.dot(left, right, preferred_element_type=jnp.float32)  86.7 us
    pallas_call x2, Pallas kernels, attend(): return rule(heads, queries, keys, values, marks[0], marks[1])  80.3 us
    pallas_call x2, Pallas kernels, attend_forward(): pl.pallas_call(functools.partial(attend_fwd_kernel, step, size), grid=gri...  53.1 us
    dot_general x6, matrix products, block(): jnp.einsum('gtd,df->gft', normed, w_qkv, preferred_element_type=jnp.float32)  26.7 us
    unnamed x278, local copies, waits for them, and re-layouts  21.5 us

profile of v2, /device:TPU:0, one launch (start us, length us, event | category | flops | bytes accessed | tf_op | source)
XLA Modules:
  0.0 767.4 jit_solution(1648869807173764341)
XLA Ops:
  18.7 4.1 multiply_sine_fusion.3
  32.1 7.2 multiply_sine_fusion.1
  39.3 4.1 scatter_custom_fusion
  43.4 4.6 gather_fusion.1
  48.0 117.5 %gather_whole.1 = (bf16[2,2,4,2,8,128]{5,4,3,2,1,0:T(8,128)(2,1)S(1)}, bf16[2,2,4,2,24,7424]{5,4,3,2,1,0:T(8,128)(2,1)S(1)}, bf16[2,2,4,2,96,768]{5,4,3,2,1,0:T(...) custom-call(bf16[8,128]{1,0:T(8,128)(2,1)S(1)} %fusion.88.refs_0_, ...), custom_call_target="tpu_custom_call" | custom-call | tf_op jit(solution)/shard_map/gather_whole/pallas_call | solution.py:703
  165.5 4.2 copy-done
  178.0 5.0 maximum_add_fusion
  183.5 4.3 convolution_bitcast_fusion.1
  190.3 10.2 %jvp_attend_forward_.2 = (bf16[1,768,392]{2,1,0:T(8,128)(2,1)}, f32[1,12,392]{2,1,0:T(8,128)}) custom-call(bf16[1,768,392]{2,1,0:T(8,128)(2,1)} %get-tuple-element.126.q_ref, bf16[1,768,392]{2,1,0:T(8,128)(2,1)} %slice.316.k_ref, bf16[1,768,392]{2,1,0:T(8,128)(2,1)} %get-tuple-element.125.v_ref, bf16[1,16,392]{2,1,0:T(8,128)(2,1)} %get-tuple-element.162.away_ref, ...), custom_call_target="tpu_custom_call" | custom-call | flops 472055808 | bytes 2408448 | tf_op jit(solution)/shard_map/jvp(attend_forward)/pallas_call | solution.py:208
  203.5 5.9 multiply_convert_fusion.2
  216.4 7.4 scatter_fusion
  237.1 42.9 %jvp_attend_forward_.3 = (bf16[2,512,784]{2,1,0:T(8,128)(2,1)}, f32[2,16,784]{2,1,0:T(8,128)}) custom-call(bf16[2,512,784]{2,1,0:T(8,128)(2,1)} %get-tuple-element.122.q_ref, bf16[2,512,784]{2,1,0:T(8,128)(2,1)} %slice.315.k_ref, bf16[2,512,784]{2,1,0:T(8,128)(2,1)} %get-tuple-element.121.v_ref, bf16[2,16,784]{2,1,0:T(8,128)(2,1)} %get-tuple-element.156.away_ref, ...), custom_call_target="tpu_custom_call" | custom-call | flops 2517630976 | bytes 6422528 | tf_op jit(solution)/shard_map/jvp(attend_forward)/pallas_call | solution.py:208
  286.4 7.9 %multiply_convert_fusion = (bf16[1568,2048]{1,0:T(8,128)(2,1)S(1)}, f32[1568,2048]{1,0:T(8,128)}) fusion(f32[2048]{0:T(1024)S(1)} %slice.249, bf16[1568,512]{1,0:T(8,128)(2,1)S(1)} %add_convert_fusion.3, bf16[512,4864]{1,0:T(8,128)(2,1)S(1)} %bitcast.143), kind=kOutput, calls=%fused_computation.9 | convolution fusion | flops 3307601920 | bytes 22978560 | tf_op jit(solution)/shard_map/jvp()/dot_general | solution.py:70
  294.3 3.8 fusion.133
  299.8 4.2 multiply_reduce_fusion.1
  305.3 5.1 fusion.139
  313.1 3.7 multiply_reduce_fusion.3
  318.6 8.3 %add_convert_fusion = bf16[1568,2048]{1,0:T(8,128)(2,1)S(1)} fusion(f32[1568,2048]{1,0:T(8,128)S(1)} %bitcast.174, bf16[1568,512]{1,0:T(8,128)(2,1)S(1)} %add_convert_fusion.5, bf16[2048,512]{1,0:T(8,128)(2,1)S(1)} %bitcast.156, f32[2048]{0:T(1024)S(1)} %slice.249), kind=kOutput, calls=%fused_computation.8 | convolution fusion | flops 3333292032 | bytes 22978560 | tf_op jit(solution)/shard_map/transpose(jvp())/dot_general | solution.py:70
  326.9 8.5 %fusion.141 = f32[2048,512]{1,0:T(8,128)} fusion(bf16[1568,2048]{1,0:T(8,128)(2,1)} %copy-done.117, bf16[1568,512]{1,0:T(8,128)(2,1)S(1)} %add_convert_fusion.5), kind=kOutput, calls=%fused_computation.359 | convolution fusion | flops 3288334336 | bytes 12222464 | tf_op jit(solution)/shard_map/transpose(jvp())/dot_general | solution.py:70
  337.1 5.9 fusion.140
  343.1 4.6 multiply_reduce_fusion.2
  358.6 67.5 %transpose_jvp_attend_backward__.2 = (bf16[2,512,784]{2,1,0:T(8,128)(2,1)}, bf16[2,512,784]{2,1,0:T(8,128)(2,1)}, bf16[2,512,784]{2,1,0:T(8,128)(2,1)}) custom-call(bf16[2,512,784]{2,1,0:T(8,128)(2,1)} %get-tuple-element.122.q_ref, bf16[2,512,784]{2,1,0:T(8,128)(2,1)} %slice.315.k_ref, bf16[2,512,784]{2,1,0:T(8,128)(2,1)} %get-tuple-element.121.v_ref, ...), custom_call_target="tpu_custom_call" | custom-call | flops 6294077440 | bytes 11239424 | tf_op jit(solution)/shard_map/transpose(jvp(attend_backward))/pallas_call | solution.py:267
  432.9 4.7 fusion.134
  437.6 6.4 fusion.16
  444.0 5.8 pad_add_fusion.2
  457.3 4.1 gather_fusion.3
  466.3 6.8 add_convert_fusion.1
  479.9 12.8 %transpose_jvp_attend_backward__.3 = (bf16[1,768,392]{2,1,0:T(8,128)(2,1)}, bf16[1,768,392]{2,1,0:T(8,128)(2,1)}, bf16[1,768,392]{2,1,0:T(8,128)(2,1)}) custom-call(bf16[1,768,392]{2,1,0:T(8,128)(2,1)} %get-tuple-element.126.q_ref, bf16[1,768,392]{2,1,0:T(8,128)(2,1)} %slice.316.k_ref, bf16[1,768,392]{2,1,0:T(8,128)(2,1)} %get-tuple-element.125.v_ref, ...), custom_call_target="tpu_custom_call" | custom-call | flops 1180139520 | bytes 4214784 | tf_op jit(solution)/shard_map/transpose(jvp(attend_backward))/pallas_call | solution.py:267
  497.2 6.1 multiply_reduce_fusion.10
  514.5 8.1 %pad_add_fusion = f32[768,7424]{1,0:T(8,128)} fusion(f32[768,768]{1,0:T(8,128)S(1)} %fusion.137, f32[768,2304]{1,0:T(8,128)S(1)} %fusion.8, f32[768,768]{1,0:T(8,128)S(1)} %fusion.41, f32[768,3072]{1,0:T(8,128)S(1)} %fusion.136, f32[768,512]{1,0:T(8,128)S(1)} %copy-done.28), kind=kLoop, calls=%fused_computation.6 | loop fusion | flops 22806528 | bytes 45613056 | tf_op jit(solution)/shard_map/transpose(jvp())/add_any | solution.py:81
  522.6 5.1 fusion.138
  527.8 225.2 %scatter_sums.1 = (f32[24,7424]{1,0:T(8,128)}, f32[96,768]{1,0:T(8,128)}, f32[16,4864]{1,0:T(8,128)}, f32[64,512]{1,0:T(8,128)}, f32[8,128]{1,0:T(8,128)}, /*index=5*/f32[2,8,128]{2,1,0:T(8,128)}) custom-call(f32[2,2,4,2,24,7424]{5,4,3,2,1,0:T(8,128)} %bitcast.157, f32[2,2,4,2,96,768]{5,4,3,2,1,0:T(8,128)} %bitcast.159, ...), custom_call_target="tpu_custom_call" | custom-call | flops 23265280 | bytes 139591680 | tf_op jit(solution)/shard_map/scatter_sums/pallas_call | solution.py:607
  (443 shorter events, 137.7 us)
Async XLA Ops:
  0.7 15.4 %copy-start.13 = (bf16[1568,768]{1,0:T(8,128)(2,1)S(1)}, bf16[1568,768]{1,0:T(8,128)(2,1)}, u32[]{:S(2)}) copy-start(bf16[1568,768]{1,0:T(8,128)(2,1)} %param.22) | copy-start | bytes 7225348
  6.7 206.4 %copy-start.81 = (u32[392]{0:T(512)}, u32[392]{0:T(512)S(1)}, u32[]{:S(2)}) copy-start(u32[392]{0:T(512)S(1)} %iota_add_fusion) | copy-start | bytes 4708
  10.6 32.8 %copy-start.98 = (s32[1024]{0:T(1024)}, s32[1024]{0:T(1024)S(1)}, u32[]{:S(2)}) copy-start(s32[1024]{0:T(1024)S(1)} %pad_clamp_fusion.1) | copy-start | bytes 12292
  43.4 132.1 %copy-start.36 = (bf16[392,768]{1,0:T(8,128)(2,1)S(1)}, bf16[392,768]{1,0:T(8,128)(2,1)}, u32[]{:S(2)}) copy-start(bf16[392,768]{1,0:T(8,128)(2,1)} %gather_fusion) | copy-start | bytes 1806340
  174.3 29.2 %copy-start.100 = (f32[3072]{0:T(1024)}, f32[3072]{0:T(1024)S(1)}, u32[]{:S(2)}) copy-start(f32[3072]{0:T(1024)S(1)} %slice.229) | copy-start | bytes 36868
  174.8 54.6 %copy-start.83 = (f32[512]{0:T(512)}, f32[512]{0:T(512)S(1)}, u32[]{:S(2)}) copy-start(f32[512]{0:T(512)S(1)} %get-tuple-element.205) | copy-start | bytes 6148
  175.4 27.7 %copy-start.71 = (f32[768]{0:T(1024)}, f32[768]{0:T(1024)S(1)}, u32[]{:S(2)}) copy-start(f32[768]{0:T(1024)S(1)} %get-tuple-element.203) | copy-start | bytes 9220
  175.4 36.6 %copy-start.73 = (f32[768]{0:T(1024)}, f32[768]{0:T(1024)S(1)}, u32[]{:S(2)}) copy-start(f32[768]{0:T(1024)S(1)} %get-tuple-element.204) | copy-start | bytes 9220
  177.9 22.6 %copy-start.14 = (f32[392,768]{1,0:T(8,128)}, f32[392,768]{1,0:T(8,128)S(1)}, u32[]{:S(2)}) copy-start(f32[392,768]{1,0:T(8,128)S(1)} %get-tuple-element.180) | copy-start | bytes 3612676
  283.6 10.7 %copy-start.8 = (f32[1568,512]{1,0:T(8,128)}, f32[1568,512]{1,0:T(8,128)S(1)}, u32[]{:S(2)}) copy-start(f32[1568,512]{1,0:T(8,128)S(1)} %get-tuple-element.116) | copy-start | bytes 9633796
  286.4 7.9 %copy-start.45 = (bf16[1568,512]{1,0:T(8,128)(2,1)}, bf16[1568,512]{1,0:T(8,128)(2,1)S(1)}, u32[]{:S(2)}) copy-start(bf16[1568,512]{1,0:T(8,128)(2,1)S(1)} %add_convert_fusion.3) | copy-start | bytes 4816900
  286.4 7.9 %copy-start.109 = (f32[512]{0:T(512)S(1)}, f32[512]{0:T(512)}, u32[]{:S(2)}) copy-start(f32[512]{0:T(512)} %get-tuple-element.137) | copy-start | bytes 6148
  286.4 13.4 %slice-start.13 = ((s8[4816896]{0:T(1024)(128)(4,1)}), s8[4194304]{0:T(1024)(128)(4,1)S(1)}, s32[]{:S(2)}) async-start(s8[4816896]{0:T(1024)(128)(4,1)} %bitcast.162), calls=%async_computation.13 | async-start | bytes 8388608
  318.3 30.9 %copy-start.6 = (f32[1568,512]{1,0:T(8,128)}, f32[1568,512]{1,0:T(8,128)S(1)}, u32[]{:S(2)}) copy-start(f32[1568,512]{1,0:T(8,128)S(1)} %get-tuple-element.114) | copy-start | bytes 9633796
  465.5 8.2 %slice-start = ((s8[11403264]{0:T(1024)(128)(4,1)}), s8[4194304]{0:T(1024)(128)(4,1)S(1)}, s32[]{:S(2)}) async-start(s8[11403264]{0:T(1024)(128)(4,1)} %bitcast.130), calls=%async_computation | async-start | bytes 8388608
  514.5 8.1 %copy-start.41 = (bf16[392,768]{1,0:T(8,128)(2,1)S(1)}, bf16[392,768]{1,0:T(8,128)(2,1)}, u32[]{:S(2)}) copy-start(bf16[392,768]{1,0:T(8,128)(2,1)} %copy-done.40) | copy-start | bytes 1806340
  514.5 8.1 %copy-start.114 = (bf16[392,3072]{1,0:T(8,128)(2,1)S(1)}, bf16[392,3072]{1,0:T(8,128)(2,1)}, u32[]{:S(2)}) copy-start(bf16[392,3072]{1,0:T(8,128)(2,1)} %copy-done.113) | copy-start | bytes 7225348
  527.7 227.5 %copy-start.110 = (f32[120]{0:T(128)S(1)}, f32[120]{0:T(128)}, u32[]{:S(2)}) copy-start(f32[120]{0:T(128)} %param.30) | copy-start | bytes 1444
  527.7 227.5 %copy-start.111 = (f32[120]{0:T(128)S(1)}, f32[120]{0:T(128)}, u32[]{:S(2)}) copy-start(f32[120]{0:T(128)} %param.42) | copy-start | bytes 1444
  527.7 227.5 %copy-start.112 = (f32[120]{0:T(128)S(1)}, f32[120]{0:T(128)}, u32[]{:S(2)}) copy-start(f32[120]{0:T(128)} %param.36) | copy-start | bytes 1444
  527.8 228.8 %copy-start.97 = (f32[520]{0:T(1024)S(1)}, f32[520]{0:T(1024)}, u32[]{:S(2)}) copy-start(f32[520]{0:T(1024)} %param.31) | copy-start | bytes 6244
  527.8 228.8 %copy-start.106 = (f32[520]{0:T(1024)S(1)}, f32[520]{0:T(1024)}, u32[]{:S(2)}) copy-start(f32[520]{0:T(1024)} %param.43) | copy-start | bytes 6244
  527.8 228.8 %copy-start.107 = (f32[520]{0:T(1024)S(1)}, f32[520]{0:T(1024)}, u32[]{:S(2)}) copy-start(f32[520]{0:T(1024)} %param.37) | copy-start | bytes 6244
  527.8 230.2 %copy-start.60 = (f32[64,512]{1,0:T(8,128)S(1)}, f32[64,512]{1,0:T(8,128)}, u32[]{:S(2)}) copy-start(f32[64,512]{1,0:T(8,128)} %param.29) | copy-start | bytes 393220
  527.8 230.2 %copy-start.66 = (f32[64,512]{1,0:T(8,128)S(1)}, f32[64,512]{1,0:T(8,128)}, u32[]{:S(2)}) copy-start(f32[64,512]{1,0:T(8,128)} %param.41) | copy-start | bytes 393220
  527.8 231.9 %copy-start.52 = (f32[96,768]{1,0:T(8,128)S(1)}, f32[96,768]{1,0:T(8,128)}, u32[]{:S(2)}) copy-start(f32[96,768]{1,0:T(8,128)} %param.27) | copy-start | bytes 884740
  753.0 8.9 %copy-start.51 = (f32[16,4864]{1,0:T(8,128)S(1)}, f32[16,4864]{1,0:T(8,128)}, u32[]{:S(2)}) copy-start(f32[16,4864]{1,0:T(8,128)} %param.28) | copy-start | bytes 933892
  753.0 8.9 %copy-start.61 = (f32[16,4864]{1,0:T(8,128)S(1)}, f32[16,4864]{1,0:T(8,128)}, u32[]{:S(2)}) copy-start(f32[16,4864]{1,0:T(8,128)} %param.40) | copy-start | bytes 933892
  753.0 11.0 %copy-start.35 = (f32[24,7424]{1,0:T(8,128)S(1)}, f32[24,7424]{1,0:T(8,128)}, u32[]{:S(2)}) copy-start(f32[24,7424]{1,0:T(8,128)} %param.26) | copy-start | bytes 2138116
  753.1 11.0 %copy-start.53 = (f32[24,7424]{1,0:T(8,128)S(1)}, f32[24,7424]{1,0:T(8,128)}, u32[]{:S(2)}) copy-start(f32[24,7424]{1,0:T(8,128)} %param.38) | copy-start | bytes 2138116
  753.1 11.0 %copy-start.54 = (f32[24,7424]{1,0:T(8,128)S(1)}, f32[24,7424]{1,0:T(8,128)}, u32[]{:S(2)}) copy-start(f32[24,7424]{1,0:T(8,128)} %param.32) | copy-start | bytes 2138116
  755.3 8.8 %copy-start.55 = (f32[24,7424]{1,0:T(8,128)S(1)}, f32[24,7424]{1,0:T(8,128)}, u32[]{:S(2)}) copy-start(f32[24,7424]{1,0:T(8,128)} %get-tuple-element.57) | copy-start | bytes 2138116
  (106 other events, 440.2 us)

commit v3 on v2

--- a/solution.py
+++ b/solution.py
@@ -120,12 +120,17 @@
 
 def sine_table(row_pos, col_pos, width):
     quarter = width // 4
+    reach = 8 * (-(-SIDE_BIG // 8))
     omega = 1.0 / 10000.0 ** (jnp.arange(quarter, dtype=jnp.float32) / quarter)
-    across = row_pos.astype(jnp.float32)[:, None] * omega[None, :]
-    downward = col_pos.astype(jnp.float32)[:, None] * omega[None, :]
-    return jnp.concatenate(
-        [jnp.sin(across), jnp.cos(across), jnp.sin(downward), jnp.cos(downward)], axis=1
+    angles = jnp.arange(reach, dtype=jnp.float32)[:, None] * omega[None, :]
+    half = jnp.concatenate([jnp.sin(angles), jnp.cos(angles)], axis=1)
+    none = jnp.zeros_like(half)
+    table = jnp.concatenate(
+        [jnp.concatenate([half, none], axis=1), jnp.concatenate([none, half], axis=1)], axis=0
     )
+    spot = jnp.arange(2 * reach, dtype=jnp.int32)[None, :]
+    hot = (spot == row_pos[:, None]) | (spot == col_pos[:, None] + reach)
+    return jnp.dot(hot.astype(jnp.float32), table, precision=lax.Precision.HIGHEST)
 
 
 def layer_norm(stream, gain, shift):
@@ -146,125 +151,512 @@
     return lax.dot_general(left, right, dims, preferred_element_type=jnp.float32)
 
 
-def attend_fwd_kernel(heads, size, q_ref, k_ref, v_ref, away_ref, own_ref, o_ref, lse_ref):
+LANES = 128
+AXES = ("dp", "fsdp")
+GRID_DIMS = (2, 2, 4, 2)
+DEVICE_BLOCKS = 32
+MESH_IDS = pl.DeviceIdType.MESH
+WHOLE_VMEM = pl.BlockSpec(memory_space=pltpu.VMEM)
+LEFT_ALONE = pl.BlockSpec(memory_space=pl.ANY)
+
+
+def place_of():
+    dp, fsdp = lax.axis_index("dp"), lax.axis_index("fsdp")
+    x, core = dp // 2, dp % 2
+    z, y = fsdp // 2, fsdp % 2
+    flip_x = ((1 - x) * 2 + core, fsdp)
+    flip_y = (dp, z * 2 + 1 - y)
+
+    def choose(zero, one):
+        return tuple(a * (1 - core) + b * core for a, b in zip(zero, one))
+
+    partners = [(x * 2 + 1 - core, fsdp), choose(flip_x, flip_y), choose(flip_y, flip_x)]
+    partners += [(dp, lax.rem(z + step, 4) * 2 + y) for step in (1, 2, 3)]
+    return x, core, z, y, partners
+
+
+def greet(partners):
+    barrier = pltpu.get_barrier_semaphore()
+    for partner in partners:
+        pl.semaphore_signal(barrier, inc=1, device_id=partner, device_id_type=MESH_IDS)
+    pl.semaphore_wait(barrier, len(partners))
+
+
+def column_cuts(columns, parts):
+    tiles = columns // LANES
+    cuts = [LANES * (tiles * part // parts) for part in range(parts + 1)]
+    return [(low, high - low) for low, high in zip(cuts[:-1], cuts[1:])]
+
+
+def xy_of(core, first, second):
+    return first * (1 - core) + second * core, second * (1 - core) + first * core
+
+
+class Terms:
+    def __init__(self, rows, columns, cuts, array=None, left=None, right=None, dims=None):
+        self.rows, self.columns, self.cuts = rows, columns, cuts
+        self.array, self.left, self.right, self.dims = array, left, right, dims
+
+    def inputs(self):
+        if self.array is None:
+            return [(self.left, WHOLE_VMEM), (self.right, WHOLE_VMEM)]
+        return [(self.array.reshape(GRID_DIMS + (self.rows, self.columns)), LEFT_ALONE)]
+
+
+class Scatter:
+    def __init__(self, terms, loss=None):
+        self.terms, self.loss = terms, loss
+        pairs = [pair for term in terms for pair in term.inputs()]
+        if loss is not None:
+            pairs.append((loss, WHOLE_VMEM))
+        self.arrays = [array for array, spec in pairs]
+        self.in_specs = [spec for array, spec in pairs]
+        self.out_shape = [jax.ShapeDtypeStruct((t.rows, t.columns), jnp.float32) for t in terms]
+        if loss is not None:
+            self.out_shape.append(jax.ShapeDtypeStruct((2, 8, LANES), jnp.float32))
+        self.out_specs = [WHOLE_VMEM] * len(self.out_shape)
+        self.chunks, self.slots, landing, kept = [], [], [], []
+        kinds, last = {}, {}
+        for term in terms:
+            kind = (term.rows, term.array is None)
+            widest = max(width for low, width in column_cuts(term.columns, term.cuts))
+            kinds[kind] = (max(widest, kinds.get(kind, (0, 0))[0]), term.cuts + kinds.get(kind, (0, 0))[1])
+        bases = {}
+        for kind, (widest, number) in kinds.items():
+            bases[kind] = (len(kept), min(2, number))
+            dims = GRID_DIMS if kind[1] else (16,)
+            kept += [pltpu.VMEM(dims + (kind[0], widest), jnp.float32)] * min(2, number)
+        seen = {}
+        for index, term in enumerate(terms):
+            kind = (term.rows, term.array is None)
+            for low, width in column_cuts(term.columns, term.cuts):
+                base, number = bases[kind]
+                slot = base + seen.get(kind, 0) % number
+                seen[kind] = seen.get(kind, 0) + 1
+                self.chunks.append((index, low, width, last.get(slot)))
+                last[slot] = len(self.chunks) - 1
+                self.slots.append((slot, width))
+                landing += [pltpu.VMEM((n, term.rows, width), jnp.float32) for n in (16, 8, 4, 3)]
+        count = len(self.chunks)
+        self.kept = len(kept)
+        self.scratch = landing + kept
+        if loss is not None:
+            self.scratch += [pltpu.VMEM((7, 2, 8, LANES), jnp.float32), pltpu.VMEM((4, 2, 8, LANES), jnp.float32)]
+            self.scratch += [pltpu.SemaphoreType.DMA((6,)), pltpu.SemaphoreType.DMA((6,))]
+        self.scratch += [
+            pltpu.SemaphoreType.DMA((count, 6)),
+            pltpu.SemaphoreType.DMA((count, 6)),
+            pltpu.SemaphoreType.DMA((count,)),
+        ]
+
+    def steps(self, ins, outs, scratch):
+        chunks, terms, count = self.chunks, self.terms, len(self.chunks)
+        sources, at = [], 0
+        for term in terms:
+            number = 2 if term.array is None else 1
+            sources.append(ins[at : at + number])
+            at += number
+        arrive = [scratch[4 * j : 4 * j + 4] for j in range(count)]
+        kept = scratch[4 * count : 4 * count + self.kept]
+        send_sem, recv_sem, own_sem = scratch[-3:]
+        x, core, z, y, partners = place_of()
+        first, second = xy_of(core, x, y)
+
+        def remote(source, target, j, phase, partner):
+            return pltpu.make_async_remote_copy(
+                source, target, send_sem.at[j, phase], recv_sem.at[j, phase], device_id=partner, device_id_type=MESH_IDS
+            )
+
+        def slot_of(j):
+            slot, width = self.slots[j]
+            lead = 1 if terms[chunks[j][0]].array is not None else 4
+            return kept[slot].at[(slice(None),) * lead + (slice(None), pl.ds(0, width))]
+
+        def view(j, side, b1, b2):
+            index, low, width, before = chunks[j]
+            at_x, at_y = xy_of(side, b1, b2)
+            if terms[index].array is None:
+                return slot_of(j).at[at_x, side, :, at_y]
+            return sources[index][0].at[at_x, side, :, at_y, :, pl.ds(low, width)]
+
+        def sent(j, phase):
+            buffer = arrive[j][min(phase, 3)]
+            buffer = buffer.at[phase - 3] if phase >= 3 else buffer
+            pltpu.make_async_copy(buffer, buffer, send_sem.at[j, phase]).wait()
+
+        def came(j, phase):
+            buffer = arrive[j][min(phase, 3)]
+            buffer = buffer.at[phase - 3] if phase >= 3 else buffer
+            pltpu.make_async_copy(buffer, buffer, recv_sem.at[j, phase]).wait()
+
+        quarters = [(b1, b2, pl.ds((b1 * 2 + b2) * 4, 4)) for b1 in range(2) for b2 in range(2)]
+
+        def begin(j):
+            index, low, width, before = chunks[j]
+            term = terms[index]
+            if term.array is None:
+                if before is not None:
+                    sent(before, 0)
+                left, right = sources[index]
+                piece = right[pl.ds(low, width), :] if term.dims == CONTRACT_LANES else right[:, pl.ds(low, width)]
+                product = tile_dot(left[...], piece, term.dims)
+                slot_of(j)[...] = product.reshape(GRID_DIMS + (term.rows, width))
+            for b1, b2, place in quarters:
+                remote(view(j, 1 - core, b1, b2), arrive[j][0].at[place], j, 0, partners[0]).start()
+                if term.array is not None:
+                    pltpu.make_async_copy(view(j, core, b1, b2), slot_of(j).at[place], own_sem.at[j]).start()
+
+        def add_into(target, other, offset, blocks):
+            def step(n, carry):
+                target[n] = target[n] + other[offset + n]
+                return carry
+
+            lax.fori_loop(0, blocks, step, 0)
+
+        def stage_one(j):
+            slot = slot_of(j)
+            product = terms[chunks[j][0]].array is None
+            if not product:
+                pltpu.make_async_copy(slot, slot, own_sem.at[j]).wait()
+            came(j, 0)
+            if product:
+                for b1, b2, place in quarters:
+                    at_x, at_y = xy_of(core, b1, b2)
+                    for at_z in range(4):
+                        n = (b1 * 2 + b2) * 4 + at_z
+                        arrive[j][0][n] = arrive[j][0][n] + slot[at_x, core, at_z, at_y]
+            else:
+                add_into(arrive[j][0], slot, 0, 16)
+            remote(arrive[j][0].at[pl.ds((1 - first) * 8, 8)], arrive[j][1], j, 1, partners[1]).start()
+
+        def stage_two(j):
+            came(j, 1)
+            add_into(arrive[j][1], arrive[j][0], first * 8, 8)
+            remote(arrive[j][1].at[pl.ds((1 - second) * 4, 4)], arrive[j][2], j, 2, partners[2]).start()
+
+        def stage_three(j):
+            came(j, 2)
+            add_into(arrive[j][2], arrive[j][1], second * 4, 4)
+            for step in range(3):
+                there = lax.rem(z + step + 1, 4)
+                remote(arrive[j][2].at[there], arrive[j][3].at[step], j, 3 + step, partners[3 + step]).start()
+
+        def stage_four(j):
+            index, low, width, before = chunks[j]
+            for step in range(3):
+                came(j, 3 + step)
+            far = arrive[j][3]
+            outs[index][:, low : low + width] = (arrive[j][2][z] + far[0]) + (far[1] + far[2])
+
+        def run(t):
+            if t == 0:
+                greet(partners)
+                begin(0)
+            if t + 1 < count:
+                begin(t + 1)
+            for back, stage in enumerate((stage_one, stage_two, stage_three, stage_four)):
+                if 0 <= t - back < count:
+                    stage(t - back)
+
+        def finish():
+            again = {before for index, low, width, before in chunks if before is not None and terms[index].array is None}
+            for j in range(count):
+                for phase in range(6):
+                    if phase > 0 or j not in again:
+                        sent(j, phase)
+
+        def totals():
+            pair, quad, last_send, last_recv = scratch[-7:-3]
+            loss_ref, total_ref, square_ins = ins[at], outs[-1], ins[at + 1 :]
+
+            def share(source, target, n, partner):
+                return pltpu.make_async_remote_copy(
+                    source, target, last_send.at[n], last_recv.at[n], device_id=partner, device_id_type=MESH_IDS
+                )
+
+            tile = jnp.zeros((8, LANES), jnp.float32)
+            for ref in list(outs[: len(terms)]) + list(square_ins):
+                square = ref[...] * ref[...]
+                rows, columns = square.shape
+                tile = functools.reduce(
+                    jnp.add,
+                    [square[r : r + 8, c : c + LANES] for r in range(0, rows, 8) for c in range(0, columns, LANES)],
+                    tile,
+                )
+            pair[0, 0] = tile
+            pair[0, 1] = loss_ref[...]
+            tail = []
+            for n in range(3):
+                copy = share(pair.at[n], pair.at[4 + n], n, partners[n])
+                copy.start()
+                copy.wait_recv()
+                tail.append(copy)
+                target = pair.at[n + 1] if n < 2 else quad.at[z]
+                target[...] = pair[n] + pair[4 + n]
+            for step in range(3):
+                copy = share(quad.at[z], quad.at[z], 3 + step, partners[3 + step])
+                copy.start()
+                tail.append(copy)
+            for copy in tail[3:]:
+                copy.wait_recv()
+            total_ref[...] = (quad[0] + quad[1]) + (quad[2] + quad[3])
+            for copy in tail:
+                copy.wait_send()
+
+        parts = [functools.partial(run, t) for t in range(count + 3)]
+        return parts + ([totals] if self.loss is not None else []) + [finish]
+
+
+class Gather:
+    def __init__(self, shards, cut_pieces):
+        self.arrays, self.in_specs = list(shards), [WHOLE_VMEM] * len(shards)
+        self.chunks, self.out_shape = [], []
+        for shard, low, width, cuts in cut_pieces:
+            for start, wide in column_cuts(width, cuts):
+                self.chunks.append((shard, low + start, len(self.out_shape), start, wide))
+            self.out_shape.append(
+                jax.ShapeDtypeStruct(GRID_DIMS + (shards[shard].shape[0], width), shards[shard].dtype)
+            )
+        self.out_specs = [LEFT_ALONE] * len(self.out_shape)
+        count = len(self.chunks)
+        self.scratch = [
+            pltpu.SemaphoreType.DMA((count, 10)),
+            pltpu.SemaphoreType.DMA((count, 10)),
+            pltpu.SemaphoreType.DMA((count,)),
+        ]
+
+    def steps(self, ins, outs, scratch):
+        chunks, count = self.chunks, len(self.chunks)
+        send_sem, recv_sem, own_sem = scratch
+        x, core, z, y, partners = place_of()
+        first, second = xy_of(core, x, y)
+
+        def remote(source, target, j, phase, partner):
+            return pltpu.make_async_remote_copy(
+                source, target, send_sem.at[j, phase], recv_sem.at[j, phase], device_id=partner, device_id_type=MESH_IDS
+            )
+
+        def line(j, b1, b2):
+            shard, source, out, low, width = chunks[j]
+            at_x, at_y = xy_of(core, b1, b2)
+            return outs[out].at[at_x, core, :, at_y, :, pl.ds(low, width)]
+
+        def mine(j):
+            shard, source, out, low, width = chunks[j]
+            return ins[shard].at[:, pl.ds(source, width)], outs[out].at[x, core, z, y, :, pl.ds(low, width)]
+
+        def own(j):
+            source, target = mine(j)
+            return pltpu.make_async_copy(source, target, own_sem.at[j])
+
+        def along_z(j):
+            source, target = mine(j)
+            return [remote(source, target, j, step, partners[3 + step]) for step in range(3)]
+
+        def along_second(j):
+            return [remote(line(j, first, second), line(j, first, second), j, 3, partners[2])]
+
+        def along_first(j):
+            return [remote(line(j, first, b2), line(j, first, b2), j, 4 + b2, partners[1]) for b2 in range(2)]
+
+        def across(j):
+            return [
+                remote(line(j, b1, b2), line(j, b1, b2), j, 6 + b1 * 2 + b2, partners[0])
+                for b1 in range(2)
+                for b2 in range(2)
+            ]
+
+        stages = (along_z, along_second, along_first, across)
+
+        def run(t):
+            if t == 0:
+                greet(partners)
+                for j in range(count):
+                    own(j).start()
+            for s, stage in enumerate(stages):
+                j = t - s
+                if 0 <= j < count:
+                    if s == 1:
+                        own(j).wait()
+                    if s > 0:
+                        for copy in stages[s - 1](j):
+                            copy.wait_recv()
+                    for copy in stage(j):
+                        copy.start()
+
+        def finish():
+            for j in range(count):
+                for copy in across(j):
+                    copy.wait_recv()
+            for j in range(count):
+                for stage in stages:
+                    for copy in stage(j):
+                        copy.wait_send()
+
+        return [functools.partial(run, t) for t in range(count + len(stages) - 1)] + [finish]
+
+
+def run_alone(plan, collective_id, name, more=()):
+    def kernel(*refs):
+        inputs = len(plan.arrays) + len(more)
+        outputs = len(plan.out_shape)
+        for step in plan.steps(refs[:inputs], refs[inputs : inputs + outputs], refs[inputs + outputs :]):
+            step()
+
+    sent = sum(array.size * array.dtype.itemsize for array in plan.arrays)
+    return pl.pallas_call(
+        kernel,
+        in_specs=plan.in_specs + [WHOLE_VMEM] * len(more),
+        out_specs=plan.out_specs,
+        out_shape=plan.out_shape,
+        scratch_shapes=plan.scratch,
+        compiler_params=pltpu.CompilerParams(
+            collective_id=collective_id, has_side_effects=True, vmem_limit_bytes=63 << 20
+        ),
+        cost_estimate=pl.CostEstimate(flops=sent, bytes_accessed=2 * sent, transcendentals=0),
+        name=name,
+    )(*plan.arrays, *more)
+
+
+def hosted_refs(refs, inputs, outputs, plan):
+    extra_in = len(plan.arrays) if plan else 0
+    extra_out = len(plan.out_shape) if plan else 0
+    cuts = [inputs, extra_in, outputs, extra_out]
+    result, at = [], 0
+    for cut in cuts:
+        result.append(refs[at : at + cut])
+        at += cut
+    own_in, plan_in, own_out, plan_out = result
+    steps = plan.steps(plan_in, plan_out, refs[at:]) if plan else []
+    return own_in, own_out, steps
+
+
+def host_steps(steps, heads, head, work):
+    blocks = pl.num_programs(1)
+    now = (pl.program_id(0) * blocks + pl.program_id(1)) * heads + head
+    places = {}
+    total = 2 * 16
+    for number, step in enumerate(steps[:-1]):
+        places.setdefault(number * total // (len(steps) - 1), []).append(step)
+    for place, group in places.items():
+
+        @pl.when(now == place)
+        def start(group=group):
+            for step in group:
+                step()
+
+    work()
+    if steps:
+        pl.when(now == total - 1)(steps[-1])
+
+
+def attend_fwd_kernel(heads, size, plan, *refs):
+    (q_ref, k_ref, v_ref, away_ref, own_ref), (o_ref, lse_ref), steps = hosted_refs(refs, 5, 2, plan)
     factor = LOG2E / math.sqrt(size)
-    away, own = away_ref[0], own_ref[0]
 
     def one_head(head, carry):
-        rows = pl.ds(pl.multiple_of(head * size, size), size)
-        queries = jnp.concatenate([q_ref[0, rows, :], away], axis=0)
-        keys = jnp.concatenate([k_ref[0, rows, :], own], axis=0)
-        scores = tile_dot(keys, queries, CONTRACT_ROWS)
-        top = jnp.max(scores, axis=0, keepdims=True)
-        shifted = jnp.exp2((scores - top) * factor)
-        total = jnp.sum(shifted, axis=0, keepdims=True)
-        weights = (shifted * (1.0 / total)).astype(jnp.bfloat16)
-        o_ref[0, rows, :] = tile_dot(v_ref[0, rows, :], weights, CONTRACT_PLAIN).astype(o_ref.dtype)
-        lse_ref[0, pl.ds(head, 1), :] = top * factor + jnp.log2(total)
+        def work():
+            rows = pl.ds(pl.multiple_of(head * size, size), size)
+            queries = jnp.concatenate([q_ref[0, rows, :], away_ref[0]], axis=0)
+            keys = jnp.concatenate([k_ref[0, rows, :], own_ref[0]], axis=0)
+            scores = tile_dot(keys, queries, CONTRACT_ROWS)
+            top = jnp.max(scores, axis=0, keepdims=True)
+            shifted = jnp.exp2((scores - top) * factor)
+            total = jnp.sum(shifted, axis=0, keepdims=True)
+            weights = (shifted * (1.0 / total)).astype(jnp.bfloat16)
+            o_ref[0, rows, :] = tile_dot(v_ref[0, rows, :], weights, CONTRACT_PLAIN).astype(o_ref.dtype)
+            lse_ref[0, pl.ds(head, 1), :] = top * factor + jnp.log2(total)
+
+        host_steps(steps, heads, head, work)
         return carry
 
     lax.fori_loop(0, heads, one_head, 0)
 
 
-def attend_bwd_kernel(
-    heads, size, q_ref, k_ref, v_ref, do_ref, lse_ref, away_ref, own_ref, dq_ref, dk_ref, dv_ref
-):
+def attend_bwd_kernel(heads, size, plan, *refs):
+    ins, (dq_ref, dk_ref, dv_ref), steps = hosted_refs(refs, 7, 3, plan)
+    q_ref, k_ref, v_ref, do_ref, lse_ref, away_ref, own_ref = ins
     scale = 1.0 / math.sqrt(size)
     factor = LOG2E * scale
-    away, own = away_ref[0], own_ref[0]
 
     def one_head(head, carry):
-        rows = pl.ds(pl.multiple_of(head * size, size), size)
-        q_rows, k_rows, do_rows = q_ref[0, rows, :], k_ref[0, rows, :], do_ref[0, rows, :]
-        queries = jnp.concatenate([q_rows, away], axis=0)
-        keys = jnp.concatenate([k_rows, own], axis=0)
-        scores = tile_dot(keys, queries, CONTRACT_ROWS)
-        weights = jnp.exp2(scores * factor - lse_ref[0, pl.ds(head, 1), :])
-        spread = tile_dot(v_ref[0, rows, :], do_rows, CONTRACT_ROWS)
-        product = weights * spread
-        inner = jnp.sum(product, axis=0, keepdims=True)
-        dscores = (product - weights * inner).astype(jnp.bfloat16)
-        rounded = weights.astype(jnp.bfloat16)
-        dv_ref[0, rows, :] = tile_dot(do_rows, rounded, CONTRACT_LANES).astype(dv_ref.dtype)
-        dk_ref[0, rows, :] = (tile_dot(q_rows, dscores, CONTRACT_LANES) * scale).astype(dk_ref.dtype)
-        dq_ref[0, rows, :] = (tile_dot(k_rows, dscores, CONTRACT_PLAIN) * scale).astype(dq_ref.dtype)
+        def work():
+            rows = pl.ds(pl.multiple_of(head * size, size), size)
+            q_rows, k_rows, do_rows = q_ref[0, rows, :], k_ref[0, rows, :], do_ref[0, rows, :]
+            queries = jnp.concatenate([q_rows, away_ref[0]], axis=0)
+            keys = jnp.concatenate([k_rows, own_ref[0]], axis=0)
+            scores = tile_dot(keys, queries, CONTRACT_ROWS)
+            weights = jnp.exp2(scores * factor - lse_ref[0, pl.ds(head, 1), :])
+            spread = tile_dot(v_ref[0, rows, :], do_rows, CONTRACT_ROWS)
+            product = weights * spread
+            inner = jnp.sum(product, axis=0, keepdims=True)
+            dscores = (product - weights * inner).astype(jnp.bfloat16)
+            rounded = weights.astype(jnp.bfloat16)
+            dv_ref[0, rows, :] = tile_dot(do_rows, rounded, CONTRACT_LANES).astype(dv_ref.dtype)
+            dk_ref[0, rows, :] = (tile_dot(q_rows, dscores, CONTRACT_LANES) * scale).astype(dk_ref.dtype)
+            dq_ref[0, rows, :] = (tile_dot(k_rows, dscores, CONTRACT_PLAIN) * scale).astype(dq_ref.dtype)
+
+        host_steps(steps, heads, head, work)
         return carry
 
     lax.fori_loop(0, heads, one_head, 0)
 
 
-def attend_specs(groups, width, count, heads):
+def attend_call(kernel, name, wides, lse, marks, heads, outputs, plan, collective_id):
+    groups, width, count = wides[0].shape
     size = width // heads
     step = 8 if heads % 8 == 0 else heads
     wide = pl.BlockSpec((1, step * size, count), lambda g, i: (g, i, 0))
     stats = pl.BlockSpec((1, step, count), lambda g, i: (g, i, 0))
-    marks = pl.BlockSpec((1, SEGMENTS, count), lambda g, i: (g, 0, 0))
-    return size, step, (groups, heads // step), wide, stats, marks
-
-
-def attend_forward(queries, keys, values, away, own, heads):
-    groups, width, count = queries.shape
-    size, step, grid, wide, stats, marks = attend_specs(groups, width, count, heads)
+    mark = pl.BlockSpec((1, SEGMENTS, count), lambda g, i: (g, 0, 0))
+    shape = jax.ShapeDtypeStruct((groups, width, count), jnp.bfloat16)
+    ins, in_specs = list(wides), [wide] * len(wides)
+    out_specs, out_shape = [wide] * outputs, [shape] * outputs
+    if lse is None:
+        out_specs.append(stats)
+        out_shape.append(jax.ShapeDtypeStruct((groups, heads, count), jnp.float32))
+    else:
+        ins.append(lse)
+        in_specs.append(stats)
+    ins += list(marks)
+    in_specs += [mark, mark]
+    extra = {}
+    if plan is not None:
+        ins += plan.arrays
+        in_specs += plan.in_specs
+        out_specs += plan.out_specs
+        out_shape += plan.out_shape
+        extra = dict(collective_id=collective_id, has_side_effects=True)
+    products = 2 if lse is None else 5
     return pl.pallas_call(
-        functools.partial(attend_fwd_kernel, step, size),
-        grid=grid,
-        in_specs=[wide, wide, wide, marks, marks],
-        out_specs=[wide, stats],
-        out_shape=[
-            jax.ShapeDtypeStruct((groups, width, count), jnp.bfloat16),
-            jax.ShapeDtypeStruct((groups, heads, count), jnp.float32),
-        ],
-        compiler_params=pltpu.CompilerParams(vmem_limit_bytes=60 << 20),
+        functools.partial(kernel, step, size, plan),
+        grid=(groups, heads // step),
+        in_specs=in_specs,
+        out_specs=out_specs,
+        out_shape=out_shape,
+        scratch_shapes=plan.scratch if plan is not None else [],
+        compiler_params=pltpu.CompilerParams(vmem_limit_bytes=62 << 20, **extra),
         cost_estimate=pl.CostEstimate(
-            flops=4 * groups * width * count * count,
+            flops=2 * products * groups * width * count * count,
             bytes_accessed=8 * groups * width * count,
             transcendentals=groups * heads * count * count,
         ),
-        name="attend_forward",
-    )(queries, keys, values, away, own)
-
-
-def attend_backward(queries, keys, values, grads, lse, away, own, heads):
-    groups, width, count = queries.shape
-    size, step, grid, wide, stats, marks = attend_specs(groups, width, count, heads)
-    shape = jax.ShapeDtypeStruct((groups, width, count), jnp.bfloat16)
-    return pl.pallas_call(
-        functools.partial(attend_bwd_kernel, step, size),
-        grid=grid,
-        in_specs=[wide, wide, wide, wide, stats, marks, marks],
-        out_specs=[wide, wide, wide],
-        out_shape=[shape, shape, shape],
-        compiler_params=pltpu.CompilerParams(vmem_limit_bytes=60 << 20),
-        cost_estimate=pl.CostEstimate(
-            flops=10 * groups * width * count * count,
-            bytes_accessed=14 * groups * width * count,
-            transcendentals=groups * heads * count * count,
-        ),
-        name="attend_backward",
-    )(queries, keys, values, grads, lse, away, own)
-
-
-def attend_plain(heads, queries, keys, values, away, own):
-    return attend_keep(heads, queries, keys, values, away, own)[0]
-
-
-def attend_keep(heads, queries, keys, values, away, own):
-    queries, keys, values = (t.astype(jnp.bfloat16) for t in (queries, keys, values))
-    mixed, lse = attend_forward(queries, keys, values, away, own, heads)
-    return mixed.astype(jnp.float32), (queries, keys, values, lse, away, own)
-
-
-def attend_pull(heads, saved, grad):
-    queries, keys, values, lse, away, own = saved
-    dq, dk, dv = attend_backward(queries, keys, values, grad.astype(jnp.bfloat16), lse, away, own, heads)
-    none = jnp.zeros_like(away)
-    return tuple(t.astype(jnp.float32) for t in (dq, dk, dv)) + (none, none)
-
-
-def attend(queries, keys, values, marks, heads):
-    rule = jax.custom_vjp(attend_plain, nondiff_argnums=(0,))
-    rule.defvjp(attend_keep, attend_pull)
-    return rule(heads, queries, keys, values, marks[0], marks[1])
+        name=name,
+    )(*ins)
+
+
+def attend_forward(queries, keys, values, marks, heads, plan=None, collective_id=None):
+    outs = attend_call(
+        attend_fwd_kernel, "attend_forward", (queries, keys, values), None, marks, heads, 1, plan, collective_id
+    )
+    return outs[0], outs[1], outs[2:]
+
+
+def attend_backward(queries, keys, values, grads, lse, marks, heads, plan=None, collective_id=None):
+    outs = attend_call(
+        attend_bwd_kernel, "attend_backward", (queries, keys, values, grads), lse, marks, heads, 3, plan, collective_id
+    )
+    return tuple(outs[:3]), outs[3:]
 
 
 def gelu(value):
@@ -277,135 +669,86 @@
     return (jnp.where(hot, 0.0, 1.0).astype(jnp.bfloat16), jnp.where(hot, FAR, 0.0).astype(jnp.bfloat16))
 
 
-def block(stream, marks, params, heads):
-    (
-        gain_one,
-        shift_one,
-        w_qkv,
-        bias_query,
-        bias_value,
-        w_out,
-        bias_out,
-        gain_two,
-        shift_two,
-        w_up,
-        bias_up,
-        w_down,
-        bias_down,
-    ) = params
+def tap_plain(value, spare):
+    return value
+
+
+def tap_fwd(value, spare):
+    return (value, None)
+
+
+def tap_bwd(unused, grad):
+    return (grad, grad.astype(jnp.bfloat16))
+
+
+def tap(value, spare):
+    rule = jax.custom_vjp(tap_plain)
+    rule.defvjp(tap_fwd, tap_bwd)
+    return rule(value, spare)
+
+
+ENCODER_GAINS = (D, D, D)
+ENCODER_BIASES = (D, D, D, D, D, D, FF, D, D, DD, DD)
+DECODER_GAINS = (DD, DD, DD)
+DECODER_BIASES = (DD, DD, DD, DD, DD, DFF, DD, DD, PIX)
+ENCODER_IN = (D, 3 * D, D, FF, DD)
+DECODER_IN = (3 * DD, DD, DFF, PIX)
+
+
+def heads_in(stream, gain, shift, weight, bias_query, bias_value, groups):
     width = stream.shape[1]
-    groups = marks[0].shape[0]
-    normed = value_round(layer_norm(stream, gain_one, shift_one)).reshape(groups, -1, width)
-    joined = jnp.einsum("gtd,df->gft", normed, w_qkv, preferred_element_type=jnp.float32)
+    normed = value_round(layer_norm(stream, gain, shift))
+    joined = jnp.einsum(
+        "gtd,df->gft", normed.reshape(groups, -1, width), weight, preferred_element_type=jnp.float32
+    )
     queries = both(joined[:, :width] + bias_query[None, :, None])
     key_rows = both(joined[:, width : 2 * width])
     values = both(joined[:, 2 * width :] + bias_value[None, :, None])
-    mixed = both(attend(queries, key_rows, values, marks, heads))
-    projected = jnp.einsum("gft,fd->gtd", mixed, w_out, preferred_element_type=jnp.float32).reshape(-1, width)
-    stream = stream + grad_round(projected + bias_out)
+    return (queries, key_rows, values), normed
+
+
+def encoder_open(gains, biases, spare, pixel_rows, positions, w_patch, w_qkv):
+    gain_one = gains[0]
+    bias_patch, shift_one, bias_query, bias_value = biases[:4]
+    stream = grad_round(tap(matmul(pixel_rows, w_patch), spare) + bias_patch) + positions
+    trio, normed = heads_in(stream, gain_one, shift_one, w_qkv, bias_query, bias_value, 1)
+    return (trio, stream), normed
+
+
+def encoder_close(mixed, stream, gains, biases, spares, weights):
+    unused, gain_two, gain_final = gains
+    bias_out, shift_two, bias_up, bias_down, shift_final, bias_lift = biases[4:10]
+    w_out, w_up, w_down, w_lift = weights
+    projected = jnp.einsum("gft,fd->gtd", mixed, w_out, preferred_element_type=jnp.float32)
+    stream = stream + grad_round(tap(projected[0], spares[0]) + bias_out)
+    normed = value_round(layer_norm(stream, gain_two, shift_two))
+    hidden = grad_round(tap(matmul(normed, w_up), spares[1]) + bias_up)
+    active = value_round(gelu(hidden))
+    stream = stream + grad_round(tap(matmul(active, w_down), spares[2]) + bias_down)
+    last = value_round(layer_norm(stream, gain_final, shift_final))
+    lifted = grad_round(tap(matmul(last, w_lift), spares[3]) + bias_lift)
+    return lifted, (normed, active, last)
+
+
+def decoder_open(lifted, mask_token, gains, biases, kept_new, positions, groups, w_qkv):
+    full = jnp.broadcast_to(mask_token[None, :], positions.shape).at[kept_new].set(lifted, unique_indices=True)
+    stream = full + positions
+    trio, normed = heads_in(stream, gains[0], biases[0], w_qkv, biases[1], biases[2], groups)
+    return trio, stream
+
+
+def decoder_close(mixed, stream, gains, biases, weights, target, weight, denom):
+    unused, gain_two, gain_final = gains
+    bias_out, shift_two, bias_up, bias_down, shift_final, bias_head = biases[3:]
+    w_out, w_up, w_down, w_head = weights
+    projected = jnp.einsum("gft,fd->gtd", mixed, w_out, preferred_element_type=jnp.float32)
+    stream = stream + grad_round(projected.reshape(stream.shape) + bias_out)
     normed = value_round(layer_norm(stream, gain_two, shift_two))
     hidden = grad_round(matmul(normed, w_up) + bias_up)
-    return stream + grad_round(
-        matmul(value_round(gelu(hidden)), w_down) + bias_down
-    )
-
-
-def section_a(mats, gain_vec, bias_vec, pixel_rows, kept, order):
-    w_patch, w_qkv, w_out, w_up, w_lift = pieces(mats[0], (D, 3 * D, D, FF, DD))
-    gain_one, gain_two, gain_final = pieces(gain_vec, (D, D, D))
-    (
-        bias_patch,
-        shift_one,
-        bias_query,
-        bias_value,
-        bias_out,
-        shift_two,
-        bias_up,
-        bias_down,
-        shift_final,
-        bias_lift,
-        mask_token,
-    ) = pieces(bias_vec, (D, D, D, D, D, D, FF, D, D, DD, DD))
-    count = pixel_rows.shape[0]
-    places, unused, kept_new = order
-    rows, cols, part, run = places(kept_new)
-    stream = grad_round(matmul(pixel_rows[kept], w_patch) + bias_patch) + sine_table(rows, cols, D)
-    runs = count // (SIDE_BIG * SIDE_BIG)
-    stream = block(
-        stream,
-        segment_marks(part * runs + run, 1),
-        (
-            gain_one,
-            shift_one,
-            w_qkv,
-            bias_query,
-            bias_value,
-            w_out,
-            bias_out,
-            gain_two,
-            shift_two,
-            w_up,
-            bias_up,
-            mats[1],
-            bias_down,
-        ),
-        HEADS,
-    )
-    lifted = grad_round(
-        matmul(value_round(layer_norm(stream, gain_final, shift_final)), w_lift) + bias_lift
-    )
-    full = jnp.broadcast_to(mask_token[None, :], (count, DD)).at[kept_new].set(lifted)
-    rows, cols, part, run = places(jnp.arange(count, dtype=jnp.int32))
-    return full + sine_table(rows, cols, DD)
-
-
-def section_b(mats, gain_vec, bias_vec, stream, pixel_rows, order, denom):
-    w_qkv, w_out, w_up, w_head = pieces(mats[0], (3 * DD, DD, DFF, PIX))
-    gain_one, gain_two, gain_final = pieces(gain_vec[3 * D :], (DD, DD, DD))
-    (
-        shift_one,
-        bias_query,
-        bias_value,
-        bias_out,
-        shift_two,
-        bias_up,
-        bias_down,
-        shift_final,
-        bias_head,
-    ) = pieces(bias_vec[8 * D + FF + 2 * DD :], (DD, DD, DD, DD, DD, DFF, DD, DD, PIX))
-    count = pixel_rows.shape[0]
-    places, old_of_new, kept_new = order
-    rows, cols, part, run = places(jnp.arange(count, dtype=jnp.int32))
-    stream = block(
-        stream,
-        segment_marks(part, count // (SIDE_BIG * SIDE_BIG)),
-        (
-            gain_one,
-            shift_one,
-            w_qkv,
-            bias_query,
-            bias_value,
-            w_out,
-            bias_out,
-            gain_two,
-            shift_two,
-            w_up,
-            bias_up,
-            mats[1],
-            bias_down,
-        ),
-        DHEADS,
-    )
-    predicted = grad_round(
-        matmul(value_round(layer_norm(stream, gain_final, shift_final)), w_head) + bias_head
-    )
-    units = pixel_rows.reshape(-1, SIDE_SMALL * SIDE_SMALL, PIX)
-    pixel_rows = units[old_of_new].reshape(count, PIX).astype(jnp.float32)
-    centered = pixel_rows - jnp.mean(pixel_rows, axis=1, keepdims=True)
-    target = centered * lax.rsqrt(jnp.mean(centered * centered, axis=1, keepdims=True) + 1e-06)
+    stream = stream + grad_round(matmul(value_round(gelu(hidden)), w_down) + bias_down)
+    last = value_round(layer_norm(stream, gain_final, shift_final))
+    predicted = grad_round(matmul(last, w_head) + bias_head)
     error = jnp.mean((predicted - target) ** 2, axis=1)
-    chosen = jnp.any(jnp.arange(count, dtype=jnp.int32)[:, None] == kept_new[None, :], axis=1)
-    weight = jnp.where(chosen, 0.1, 1.0)
     return jnp.sum(error * weight) / denom
 
 
@@ -718,10 +1061,6 @@
     return [w.reshape((math.prod(GRID_DIMS),) + s.shape) for w, s in zip(wholes, shards)]
 
 
-def widen(arrays):
-    return tuple((array.astype(jnp.float32) for array in arrays))
-
-
 def vector_tile(vectors):
     joined = jnp.concatenate(vectors, axis=-1)
     lead, length = joined.shape[:-1], joined.shape[-1]
@@ -731,75 +1070,170 @@
 
 
 def cut_tile(tile, lengths):
-    lead = tile.shape[:-2]
-    flat = tile.reshape(lead + (-1,))
-    return pieces(flat, lengths)
-
-
-def kernels_fit():
-    return (lax.axis_size("dp"), lax.axis_size("fsdp")) == (4, 8)
-
-
-def gather_weights(matrices, vectors):
-    matrices = [m.astype(jnp.bfloat16) for m in matrices]
-    vectors = [v.astype(jnp.bfloat16) for v in vectors]
-    if not kernels_fit():
-        whole = [lax.all_gather(a, AXES, axis=0, tiled=True) for a in matrices + vectors]
-        return whole[: len(matrices)], whole[len(matrices) :]
-    tile = vector_tile(vectors)
-    whole = gather_whole([tile] + matrices, (1,) + GATHER_CUTS, 1)
-    cut = cut_tile(whole[0], [v.shape[0] for v in vectors])
-    full = [w.reshape((-1, w.shape[-1])) for w in whole[1:]]
-    return full, [c.reshape(-1) for c in cut]
-
-
-def scatter_grads(matrices, vectors, loss):
-    if not kernels_fit():
-        sums = [lax.psum_scatter(g, AXES, scatter_dimension=0, tiled=True) for g in matrices + vectors]
-        squares = sum(jnp.sum(g * g) for g in sums)
-        return sums, lax.psum(squares, AXES), lax.psum(loss, AXES)
-    devices = math.prod(GRID_DIMS)
-    blocks = [m.reshape((devices, -1, m.shape[-1])) for m in matrices]
-    tile = vector_tile([v.reshape(devices, -1) for v in vectors])
-    corner = lax.broadcasted_iota(jnp.int32, (8, LANES), 0) + lax.broadcasted_iota(jnp.int32, (8, LANES), 1) == 0
-    outs = scatter_sums(blocks + [tile], SCATTER_CUTS + (1,), jnp.where(corner, loss, 0.0), 2)
-    cut = cut_tile(outs[len(matrices)], [v.shape[0] // devices for v in vectors])
-    totals = outs[-1]
-    return list(outs[: len(matrices)]) + list(cut), jnp.sum(totals[0]), jnp.sum(totals[1])
-
-
-GATHER_CUTS = (4, 2, 2, 1)
-SCATTER_CUTS = (8, 3, 4, 2)
-
-
-def per_device(
-    pixels,
-    resolution,
-    kept,
-    step_count,
-    *state,
-):
+    return pieces(tile.reshape(tile.shape[:-2] + (-1,)), lengths)
+
+
+def starts_of(widths):
+    return [sum(widths[:index]) for index in range(len(widths))]
+
+
+def wide(array):
+    return array.astype(jnp.float32)
+
+
+def narrow(array):
+    return array.astype(jnp.bfloat16)
+
+
+def per_device(pixels, resolution, kept, step_count, *state):
     masters, firsts, seconds = state[:6], state[6:12], state[12:]
     devices = lax.axis_size("dp") * lax.axis_size("fsdp")
-    patches_all = pixels.shape[0] * devices
+    kernels = (lax.axis_size("dp"), lax.axis_size("fsdp")) == (4, 8)
+    count = pixels.shape[0]
+    patches_all = count * devices
     denom = (0.75 + 0.1 * 0.25) * patches_all
-    order = layout(resolution, kept, pixels.shape[0])
-
-    def forward_a(mats, gain_vec, bias_vec):
-        return section_a(mats, gain_vec, bias_vec, pixels, kept, order)
-
-    def forward_b(mats, gain_vec, bias_vec, stream):
-        return section_b(mats, gain_vec, bias_vec, stream, pixels, order, denom)
-
-    matrices, vectors = gather_weights(masters[:4], masters[4:])
-    matrices, vectors = widen(matrices), widen(vectors)
-    lifted, pull_encoder = jax.vjp(forward_a, matrices[:2], *vectors)
-    loss_local, pull_decoder = jax.vjp(forward_b, matrices[2:], *vectors, lifted)
-    decoder_terms, gain_back, bias_back, stream_back = pull_decoder(jnp.ones((), jnp.float32))
-    encoder_terms, gain_front, bias_front = pull_encoder(stream_back)
-    grads, total_squares, loss_total = scatter_grads(
-        list(encoder_terms) + list(decoder_terms), [gain_front + gain_back, bias_front + bias_back], loss_local
+    groups = count // (SIDE_BIG * SIDE_BIG)
+    shards = [narrow(master) for master in masters]
+    lengths = [master.shape[0] for master in masters[4:]]
+    in_starts, out_starts = starts_of(ENCODER_IN), starts_of(DECODER_IN)
+
+    if kernels:
+        tile = vector_tile(shards[4:])
+        listed = [(0, 0, tile.shape[1], 1)]
+        listed += [(1, low, width, cut) for low, width, cut in zip(in_starts, ENCODER_IN, (1, 2, 1, 2, 1))]
+        listed += [(2, 0, D, 2)]
+        listed += [(3, low, width, 1) for low, width in zip(out_starts[:2], DECODER_IN[:2])]
+        whole = run_alone(Gather([tile] + shards[:3], listed), 1, "gather_first")
+        vectors = [v.reshape(-1) for v in cut_tile(whole[0].reshape((devices,) + tile.shape), lengths)]
+        early = [wide(w.reshape(-1, w.shape[-1])) for w in whole[1:]]
+        gather = Gather(shards[2:4], [(0, out_starts[2], DFF, 2), (0, out_starts[3], PIX, 1), (1, 0, DD, 2)])
+    else:
+        whole = [lax.all_gather(shard, AXES, axis=0, tiled=True) for shard in shards]
+        vectors = whole[4:]
+        late = [wide(part) for part in pieces(whole[2], DECODER_IN)]
+        early = [wide(part) for part in pieces(whole[0], ENCODER_IN)] + [wide(whole[1])] + late[:2]
+        gather = None
+    w_patch, w_qkv, w_out, w_up, w_lift, w_down, w_qkv_decoder, w_out_decoder = early
+    vectors = [wide(vector) for vector in vectors]
+    gains = pieces(vectors[0], ENCODER_GAINS + DECODER_GAINS)
+    biases = pieces(vectors[1], ENCODER_BIASES + DECODER_BIASES)
+    enc_gains, dec_gains = gains[:3], gains[3:]
+    enc_biases, mask_token, dec_biases = biases[:10], biases[10], biases[11:]
+
+    places, old_of_new, kept_new = layout(resolution, kept, count)
+    rows, cols, part, run = places(kept_new)
+    enc_marks = segment_marks(part * groups + run, 1)
+    enc_positions = sine_table(rows, cols, D)
+    rows, cols, part, run = places(jnp.arange(count, dtype=jnp.int32))
+    dec_marks = segment_marks(part, groups)
+    dec_positions = sine_table(rows, cols, DD)
+    units = pixels.reshape(-1, SIDE_SMALL * SIDE_SMALL, PIX)
+    pixel_rows = wide(units[old_of_new].reshape(count, PIX))
+    centered = pixel_rows - jnp.mean(pixel_rows, axis=1, keepdims=True)
+    target = centered * lax.rsqrt(jnp.mean(centered * centered, axis=1, keepdims=True) + 1e-06)
+    chosen = jnp.any(jnp.arange(count, dtype=jnp.int32)[:, None] == kept_new[None, :], axis=1)
+    weight = jnp.where(chosen, 0.1, 1.0)
+    kept_pixels = pixels[kept]
+
+    def open_encoder(gains, biases, spare):
+        return encoder_open(gains, biases, spare, wide(kept_pixels), enc_positions, w_patch, w_qkv)
+
+    def close_encoder(mixed, stream, gains, biases, spares):
+        return encoder_close(mixed, stream, gains, biases, spares, (w_out, w_up, w_down, w_lift))
+
+    def open_decoder(lifted, mask_token, gains, biases, weight_in):
+        return decoder_open(lifted, mask_token, gains, biases, kept_new, dec_positions, groups, weight_in)
+
+    def close_decoder(mixed, stream, gains, biases, weights):
+        return decoder_close(mixed, stream, gains, biases, weights, target, weight, denom)
+
+    def spare(width):
+        return jnp.zeros((kept.shape[0], width), jnp.bfloat16)
+
+    (trio, stream), pull_open, normed = jax.vjp(open_encoder, enc_gains, enc_biases, spare(D), has_aux=True)
+    enc_trio = [narrow(t) for t in trio]
+    enc_mixed, enc_lse, unused = attend_forward(*enc_trio, enc_marks, HEADS)
+    spares = [spare(width) for width in (D, FF, D, DD)]
+    lifted, pull_close, saved = jax.vjp(
+        close_encoder, wide(enc_mixed), stream, enc_gains, enc_biases, spares, has_aux=True
     )
+    (trio, stream), pull_dec_open = jax.vjp(open_decoder, lifted, mask_token, dec_gains, dec_biases, w_qkv_decoder)
+    dec_trio = [narrow(t) for t in trio]
+    dec_mixed, dec_lse, late_weights = attend_forward(*dec_trio, dec_marks, DHEADS, gather, 2)
+    if kernels:
+        late = [None, None] + [wide(w.reshape(-1, w.shape[-1])) for w in late_weights]
+        w_down_decoder = late[4]
+    else:
+        w_down_decoder = wide(whole[3])
+    dec_weights = (w_out_decoder, late[2], w_down_decoder, late[3])
+    loss_local, pull_dec_close = jax.vjp(close_decoder, wide(dec_mixed), stream, dec_gains, dec_biases, dec_weights)
+
+    d_mixed, d_stream, d_gains_a, d_biases_a, d_weights = pull_dec_close(jnp.ones((), jnp.float32))
+
+    def terms_of(array, cuts):
+        width = array.shape[1]
+        return Terms(array.shape[0] // devices, width, cuts, array=array)
+
+    late_terms = [terms_of(array, cuts) for array, cuts in zip(d_weights, (1, 4, 4, 2))]
+    scatter = Scatter(late_terms) if kernels else None
+    dec_back, late_sums = attend_backward(
+        *dec_trio, narrow(d_mixed), dec_lse, dec_marks, DHEADS, scatter, 3
+    )
+    d_lifted, d_mask, d_gains_b, d_biases_b, d_qkv = pull_dec_open((tuple(wide(t) for t in dec_back), d_stream))
+    d_mixed, d_stream, e_gains_a, e_biases_a, d_spares = pull_close(d_lifted)
+    enc_back, unused = attend_backward(*enc_trio, narrow(d_mixed), enc_lse, enc_marks, HEADS)
+    e_gains_b, e_biases_b, d_patch = pull_open((tuple(wide(t) for t in enc_back), d_stream))
+
+    def total(a, b):
+        return [x + y for x, y in zip(a, b)]
+
+    gain_terms = jnp.concatenate(total(e_gains_a, e_gains_b) + total(d_gains_a, d_gains_b))
+    bias_terms = jnp.concatenate(total(e_biases_a, e_biases_b) + [d_mask] + total(d_biases_a, d_biases_b))
+    normed_two, active, last = (narrow(value) for value in saved)
+    joined_back = jnp.concatenate([t[0] for t in enc_back], axis=0)
+
+    def product(left, right, dims, cuts):
+        left_axis, right_axis = dims[0][0][0], dims[0][1][0]
+        return Terms(left.shape[1 - left_axis] // devices, right.shape[1 - right_axis], cuts, None, left, right, dims)
+
+    terms = [
+        product(last, d_spares[3], CONTRACT_ROWS, 1),
+        product(active, d_spares[2], CONTRACT_ROWS, 3),
+        product(normed_two, d_spares[1], CONTRACT_ROWS, 4),
+        product(enc_mixed[0], d_spares[0], CONTRACT_PLAIN, 1),
+        terms_of(d_qkv, 2),
+        product(narrow(normed).T, joined_back, CONTRACT_LANES, 3),
+        product(kept_pixels, d_patch, CONTRACT_ROWS, 2),
+    ]
+    if kernels:
+        tile = vector_tile([vector.reshape(devices, -1) for vector in (gain_terms, bias_terms)])
+        tile_terms = Terms(tile.shape[1], tile.shape[2], 1, array=tile)
+        spot = lax.broadcasted_iota(jnp.int32, (8, LANES), 0) + lax.broadcasted_iota(jnp.int32, (8, LANES), 1)
+        plan = Scatter(terms[:5] + [tile_terms] + terms[5:], jnp.where(spot == 0, loss_local, 0.0))
+        sums = list(run_alone(plan, 4, "scatter_last", late_sums))
+        totals = sums.pop()
+        vector_sums = cut_tile(sums.pop(5), lengths)
+        total_squares, loss_total = jnp.sum(totals[0]), jnp.sum(totals[1])
+    else:
+
+        def scattered(array):
+            return lax.psum_scatter(array, AXES, scatter_dimension=0, tiled=True)
+
+        sums = [
+            scattered(t.array if t.array is not None else tile_dot(t.left, t.right, t.dims)) for t in terms
+        ]
+        late_sums = [scattered(array) for array in d_weights]
+        vector_sums = [scattered(vector) for vector in (gain_terms, bias_terms)]
+        squares = sum(jnp.sum(g * g) for g in list(sums) + list(late_sums) + list(vector_sums))
+        total_squares, loss_total = lax.psum(squares, AXES), lax.psum(loss_local, AXES)
+    g_lift, g_down, g_up, g_out, g_qkv_decoder, g_qkv, g_patch = sums
+    g_out_decoder, g_up_decoder, g_down_decoder, g_head = late_sums
+    grads = [
+        jnp.concatenate([g_patch, g_qkv, g_out, g_up, g_lift], axis=1),
+        g_down,
+        jnp.concatenate([g_qkv_decoder, g_out_decoder, g_up_decoder, g_head], axis=1),
+        g_down_decoder,
+    ] + list(vector_sums)
     grad_norm = jnp.sqrt(total_squares)
     factor = jnp.minimum(1.0, 0.5 / math.sqrt(patches_all) / (grad_norm + 1e-06))
     times = step_count[0].astype(jnp.float32)

time: 774 us -> 718 us (0.928)
  Pallas kernels: 476 us -> 443 us
  other arithmetic: 105 us -> 76.7 us
  matrix products: 127 us -> 110 us
  local copies, waits for them, and re-layouts: 52.2 us -> 68.6 us
    pallas_call x6, Pallas kernels: 476 us -> 443 us  [the longest x2 276 us: run_alone(): pl.pallas_call(kernel, in_specs=plan.in_specs + [WHOLE_VMEM] * len(more),...]
    dot_general x0 -> x4, local copies, waits for them, and re-layouts: none -> 14.8 us  [the longest x2 10.1 us: heads_in(): jnp.einsum('gtd,df->gft', normed.reshape(groups, -1, width), weight, pref...]
    add_any x4 -> x1, other arithmetic: 13.9 us -> 1.13 us  [layer_norm(): centered = stream - jnp.mean(stream, axis=1, keepdims=True)]
    sin x2, other arithmetic: 11.3 us -> 0.22 us  [sine_table(): half = jnp.concatenate([jnp.sin(angles), jnp.cos(angles)], axis=1)]
    dot_general x20 -> x16, matrix products: 86.7 us -> 75.7 us  [matmul(): return jnp.dot(left, right, preferred_element_type=jnp.float32)]
    unnamed x278 -> x284, local copies, waits for them, and re-layouts: 21.5 us -> 23.6 us
    reduce_sum x19 -> x18, other arithmetic: 18 us -> 17.7 us  [the longest x2 3.95 us: heads_in(): values = both(joined[:, 2 * width:] + bias_value[None, :, None])]
where the time goes in v3:
time: 718 us; the launch traced here: 706 us
  Pallas kernels  443 us (62%)
  matrix products  110 us (15%)
  other arithmetic  76.7 us (11%)
  local copies, waits for them, and re-layouts  68.6 us (10%)
  between operations  7.68 us (1%)
    pallas_call x2, Pallas kernels, run_alone(): pl.pallas_call(kernel, in_specs=plan.in_specs + [WHOLE_VMEM] * len(more),...  276 us
    pallas_call x4, Pallas kernels, attend_call(): pl.pallas_call(functools.partial(kernel, step, size, plan), grid=(groups,...  167 us
    dot_general x16, matrix products, matmul(): return jnp.dot(left, right, preferred_element_type=jnp.float32)  75.7 us
    unnamed x284, local copies, waits for them, and re-layouts  23.6 us
    dot_general x5, matrix products, heads_in(): jnp.einsum('gtd,df->gft', normed.reshape(groups, -1, width), weight, pref...  23.1 us

profile of v3, /device:TPU:0, one launch (start us, length us, event | category | flops | bytes accessed | tf_op | source)
XLA Modules:
  0.0 706.3 jit_solution(11605990806656154308)
XLA Ops:
  28.0 2.7 reshape.639
  30.7 93.6 %gather_first.1 = (bf16[2,2,4,2,8,128]{5,4,3,2,1,0:T(8,128)(2,1)}, bf16[2,2,4,2,24,768]{5,4,3,2,1,0:T(8,128)(2,1)}, bf16[2,2,4,2,24,2304]{5,4,3,2,1,0:T(8,128)(2...) custom-call(bf16[8,128]{1,0:T(8,128)(2,1)} %fusion.98.refs_0_, ...), custom_call_target="tpu_custom_call" | custom-call | flops 661504 | bytes 1323008 | tf_op jit(solution)/shard_map/gather_first/pallas_call | solution.py:507
  132.2 4.1 convolution_bitcast_fusion.1
  138.8 10.2 %attend_forward.2 = (bf16[1,768,392]{2,1,0:T(8,128)(2,1)}, f32[1,12,392]{2,1,0:T(8,128)}) custom-call(bf16[1,768,392]{2,1,0:T(8,128)(2,1)} %get-tuple-element.149.refs_0_, bf16[1,768,392]{2,1,0:T(8,128)(2,1)} %slice.223.refs_1_, bf16[1,768,392]{2,1,0:T(8,128)(2,1)} %get-tuple-element.148.refs_2_, bf16[1,16,392]{2,1,0:T(8,128)(2,1)} %get-tuple-element.181.refs_3_.refs_5_, ...), custom_call_target="tpu_custom_call" | custom-call | flops 472055808 | bytes 2408448 | tf_op jit(solution)/shard_map/attend_forward/pallas_call | solution.py:631
  153.2 6.2 multiply_convert_fusion.2
  164.9 3.6 scatter_fusion
  175.2 3.1 convolution_bitcast_fusion
  182.1 56.9 %attend_forward.3 = (bf16[2,512,784]{2,1,0:T(8,128)(2,1)}, f32[2,16,784]{2,1,0:T(8,128)}, bf16[2,2,4,2,16,2048]{5,4,3,2,1,0:T(8,128)(2,1)}, bf16[2,2,4,2,16,768]...) custom-call(bf16[2,512,784]{2,1,0:T(8,128)(2,1)} %get-tuple-element.145.refs_0_, bf16[2,512,784]{2,1,0:T(8,128)(2,1)} %slice.222.refs_1_, ...), custom_call_target="tpu_custom_call" | custom-call | flops 2517630976 | bytes 6422528 | tf_op jit(solution)/shard_map/attend_forward/pallas_call | solution.py:631
  239.0 3.6 copy.74
  242.7 2.6 fusion.141
  248.0 8.2 %multiply_convert_fusion = (bf16[1568,2048]{1,0:T(8,128)(2,1)S(1)}, f32[1568,2048]{1,0:T(8,128)}) fusion(f32[2048]{0:T(1024)S(1)} %slice.189, bf16[1568,512]{1,0:T(8,128)(2,1)S(1)} %add_convert_fusion.3, bf16[512,2048]{1,0:T(8,128)(2,1)S(1)} %bitcast.183), kind=kOutput, calls=%fused_computation.7 | convolution fusion | flops 3307601920 | bytes 22978560 | tf_op jit(solution)/shard_map/jvp()/dot_general | solution.py:70
  256.3 3.7 fusion.142
  261.8 3.9 multiply_reduce_fusion.1
  266.9 5.1 fusion.145
  273.1 2.9 multiply_reduce_fusion.2
  280.1 11.5 %add_convert_fusion = bf16[1568,2048]{1,0:T(8,128)(2,1)S(1)} fusion(f32[1568,2048]{1,0:T(8,128)} %get-tuple-element.207, bf16[1568,512]{1,0:T(8,128)(2,1)S(1)} %add_convert_fusion.5, bf16[2048,512]{1,0:T(8,128)(2,1)S(1)} %bitcast.186, f32[2048]{0:T(1024)S(1)} %slice.189), kind=kOutput, calls=%fused_computation.6 | convolution fusion | flops 3333292032 | bytes 22978560 | tf_op jit(solution)/shard_map/transpose(jvp())/dot_general | solution.py:70
  291.6 5.7 fusion.144
  300.1 5.0 multiply_reduce_fusion.3
  305.2 5.6 fusion.143
  321.4 87.4 %attend_backward.2 = (bf16[2,512,784]{2,1,0:T(8,128)(2,1)}, bf16[2,512,784]{2,1,0:T(8,128)(2,1)}, bf16[2,512,784]{2,1,0:T(8,128)(2,1)}, f32[16,512]{1,0:T(8,128)...) custom-call(bf16[2,512,784]{2,1,0:T(8,128)(2,1)} %get-tuple-element.145.refs_0_, ...), custom_call_target="tpu_custom_call" | custom-call | flops 6294077440 | bytes 6422528 | tf_op jit(solution)/shard_map/attend_backward/pallas_call | solution.py:631
  419.9 4.8 fusion
  424.6 6.1 fusion.2
  430.7 8.2 %copy.78 = bf16[2,784,1536]{2,1,0:T(8,128)(2,1)} copy(bf16[2,784,1536]{1,2,0:T(8,128)(2,1)} %fusion.2) | data formatting | bytes 9633792 | tf_op jit(solution)/shard_map/transpose(jvp(gtd,df->gft))/dot_general | solution.py:701
  438.9 7.1 %multiply_reduce_fusion.4 = (f32[512]{0:T(512)}, f32[1568]{0:T(1024)S(1)}, f32[512]{0:T(512)}, f32[1568,512]{1,0:T(8,128)S(1)}) fusion(f32[1568,512]{1,0:T(8,128)S(1)} %copy-done.2, f32[1568]{0:T(1024)S(1)} %fusion.81, f32[1568]{0:T(1024)S(1)} %broadcast_multiply_fusion.3, f32[512]{0:T(512)S(1)} %get-tuple-element.223, bf16[1568,1536]{1,0:T(8,128)(2,1)} %bitcast.147, ...), kind=kOutput, calls=%fused_computation.47 | convolution fusion | flops 2472670720 | bytes 12837248 | tf_op jit(solution)/shard_map/transpose(jvp(gtd,df->gft))/dot_general | solution.py:701
  454.9 3.6 scatter_custom_fusion.1
  461.4 2.9 multiply_reduce_fusion.12
  465.1 6.6 add_convert_fusion.1.refs_5_
  471.8 2.9 multiply_reduce_fusion.13
  479.1 12.8 %attend_backward.3 = (bf16[1,768,392]{2,1,0:T(8,128)(2,1)}, bf16[1,768,392]{2,1,0:T(8,128)(2,1)}, bf16[1,768,392]{2,1,0:T(8,128)(2,1)}) custom-call(bf16[1,768,392]{2,1,0:T(8,128)(2,1)} %get-tuple-element.149.refs_0_, bf16[1,768,392]{2,1,0:T(8,128)(2,1)} %slice.223.refs_1_, bf16[1,768,392]{2,1,0:T(8,128)(2,1)} %get-tuple-element.148.refs_2_, ...), custom_call_target="tpu_custom_call" | custom-call | flops 1180139520 | bytes 2408448 | tf_op jit(solution)/shard_map/attend_backward/pallas_call | solution.py:631
  498.1 4.0 multiply_reduce_fusion.14
  506.9 2.9 pad_maximum_fusion.refs_11_
  509.9 182.1 %scatter_last.1 = (f32[24,512]{1,0:T(8,128)}, f32[96,768]{1,0:T(8,128)}, f32[24,3072]{1,0:T(8,128)}, f32[24,768]{1,0:T(8,128)}, f32[16,1536]{1,0:T(8,128)}, /*in...) custom-call(bf16[392,768]{1,0:T(8,128)(2,1)} %copy-done.35, ...), custom_call_target="tpu_custom_call" | custom-call | flops 15122432 | bytes 30244864 | tf_op jit(solution)/shard_map/scatter_last/pallas_call | solution.py:507
  (443 shorter events, 128.8 us)
Async XLA Ops:
  0.7 19.0 %copy-start.12 = (bf16[1568,768]{1,0:T(8,128)(2,1)S(1)}, bf16[1568,768]{1,0:T(8,128)(2,1)}, u32[]{:S(2)}) copy-start(bf16[1568,768]{1,0:T(8,128)(2,1)} %param.22) | copy-start | bytes 7225348
  10.7 154.3 %copy-start.87 = (s32[392]{0:T(512)}, s32[392]{0:T(512)S(1)}, u32[]{:S(2)}) copy-start(s32[392]{0:T(512)S(1)} %get-tuple-element.176) | copy-start | bytes 4708
  21.9 103.7 %copy-start.36 = (bf16[392,768]{1,0:T(8,128)(2,1)}, bf16[392,768]{1,0:T(8,128)(2,1)S(1)}, u32[]{:S(2)}) copy-start(bf16[392,768]{1,0:T(8,128)(2,1)S(1)} %gather_fusion) | copy-start | bytes 1806340
  125.5 27.7 %copy-start.89 = (f32[3072]{0:T(1024)}, f32[3072]{0:T(1024)S(1)}, u32[]{:S(2)}) copy-start(f32[3072]{0:T(1024)S(1)} %slice.173) | copy-start | bytes 36868
  125.6 26.7 %copy-start.65 = (f32[768]{0:T(1024)}, f32[768]{0:T(1024)S(1)}, u32[]{:S(2)}) copy-start(f32[768]{0:T(1024)S(1)} %get-tuple-element.221) | copy-start | bytes 9220
  125.6 36.5 %copy-start.67 = (f32[768]{0:T(1024)}, f32[768]{0:T(1024)S(1)}, u32[]{:S(2)}) copy-start(f32[768]{0:T(1024)S(1)} %get-tuple-element.222) | copy-start | bytes 9220
  128.4 20.6 %copy-start.8 = (f32[392,768]{1,0:T(8,128)}, f32[392,768]{1,0:T(8,128)S(1)}, u32[]{:S(2)}) copy-start(f32[392,768]{1,0:T(8,128)S(1)} %get-tuple-element.195) | copy-start | bytes 3612676
  128.7 7.6 %copy-start.75 = (f32[392]{0:T(512)}, f32[392]{0:T(512)S(1)}, u32[]{:S(2)}) copy-start(f32[392]{0:T(512)S(1)} %fusion.103) | copy-start | bytes 4708
  151.3 8.1 %copy-start.13 = (f32[392,768]{1,0:T(8,128)}, f32[392,768]{1,0:T(8,128)S(1)}, u32[]{:S(2)}) copy-start(f32[392,768]{1,0:T(8,128)S(1)} %get-tuple-element.197) | copy-start | bytes 3612676
  161.7 6.8 copy-start.73
  245.3 10.9 %copy-start.5 = (f32[1568,512]{1,0:T(8,128)}, f32[1568,512]{1,0:T(8,128)S(1)}, u32[]{:S(2)}) copy-start(f32[1568,512]{1,0:T(8,128)S(1)} %get-tuple-element.205) | copy-start | bytes 9633796
  248.0 8.2 %copy-start.41 = (bf16[1568,512]{1,0:T(8,128)(2,1)}, bf16[1568,512]{1,0:T(8,128)(2,1)S(1)}, u32[]{:S(2)}) copy-start(bf16[1568,512]{1,0:T(8,128)(2,1)S(1)} %add_convert_fusion.3) | copy-start | bytes 4816900
  248.0 8.2 %copy-start.114 = (bf16[2,2,4,2,64,512]{5,4,3,2,1,0:T(8,128)(2,1)S(1)}, bf16[2,2,4,2,64,512]{5,4,3,2,1,0:T(8,128)(2,1)}, u32[]{:S(2)}) copy-start(bf16[2,2,4,2,64,512]{5,4,3,2,1,0:T(8,128)(2,1)} %get-tuple-element.67) | copy-start | bytes 6291460
  248.0 13.2 %slice-start = ((s8[4816896]{0:T(1024)(128)(4,1)}), s8[4194304]{0:T(1024)(128)(4,1)S(1)}, s32[]{:S(2)}) async-start(s8[4816896]{0:T(1024)(128)(4,1)} %bitcast.145), calls=%async_computation | async-start | bytes 8388608
  277.3 34.9 %copy-start.3 = (f32[1568,512]{1,0:T(8,128)}, f32[1568,512]{1,0:T(8,128)S(1)}, u32[]{:S(2)}) copy-start(f32[1568,512]{1,0:T(8,128)S(1)} %get-tuple-element.141) | copy-start | bytes 9633796
  277.3 14.2 %slice-start.6 = ((s8[6422528]{0:T(1024)(128)(4,1)}), s8[4194304]{0:T(1024)(128)(4,1)S(1)}, s32[]{:S(2)}) async-start(s8[6422528]{0:T(1024)(128)(4,1)} %bitcast.189), calls=%async_computation.6 | async-start | bytes 8388608
  280.1 11.5 %slice-start.7 = ((s8[6422528]{0:T(1024)(128)(4,1)}), s8[2228224]{0:T(1024)(128)(4,1)S(1)}, s32[]{:S(2)}) async-start(s8[6422528]{0:T(1024)(128)(4,1)} %bitcast.189), calls=%async_computation.7 | async-start | bytes 4456448
  430.7 8.2 %copy-start.2 = (f32[1568,512]{1,0:T(8,128)S(1)}, f32[1568,512]{1,0:T(8,128)}, u32[]{:S(2)}) copy-start(f32[1568,512]{1,0:T(8,128)} %copy-done) | copy-start | bytes 9633796
  438.9 7.1 %copy-start.58 = (f32[1568]{0:T(1024)S(1)}, f32[1568]{0:T(1024)}, u32[]{:S(2)}) copy-start(f32[1568]{0:T(1024)} %copy-done.57) | copy-start | bytes 18820
  464.3 7.4 %slice-start.2 = ((s8[4718592]{0:T(1024)(128)(4,1)}), s8[4194304]{0:T(1024)(128)(4,1)S(1)}, s32[]{:S(2)}) async-start(s8[4718592]{0:T(1024)(128)(4,1)} %bitcast.167), calls=%async_computation.2 | async-start | bytes 8388608
  465.0 10.3 %copy-start.28 = (bf16[392,768]{1,0:T(8,128)(2,1)}, bf16[392,768]{1,0:T(8,128)(2,1)S(1)}, u32[]{:S(2)}) copy-start(bf16[392,768]{1,0:T(8,128)(2,1)S(1)} %add_convert_fusion.10.refs_3_) | copy-start | bytes 1806340
  509.8 187.1 %copy-start.50 = (f32[64,512]{1,0:T(8,128)S(1)}, f32[64,512]{1,0:T(8,128)}, u32[]{:S(2)}) copy-start(f32[64,512]{1,0:T(8,128)} %get-tuple-element.79.refs_17_) | copy-start | bytes 393220
  509.8 187.1 %copy-start.52 = (f32[64,512]{1,0:T(8,128)S(1)}, f32[64,512]{1,0:T(8,128)}, u32[]{:S(2)}) copy-start(f32[64,512]{1,0:T(8,128)} %param.29) | copy-start | bytes 393220
  509.8 189.0 %copy-start.45 = (f32[96,768]{1,0:T(8,128)S(1)}, f32[96,768]{1,0:T(8,128)}, u32[]{:S(2)}) copy-start(f32[96,768]{1,0:T(8,128)} %param.27) | copy-start | bytes 884740
  509.9 191.2 %copy-start.49 = (f32[16,2048]{1,0:T(8,128)S(1)}, f32[16,2048]{1,0:T(8,128)}, u32[]{:S(2)}) copy-start(f32[16,2048]{1,0:T(8,128)} %get-tuple-element.78.refs_16_) | copy-start | bytes 393220
  692.0 9.0 %copy-start.43 = (f32[16,4864]{1,0:T(8,128)S(1)}, f32[16,4864]{1,0:T(8,128)}, u32[]{:S(2)}) copy-start(f32[16,4864]{1,0:T(8,128)} %param.28) | copy-start | bytes 933892
  692.0 9.0 %copy-start.53 = (f32[16,4864]{1,0:T(8,128)S(1)}, f32[16,4864]{1,0:T(8,128)}, u32[]{:S(2)}) copy-start(f32[16,4864]{1,0:T(8,128)} %param.40) | copy-start | bytes 933892
  692.0 9.0 %copy-start.54 = (f32[16,4864]{1,0:T(8,128)S(1)}, f32[16,4864]{1,0:T(8,128)}, u32[]{:S(2)}) copy-start(f32[16,4864]{1,0:T(8,128)} %param.34) | copy-start | bytes 933892
  692.0 11.0 %copy-start.60 = (f32[24,768]{1,0:T(8,128)S(1)}, f32[24,768]{1,0:T(8,128)}, u32[]{:S(2)}) copy-start(f32[24,768]{1,0:T(8,128)} %get-tuple-element.82) | copy-start | bytes 221188
  692.0 11.1 %copy-start.59 = (f32[24,768]{1,0:T(8,128)S(1)}, f32[24,768]{1,0:T(8,128)}, u32[]{:S(2)}) copy-start(f32[24,768]{1,0:T(8,128)} %get-tuple-element.84) | copy-start | bytes 221188
  692.1 11.1 %copy-start.55 = (f32[24,3072]{1,0:T(8,128)S(1)}, f32[24,3072]{1,0:T(8,128)}, u32[]{:S(2)}) copy-start(f32[24,3072]{1,0:T(8,128)} %get-tuple-element.85) | copy-start | bytes 884740
  694.2 8.9 %copy-start.56 = (f32[24,2304]{1,0:T(8,128)S(1)}, f32[24,2304]{1,0:T(8,128)}, u32[]{:S(2)}) copy-start(f32[24,2304]{1,0:T(8,128)} %get-tuple-element.83) | copy-start | bytes 663556
  (95 other events, 334.1 us)

commit v4 on v3

--- a/solution.py
+++ b/solution.py
@@ -156,6 +156,7 @@
 GRID_DIMS = (2, 2, 4, 2)
 DEVICE_BLOCKS = 32
 MESH_IDS = pl.DeviceIdType.MESH
+SPACING = 2
 WHOLE_VMEM = pl.BlockSpec(memory_space=pltpu.VMEM)
 LEFT_ALONE = pl.BlockSpec(memory_space=pl.ANY)
 
@@ -354,9 +355,10 @@
                 begin(0)
             if t + 1 < count:
                 begin(t + 1)
-            for back, stage in enumerate((stage_one, stage_two, stage_three, stage_four)):
-                if 0 <= t - back < count:
-                    stage(t - back)
+            for number, stage in enumerate((stage_one, stage_two, stage_three, stage_four)):
+                j = t - SPACING * number
+                if 0 <= j < count:
+                    stage(j)
 
         def finish():
             again = {before for index, low, width, before in chunks if before is not None and terms[index].array is None}
@@ -403,7 +405,7 @@
             for copy in tail:
                 copy.wait_send()
 
-        parts = [functools.partial(run, t) for t in range(count + 3)]
+        parts = [functools.partial(run, t) for t in range(count + 3 * SPACING)]
         return parts + ([totals] if self.loss is not None else []) + [finish]
 
 
@@ -415,11 +417,11 @@
             for start, wide in column_cuts(width, cuts):
                 self.chunks.append((shard, low + start, len(self.out_shape), start, wide))
             self.out_shape.append(
-                jax.ShapeDtypeStruct(GRID_DIMS + (shards[shard].shape[0], width), shards[shard].dtype)
+                jax.ShapeDtypeStruct(GRID_DIMS + (shards[shard].shape[0], width), jnp.bfloat16)
             )
         self.out_specs = [LEFT_ALONE] * len(self.out_shape)
         count = len(self.chunks)
-        self.scratch = [
+        self.scratch = [pltpu.VMEM(shard.shape, jnp.bfloat16) for shard in shards] + [
             pltpu.SemaphoreType.DMA((count, 10)),
             pltpu.SemaphoreType.DMA((count, 10)),
             pltpu.SemaphoreType.DMA((count,)),
@@ -427,7 +429,8 @@
 
     def steps(self, ins, outs, scratch):
         chunks, count = self.chunks, len(self.chunks)
-        send_sem, recv_sem, own_sem = scratch
+        sources, rounded = ins, scratch[:-3]
+        send_sem, recv_sem, own_sem = scratch[-3:]
         x, core, z, y, partners = place_of()
         first, second = xy_of(core, x, y)
 
@@ -443,7 +446,7 @@
 
         def mine(j):
             shard, source, out, low, width = chunks[j]
-            return ins[shard].at[:, pl.ds(source, width)], outs[out].at[x, core, z, y, :, pl.ds(low, width)]
+            return rounded[shard].at[:, pl.ds(source, width)], outs[out].at[x, core, z, y, :, pl.ds(low, width)]
 
         def own(j):
             source, target = mine(j)
@@ -470,11 +473,13 @@
 
         def run(t):
             if t == 0:
+                for source, target in zip(sources, rounded):
+                    target[...] = source[...].astype(jnp.bfloat16)
                 greet(partners)
                 for j in range(count):
                     own(j).start()
             for s, stage in enumerate(stages):
-                j = t - s
+                j = t - SPACING * s
                 if 0 <= j < count:
                     if s == 1:
                         own(j).wait()
@@ -493,7 +498,7 @@
                     for copy in stage(j):
                         copy.wait_send()
 
-        return [functools.partial(run, t) for t in range(count + len(stages) - 1)] + [finish]
+        return [functools.partial(run, t) for t in range(count + SPACING * (len(stages) - 1))] + [finish]
 
 
 def run_alone(plan, collective_id, name, more=()):
@@ -551,20 +556,20 @@
 
 
 def attend_fwd_kernel(heads, size, plan, *refs):
-    (q_ref, k_ref, v_ref, away_ref, own_ref), (o_ref, lse_ref), steps = hosted_refs(refs, 5, 2, plan)
+    (qkv_ref, away_ref, own_ref), (o_ref, lse_ref), steps = hosted_refs(refs, 3, 2, plan)
     factor = LOG2E / math.sqrt(size)
 
     def one_head(head, carry):
         def work():
             rows = pl.ds(pl.multiple_of(head * size, size), size)
-            queries = jnp.concatenate([q_ref[0, rows, :], away_ref[0]], axis=0)
-            keys = jnp.concatenate([k_ref[0, rows, :], own_ref[0]], axis=0)
+            queries = jnp.concatenate([qkv_ref[0, 0, rows, :], away_ref[0]], axis=0)
+            keys = jnp.concatenate([qkv_ref[0, 1, rows, :], own_ref[0]], axis=0)
             scores = tile_dot(keys, queries, CONTRACT_ROWS)
             top = jnp.max(scores, axis=0, keepdims=True)
             shifted = jnp.exp2((scores - top) * factor)
             total = jnp.sum(shifted, axis=0, keepdims=True)
             weights = (shifted * (1.0 / total)).astype(jnp.bfloat16)
-            o_ref[0, rows, :] = tile_dot(v_ref[0, rows, :], weights, CONTRACT_PLAIN).astype(o_ref.dtype)
+            o_ref[0, rows, :] = tile_dot(qkv_ref[0, 2, rows, :], weights, CONTRACT_PLAIN).astype(o_ref.dtype)
             lse_ref[0, pl.ds(head, 1), :] = top * factor + jnp.log2(total)
 
         host_steps(steps, heads, head, work)
@@ -574,27 +579,27 @@
 
 
 def attend_bwd_kernel(heads, size, plan, *refs):
-    ins, (dq_ref, dk_ref, dv_ref), steps = hosted_refs(refs, 7, 3, plan)
-    q_ref, k_ref, v_ref, do_ref, lse_ref, away_ref, own_ref = ins
+    ins, (back_ref,), steps = hosted_refs(refs, 5, 1, plan)
+    qkv_ref, do_ref, lse_ref, away_ref, own_ref = ins
     scale = 1.0 / math.sqrt(size)
     factor = LOG2E * scale
 
     def one_head(head, carry):
         def work():
             rows = pl.ds(pl.multiple_of(head * size, size), size)
-            q_rows, k_rows, do_rows = q_ref[0, rows, :], k_ref[0, rows, :], do_ref[0, rows, :]
+            q_rows, k_rows, do_rows = qkv_ref[0, 0, rows, :], qkv_ref[0, 1, rows, :], do_ref[0, rows, :]
             queries = jnp.concatenate([q_rows, away_ref[0]], axis=0)
             keys = jnp.concatenate([k_rows, own_ref[0]], axis=0)
             scores = tile_dot(keys, queries, CONTRACT_ROWS)
             weights = jnp.exp2(scores * factor - lse_ref[0, pl.ds(head, 1), :])
-            spread = tile_dot(v_ref[0, rows, :], do_rows, CONTRACT_ROWS)
+            spread = tile_dot(qkv_ref[0, 2, rows, :], do_rows, CONTRACT_ROWS)
             product = weights * spread
             inner = jnp.sum(product, axis=0, keepdims=True)
             dscores = (product - weights * inner).astype(jnp.bfloat16)
             rounded = weights.astype(jnp.bfloat16)
-            dv_ref[0, rows, :] = tile_dot(do_rows, rounded, CONTRACT_LANES).astype(dv_ref.dtype)
-            dk_ref[0, rows, :] = (tile_dot(q_rows, dscores, CONTRACT_LANES) * scale).astype(dk_ref.dtype)
-            dq_ref[0, rows, :] = (tile_dot(k_rows, dscores, CONTRACT_PLAIN) * scale).astype(dq_ref.dtype)
+            back_ref[0, 2, rows, :] = tile_dot(do_rows, rounded, CONTRACT_LANES).astype(back_ref.dtype)
+            back_ref[0, 1, rows, :] = (tile_dot(q_rows, dscores, CONTRACT_LANES) * scale).astype(back_ref.dtype)
+            back_ref[0, 0, rows, :] = (tile_dot(k_rows, dscores, CONTRACT_PLAIN) * scale).astype(back_ref.dtype)
 
         host_steps(steps, heads, head, work)
         return carry
@@ -602,22 +607,26 @@
     lax.fori_loop(0, heads, one_head, 0)
 
 
-def attend_call(kernel, name, wides, lse, marks, heads, outputs, plan, collective_id):
-    groups, width, count = wides[0].shape
+def attend_call(kernel, name, trio, grads, lse, marks, heads, plan, collective_id):
+    groups, three, width, count = trio.shape
     size = width // heads
     step = 8 if heads % 8 == 0 else heads
+    triple = pl.BlockSpec((1, three, step * size, count), lambda g, i: (g, 0, i, 0))
     wide = pl.BlockSpec((1, step * size, count), lambda g, i: (g, i, 0))
     stats = pl.BlockSpec((1, step, count), lambda g, i: (g, i, 0))
     mark = pl.BlockSpec((1, SEGMENTS, count), lambda g, i: (g, 0, 0))
-    shape = jax.ShapeDtypeStruct((groups, width, count), jnp.bfloat16)
-    ins, in_specs = list(wides), [wide] * len(wides)
-    out_specs, out_shape = [wide] * outputs, [shape] * outputs
-    if lse is None:
-        out_specs.append(stats)
-        out_shape.append(jax.ShapeDtypeStruct((groups, heads, count), jnp.float32))
+    forward = grads is None
+    ins, in_specs = [trio], [triple]
+    if forward:
+        out_specs = [wide, stats]
+        out_shape = [
+            jax.ShapeDtypeStruct((groups, width, count), jnp.bfloat16),
+            jax.ShapeDtypeStruct((groups, heads, count), jnp.float32),
+        ]
     else:
-        ins.append(lse)
-        in_specs.append(stats)
+        ins += [grads, lse]
+        in_specs += [wide, stats]
+        out_specs, out_shape = [triple], [jax.ShapeDtypeStruct(trio.shape, jnp.bfloat16)]
     ins += list(marks)
     in_specs += [mark, mark]
     extra = {}
@@ -627,7 +636,7 @@
         out_specs += plan.out_specs
         out_shape += plan.out_shape
         extra = dict(collective_id=collective_id, has_side_effects=True)
-    products = 2 if lse is None else 5
+    products = 2 if forward else 5
     return pl.pallas_call(
         functools.partial(kernel, step, size, plan),
         grid=(groups, heads // step),
@@ -645,18 +654,14 @@
     )(*ins)
 
 
-def attend_forward(queries, keys, values, marks, heads, plan=None, collective_id=None):
-    outs = attend_call(
-        attend_fwd_kernel, "attend_forward", (queries, keys, values), None, marks, heads, 1, plan, collective_id
-    )
+def attend_forward(trio, marks, heads, plan=None, collective_id=None):
+    outs = attend_call(attend_fwd_kernel, "attend_forward", trio, None, None, marks, heads, plan, collective_id)
     return outs[0], outs[1], outs[2:]
 
 
-def attend_backward(queries, keys, values, grads, lse, marks, heads, plan=None, collective_id=None):
-    outs = attend_call(
-        attend_bwd_kernel, "attend_backward", (queries, keys, values, grads), lse, marks, heads, 3, plan, collective_id
-    )
-    return tuple(outs[:3]), outs[3:]
+def attend_backward(trio, grads, lse, marks, heads, plan=None, collective_id=None):
+    outs = attend_call(attend_bwd_kernel, "attend_backward", trio, grads, lse, marks, heads, plan, collective_id)
+    return outs[0], outs[1:]
 
 
 def gelu(value):
@@ -701,10 +706,9 @@
     joined = jnp.einsum(
         "gtd,df->gft", normed.reshape(groups, -1, width), weight, preferred_element_type=jnp.float32
     )
-    queries = both(joined[:, :width] + bias_query[None, :, None])
-    key_rows = both(joined[:, width : 2 * width])
-    values = both(joined[:, 2 * width :] + bias_value[None, :, None])
-    return (queries, key_rows, values), normed
+    added = jnp.concatenate([bias_query, jnp.zeros_like(bias_query), bias_value])
+    trio = both(joined + added[None, :, None])
+    return trio.reshape(groups, 3, width, -1), normed
 
 
 def encoder_open(gains, biases, spare, pixel_rows, positions, w_patch, w_qkv):
@@ -765,6 +769,7 @@
 AXES = ("dp", "fsdp")
 GRID_DIMS = (2, 2, 4, 2)
 MESH_IDS = pl.DeviceIdType.MESH
+SPACING = 2
 
 
 def place_of():
@@ -1093,22 +1098,21 @@
     patches_all = count * devices
     denom = (0.75 + 0.1 * 0.25) * patches_all
     groups = count // (SIDE_BIG * SIDE_BIG)
-    shards = [narrow(master) for master in masters]
     lengths = [master.shape[0] for master in masters[4:]]
     in_starts, out_starts = starts_of(ENCODER_IN), starts_of(DECODER_IN)
 
     if kernels:
-        tile = vector_tile(shards[4:])
+        tile = vector_tile(masters[4:])
         listed = [(0, 0, tile.shape[1], 1)]
         listed += [(1, low, width, cut) for low, width, cut in zip(in_starts, ENCODER_IN, (1, 2, 1, 2, 1))]
         listed += [(2, 0, D, 2)]
         listed += [(3, low, width, 1) for low, width in zip(out_starts[:2], DECODER_IN[:2])]
-        whole = run_alone(Gather([tile] + shards[:3], listed), 1, "gather_first")
+        whole = run_alone(Gather([tile] + list(masters[:3]), listed), 1, "gather_first")
         vectors = [v.reshape(-1) for v in cut_tile(whole[0].reshape((devices,) + tile.shape), lengths)]
         early = [wide(w.reshape(-1, w.shape[-1])) for w in whole[1:]]
-        gather = Gather(shards[2:4], [(0, out_starts[2], DFF, 2), (0, out_starts[3], PIX, 1), (1, 0, DD, 2)])
+        gather = Gather(masters[2:4], [(0, out_starts[2], DFF, 2), (0, out_starts[3], PIX, 1), (1, 0, DD, 2)])
     else:
-        whole = [lax.all_gather(shard, AXES, axis=0, tiled=True) for shard in shards]
+        whole = [lax.all_gather(narrow(master), AXES, axis=0, tiled=True) for master in masters]
         vectors = whole[4:]
         late = [wide(part) for part in pieces(whole[2], DECODER_IN)]
         early = [wide(part) for part in pieces(whole[0], ENCODER_IN)] + [wide(whole[1])] + late[:2]
@@ -1151,15 +1155,15 @@
         return jnp.zeros((kept.shape[0], width), jnp.bfloat16)
 
     (trio, stream), pull_open, normed = jax.vjp(open_encoder, enc_gains, enc_biases, spare(D), has_aux=True)
-    enc_trio = [narrow(t) for t in trio]
-    enc_mixed, enc_lse, unused = attend_forward(*enc_trio, enc_marks, HEADS)
+    enc_trio = narrow(trio)
+    enc_mixed, enc_lse, unused = attend_forward(enc_trio, enc_marks, HEADS)
     spares = [spare(width) for width in (D, FF, D, DD)]
     lifted, pull_close, saved = jax.vjp(
         close_encoder, wide(enc_mixed), stream, enc_gains, enc_biases, spares, has_aux=True
     )
     (trio, stream), pull_dec_open = jax.vjp(open_decoder, lifted, mask_token, dec_gains, dec_biases, w_qkv_decoder)
-    dec_trio = [narrow(t) for t in trio]
-    dec_mixed, dec_lse, late_weights = attend_forward(*dec_trio, dec_marks, DHEADS, gather, 2)
+    dec_trio = narrow(trio)
+    dec_mixed, dec_lse, late_weights = attend_forward(dec_trio, dec_marks, DHEADS, gather, 2)
     if kernels:
         late = [None, None] + [wide(w.reshape(-1, w.shape[-1])) for w in late_weights]
         w_down_decoder = late[4]
@@ -1177,12 +1181,12 @@
     late_terms = [terms_of(array, cuts) for array, cuts in zip(d_weights, (1, 4, 4, 2))]
     scatter = Scatter(late_terms) if kernels else None
     dec_back, late_sums = attend_backward(
-        *dec_trio, narrow(d_mixed), dec_lse, dec_marks, DHEADS, scatter, 3
+        dec_trio, narrow(d_mixed), dec_lse, dec_marks, DHEADS, scatter, 3
     )
-    d_lifted, d_mask, d_gains_b, d_biases_b, d_qkv = pull_dec_open((tuple(wide(t) for t in dec_back), d_stream))
+    d_lifted, d_mask, d_gains_b, d_biases_b, d_qkv = pull_dec_open((wide(dec_back), d_stream))
     d_mixed, d_stream, e_gains_a, e_biases_a, d_spares = pull_close(d_lifted)
-    enc_back, unused = attend_backward(*enc_trio, narrow(d_mixed), enc_lse, enc_marks, HEADS)
-    e_gains_b, e_biases_b, d_patch = pull_open((tuple(wide(t) for t in enc_back), d_stream))
+    enc_back, unused = attend_backward(enc_trio, narrow(d_mixed), enc_lse, enc_marks, HEADS)
+    e_gains_b, e_biases_b, d_patch = pull_open((wide(enc_back), d_stream))
 
     def total(a, b):
         return [x + y for x, y in zip(a, b)]
@@ -1190,7 +1194,7 @@
     gain_terms = jnp.concatenate(total(e_gains_a, e_gains_b) + total(d_gains_a, d_gains_b))
     bias_terms = jnp.concatenate(total(e_biases_a, e_biases_b) + [d_mask] + total(d_biases_a, d_biases_b))
     normed_two, active, last = (narrow(value) for value in saved)
-    joined_back = jnp.concatenate([t[0] for t in enc_back], axis=0)
+    joined_back = enc_back.reshape(-1, kept.shape[0])
 
     def product(left, right, dims, cuts):
         left_axis, right_axis = dims[0][0][0], dims[0][1][0]

time: 718 us -> 696 us (0.969)
  other arithmetic: 76.7 us -> 47.5 us
    optimization_barrier x0 -> x3, local copies, waits for them, and re-layouts: none -> 19.7 us  [the longest x2 11.5 us: round_plain(): lax.optimization_barrier(value.astype(jnp.bfloat16)).astype(jnp.float32)]
    dot_general x2 -> x1, local copies, waits for them, and re-layouts: 10.1 us -> 1.87 us  [heads_in(): jnp.einsum('gtd,df->gft', normed.reshape(groups, -1, width), weight, pref...]
    convert_element_type x6 -> x0, other arithmetic: 8.06 us -> none  [narrow(): return array.astype(jnp.bfloat16)]
    unnamed x284 -> x252, local copies, waits for them, and re-layouts: 23.6 us -> 18.2 us
where the time goes in v4:
time: 696 us; the launch traced here: 685 us
  Pallas kernels  447 us (64%)
  matrix products  109 us (16%)
  local copies, waits for them, and re-layouts  72.9 us (10%)
  other arithmetic  47.5 us (7%)
  between operations  7.83 us (1%)
    pallas_call x2, Pallas kernels, run_alone(): pl.pallas_call(kernel, in_specs=plan.in_specs + [WHOLE_VMEM] * len(more),...  280 us
    pallas_call x4, Pallas kernels, attend_call(): pl.pallas_call(functools.partial(kernel, step, size, plan), grid=(groups,...  168 us
    dot_general x16, matrix products, matmul(): return jnp.dot(left, right, preferred_element_type=jnp.float32)  73.8 us
    dot_general x5, matrix products, heads_in(): jnp.einsum('gtd,df->gft', normed.reshape(groups, -1, width), weight, pref...  23.9 us
    unnamed x252, local copies, waits for them, and re-layouts  18.2 us

profile of v4, /device:TPU:0, one launch (start us, length us, event | category | flops | bytes accessed | tf_op | source)
XLA Modules:
  0.0 684.7 jit_solution(4841179808529835232)
XLA Ops:
  12.3 4.5 gather_fusion
  23.0 2.8 reshape.675
  25.7 97.7 %gather_first.1 = (bf16[2,2,4,2,8,128]{5,4,3,2,1,0:T(8,128)(2,1)}, bf16[2,2,4,2,24,768]{5,4,3,2,1,0:T(8,128)(2,1)}, bf16[2,2,4,2,24,2304]{5,4,3,2,1,0:T(8,128)(2...) custom-call(f32[8,128]{1,0:T(8,128)} %fusion.76.refs_0_, ...), custom_call_target="tpu_custom_call" | custom-call | flops 1323008 | bytes 2646016 | tf_op jit(solution)/shard_map/gather_first/pallas_call | solution.py:512
  129.4 4.8 fusion.3
  134.2 4.0 copy.72
  138.2 10.3 %attend_forward.2 = (bf16[1,768,392]{2,1,0:T(8,128)(2,1)}, f32[1,12,392]{2,1,0:T(8,128)}) custom-call(bf16[1,3,768,392]{3,2,1,0:T(8,128)(2,1)} %bitcast.146, bf16[1,16,392]{2,1,0:T(8,128)(2,1)} %get-tuple-element.167.refs_1_.refs_3_, bf16[1,16,392]{2,1,0:T(8,128)(2,1)} %get-tuple-element.166.refs_2_.refs_4_), custom_call_target="tpu_custom_call" | custom-call | flops 472055808 | bytes 2408448 | tf_op jit(solution)/shard_map/attend_forward/pallas_call | solution.py:640
  153.3 6.1 multiply_convert_fusion.2
  164.9 3.6 scatter_fusion
  171.9 2.7 copy.79
  174.7 4.3 fusion.4
  179.0 7.5 %copy.73 = bf16[2,1536,784]{2,1,0:T(8,128)(2,1)} copy(bf16[2,1536,784]{1,2,0:T(8,128)(2,1)} %fusion.4) | data formatting | bytes 9633792 | tf_op jit(solution)/shard_map/jvp()/optimization_barrier | solution.py:30
  186.4 61.3 %attend_forward.3 = (bf16[2,512,784]{2,1,0:T(8,128)(2,1)}, f32[2,16,784]{2,1,0:T(8,128)}, bf16[2,2,4,2,16,2048]{5,4,3,2,1,0:T(8,128)(2,1)}, bf16[2,2,4,2,16,768]...) custom-call(bf16[2,3,512,784]{3,2,1,0:T(8,128)(2,1)} %bitcast.153, ...), custom_call_target="tpu_custom_call" | custom-call | flops 2517630976 | bytes 6422528 | tf_op jit(solution)/shard_map/attend_forward/pallas_call | solution.py:640
  247.8 3.6 copy.74
  251.4 2.6 fusion.125
  256.8 7.8 %multiply_convert_fusion = (bf16[1568,2048]{1,0:T(8,128)(2,1)S(1)}, f32[1568,2048]{1,0:T(8,128)}) fusion(f32[2048]{0:T(1024)S(1)} %slice.161, bf16[1568,512]{1,0:T(8,128)(2,1)S(1)} %add_convert_fusion.4, bf16[512,2048]{1,0:T(8,128)(2,1)S(1)} %bitcast.193), kind=kOutput, calls=%fused_computation.7 | convolution fusion | flops 3307601920 | bytes 22978560 | tf_op jit(solution)/shard_map/jvp()/dot_general | solution.py:70
  264.5 3.7 fusion.126
  270.0 4.1 multiply_reduce_fusion.1
  275.4 5.1 fusion.129
  288.0 11.5 %add_convert_fusion = bf16[1568,2048]{1,0:T(8,128)(2,1)S(1)} fusion(f32[1568,2048]{1,0:T(8,128)} %get-tuple-element.193, bf16[1568,512]{1,0:T(8,128)(2,1)S(1)} %add_convert_fusion.6, bf16[2048,512]{1,0:T(8,128)(2,1)S(1)} %bitcast.196, f32[2048]{0:T(1024)S(1)} %slice.161), kind=kOutput, calls=%fused_computation.6 | convolution fusion | flops 3333292032 | bytes 22978560 | tf_op jit(solution)/shard_map/transpose(jvp())/dot_general | solution.py:70
  299.5 5.7 fusion.128
  308.0 4.6 multiply_reduce_fusion.3
  312.6 5.7 fusion.127
  328.3 82.8 %attend_backward.2 = (bf16[2,3,512,784]{3,2,1,0:T(8,128)(2,1)}, f32[16,512]{1,0:T(8,128)}, f32[16,2048]{1,0:T(8,128)}, f32[64,512]{1,0:T(8,128)}, f32[16,768]{1,0:T(8,128)}) custom-call(bf16[2,3,512,784]{3,2,1,0:T(8,128)(2,1)} %bitcast.154, bf16[2,512,784]{2,1,0:T(8,128)(2,1)} %bitcast.163, f32[2,16,784]{2,1,0:T(8,128)} %get-tuple-element.64.refs_2_, ...), custom_call_target="tpu_custom_call" | custom-call | flops 6294077440 | bytes 6422528 | tf_op jit(solution)/shard_map/attend_backward/pallas_call | solution.py:640
  411.2 3.4 convert_reduce_fusion.1
  414.6 8.2 %copy.78 = bf16[2,1536,784]{1,2,0:T(8,128)(2,1)} copy(bf16[2,1536,784]{2,1,0:T(8,128)(2,1)} %bitcast.141) | data formatting | bytes 9633792 | tf_op jit(solution)/shard_map/transpose(jvp())/optimization_barrier | solution.py:66
  422.8 5.1 fusion
  431.5 3.7 multiply_reduce_fusion.4
  441.4 3.4 scatter_custom_fusion.1
  449.6 7.1 %add_convert_fusion.2.refs_5_ = bf16[392,3072]{1,0:T(8,128)(2,1)S(1)} fusion(f32[392,3072]{1,0:T(8,128)} %get-tuple-element.185, f32[3072]{0:T(1024)S(1)} %copy-done.84, bf16[392,768]{1,0:T(8,128)(2,1)S(1)} %add_convert_fusion.11.refs_3_, bf16[3072,768]{1,0:T(8,128)(2,1)} %bitcast.180), kind=kOutput, calls=%fused_computation.17 | convolution fusion | flops 1866547200 | bytes 12558336 | tf_op jit(solution)/shard_map/transpose(jvp())/dot_general | solution.py:70
  463.3 13.2 %attend_backward.3 = bf16[1,3,768,392]{3,2,1,0:T(8,128)(2,1)} custom-call(bf16[1,3,768,392]{3,2,1,0:T(8,128)(2,1)} %bitcast.147, bf16[1,768,392]{2,1,0:T(8,128)(2,1)} %fusion.17.refs_1_, f32[1,12,392]{2,1,0:T(8,128)} %get-tuple-element.66.refs_2_, bf16[1,16,392]{2,1,0:T(8,128)(2,1)} %get-tuple-element.167.refs_1_.refs_3_, ...), custom_call_target="tpu_custom_call" | custom-call | flops 1180139520 | bytes 2408448 | tf_op jit(solution)/shard_map/attend_backward/pallas_call | solution.py:640
  476.5 6.0 multiply_reduce_fusion.14
  488.3 181.9 %scatter_last.1 = (f32[24,512]{1,0:T(8,128)}, f32[96,768]{1,0:T(8,128)}, f32[24,3072]{1,0:T(8,128)}, f32[24,768]{1,0:T(8,128)}, f32[16,1536]{1,0:T(8,128)}, /*in...) custom-call(bf16[392,768]{1,0:T(8,128)(2,1)} %copy-done.31, ...), custom_call_target="tpu_custom_call" | custom-call | flops 15122432 | bytes 30244864 | tf_op jit(solution)/shard_map/scatter_last/pallas_call | solution.py:512
  (406 shorter events, 98.1 us)
Async XLA Ops:
  0.7 16.2 %copy-start.11 = (bf16[1568,768]{1,0:T(8,128)(2,1)S(1)}, bf16[1568,768]{1,0:T(8,128)(2,1)}, u32[]{:S(2)}) copy-start(bf16[1568,768]{1,0:T(8,128)(2,1)} %param.22) | copy-start | bytes 7225348
  10.0 154.9 %copy-start.80 = (s32[392]{0:T(512)}, s32[392]{0:T(512)S(1)}, u32[]{:S(2)}) copy-start(s32[392]{0:T(512)S(1)} %get-tuple-element.162) | copy-start | bytes 4708
  16.9 107.9 %copy-start.32 = (bf16[392,768]{1,0:T(8,128)(2,1)}, bf16[392,768]{1,0:T(8,128)(2,1)S(1)}, u32[]{:S(2)}) copy-start(bf16[392,768]{1,0:T(8,128)(2,1)S(1)} %gather_fusion) | copy-start | bytes 1806340
  124.6 28.6 %copy-start.83 = (f32[3072]{0:T(1024)}, f32[3072]{0:T(1024)S(1)}, u32[]{:S(2)}) copy-start(f32[3072]{0:T(1024)S(1)} %slice.148) | copy-start | bytes 36868
  124.7 27.3 %copy-start.58 = (f32[768]{0:T(1024)}, f32[768]{0:T(1024)S(1)}, u32[]{:S(2)}) copy-start(f32[768]{0:T(1024)S(1)} %get-tuple-element.207) | copy-start | bytes 9220
  124.7 37.3 %copy-start.60 = (f32[768]{0:T(1024)}, f32[768]{0:T(1024)S(1)}, u32[]{:S(2)}) copy-start(f32[768]{0:T(1024)S(1)} %get-tuple-element.208) | copy-start | bytes 9220
  127.6 20.9 %copy-start.7 = (f32[392,768]{1,0:T(8,128)}, f32[392,768]{1,0:T(8,128)S(1)}, u32[]{:S(2)}) copy-start(f32[392,768]{1,0:T(8,128)S(1)} %get-tuple-element.181) | copy-start | bytes 3612676
  254.0 10.5 %copy-start.5 = (f32[1568,512]{1,0:T(8,128)}, f32[1568,512]{1,0:T(8,128)S(1)}, u32[]{:S(2)}) copy-start(f32[1568,512]{1,0:T(8,128)S(1)} %get-tuple-element.191) | copy-start | bytes 9633796
  256.8 12.7 %slice-start = ((s8[4816896]{0:T(1024)(128)(4,1)}), s8[4194304]{0:T(1024)(128)(4,1)S(1)}, s32[]{:S(2)}) async-start(s8[4816896]{0:T(1024)(128)(4,1)} %bitcast.155), calls=%async_computation | async-start | bytes 8388608
  285.2 34.5 %copy-start.3 = (f32[1568,512]{1,0:T(8,128)}, f32[1568,512]{1,0:T(8,128)S(1)}, u32[]{:S(2)}) copy-start(f32[1568,512]{1,0:T(8,128)S(1)} %get-tuple-element.131) | copy-start | bytes 9633796
  285.3 14.2 %slice-start.7 = ((s8[6422528]{0:T(1024)(128)(4,1)}), s8[4194304]{0:T(1024)(128)(4,1)S(1)}, s32[]{:S(2)}) async-start(s8[6422528]{0:T(1024)(128)(4,1)} %bitcast.199), calls=%async_computation.7 | async-start | bytes 8388608
  288.0 11.5 %slice-start.8 = ((s8[6422528]{0:T(1024)(128)(4,1)}), s8[2228224]{0:T(1024)(128)(4,1)S(1)}, s32[]{:S(2)}) async-start(s8[6422528]{0:T(1024)(128)(4,1)} %bitcast.199), calls=%async_computation.8 | async-start | bytes 4456448
  449.4 11.0 %copy-start.15 = (f32[392,768]{1,0:T(8,128)}, f32[392,768]{1,0:T(8,128)S(1)}, u32[]{:S(2)}) copy-start(f32[392,768]{1,0:T(8,128)S(1)} %get-tuple-element.123) | copy-start | bytes 3612676
  461.5 24.0 %copy-start.25 = (bf16[392,768]{1,0:T(8,128)(2,1)}, bf16[392,768]{1,0:T(8,128)(2,1)S(1)}, u32[]{:S(2)}) copy-start(bf16[392,768]{1,0:T(8,128)(2,1)S(1)} %fusion.102.refs_7_) | copy-start | bytes 1806340
  463.3 13.2 %copy-start.8 = (f32[392,768]{1,0:T(8,128)S(1)}, f32[392,768]{1,0:T(8,128)}, u32[]{:S(2)}) copy-start(f32[392,768]{1,0:T(8,128)} %copy-done.7) | copy-start | bytes 3612676
  463.3 13.2 %copy-start.57 = (f32[768]{0:T(1024)S(1)}, f32[768]{0:T(1024)}, u32[]{:S(2)}) copy-start(f32[768]{0:T(1024)} %copy-done.56) | copy-start | bytes 9220
  463.3 13.2 %copy-start.63 = (f32[392]{0:T(512)S(1)}, f32[392]{0:T(512)}, u32[]{:S(2)}) copy-start(f32[392]{0:T(512)} %copy-done.62) | copy-start | bytes 4708
  463.3 13.2 %copy-start.69 = (f32[392]{0:T(512)S(1)}, f32[392]{0:T(512)}, u32[]{:S(2)}) copy-start(f32[392]{0:T(512)} %copy-done.68) | copy-start | bytes 4708
  488.2 184.2 %copy-start.89 = (f32[120]{0:T(128)S(1)}, f32[120]{0:T(128)}, u32[]{:S(2)}) copy-start(f32[120]{0:T(128)} %param.30) | copy-start | bytes 1444
  488.2 184.2 %copy-start.91 = (f32[120]{0:T(128)S(1)}, f32[120]{0:T(128)}, u32[]{:S(2)}) copy-start(f32[120]{0:T(128)} %param.42) | copy-start | bytes 1444
  488.2 184.2 %copy-start.92 = (f32[120]{0:T(128)S(1)}, f32[120]{0:T(128)}, u32[]{:S(2)}) copy-start(f32[120]{0:T(128)} %param.36) | copy-start | bytes 1444
  488.2 185.5 %copy-start.82 = (f32[520]{0:T(1024)S(1)}, f32[520]{0:T(1024)}, u32[]{:S(2)}) copy-start(f32[520]{0:T(1024)} %param.31) | copy-start | bytes 6244
  488.2 185.5 %copy-start.87 = (f32[520]{0:T(1024)S(1)}, f32[520]{0:T(1024)}, u32[]{:S(2)}) copy-start(f32[520]{0:T(1024)} %param.43) | copy-start | bytes 6244
  488.2 185.5 %copy-start.88 = (f32[520]{0:T(1024)S(1)}, f32[520]{0:T(1024)}, u32[]{:S(2)}) copy-start(f32[520]{0:T(1024)} %param.37) | copy-start | bytes 6244
  488.2 186.8 %copy-start.44 = (f32[64,512]{1,0:T(8,128)S(1)}, f32[64,512]{1,0:T(8,128)}, u32[]{:S(2)}) copy-start(f32[64,512]{1,0:T(8,128)} %get-tuple-element.69.refs_17_) | copy-start | bytes 393220
  488.3 188.8 %copy-start.40 = (f32[96,768]{1,0:T(8,128)S(1)}, f32[96,768]{1,0:T(8,128)}, u32[]{:S(2)}) copy-start(f32[96,768]{1,0:T(8,128)} %refs_2_.1) | copy-start | bytes 884740
  488.3 191.0 %copy-start.43 = (f32[16,2048]{1,0:T(8,128)S(1)}, f32[16,2048]{1,0:T(8,128)}, u32[]{:S(2)}) copy-start(f32[16,2048]{1,0:T(8,128)} %get-tuple-element.68.refs_16_) | copy-start | bytes 393220
  488.3 191.0 %copy-start.50 = (f32[16,768]{1,0:T(8,128)S(1)}, f32[16,768]{1,0:T(8,128)}, u32[]{:S(2)}) copy-start(f32[16,768]{1,0:T(8,128)} %get-tuple-element.70.refs_18_) | copy-start | bytes 147460
  488.3 191.0 %copy-start.51 = (f32[16,512]{1,0:T(8,128)S(1)}, f32[16,512]{1,0:T(8,128)}, u32[]{:S(2)}) copy-start(f32[16,512]{1,0:T(8,128)} %get-tuple-element.67.refs_15_) | copy-start | bytes 98308
  670.2 11.0 %copy-start.53 = (f32[24,768]{1,0:T(8,128)S(1)}, f32[24,768]{1,0:T(8,128)}, u32[]{:S(2)}) copy-start(f32[24,768]{1,0:T(8,128)} %get-tuple-element.72) | copy-start | bytes 221188
  670.2 11.0 %copy-start.52 = (f32[24,768]{1,0:T(8,128)S(1)}, f32[24,768]{1,0:T(8,128)}, u32[]{:S(2)}) copy-start(f32[24,768]{1,0:T(8,128)} %get-tuple-element.74) | copy-start | bytes 221188
  670.3 11.1 %copy-start.48 = (f32[24,3072]{1,0:T(8,128)S(1)}, f32[24,3072]{1,0:T(8,128)}, u32[]{:S(2)}) copy-start(f32[24,3072]{1,0:T(8,128)} %get-tuple-element.75) | copy-start | bytes 884740
  (80 other events, 360.2 us)
